TPU v7x, 32 devices: a whole 2x2x4 slice. The times are simulated.
32 devices in a mesh: rows: 32 (over z, y, x, core).
Axes of the slice: x: 2, y: 2, z: 4, core: 2. Of those that a mesh axis runs over, the one named last changes fastest.
Arguments:
- right_side: float32 [524288], P('rows'), may hold values from -24 to 24
- diag_shift: float32 [524288], P('rows'), may hold values from 0.05 to 0.5
- dictionary: float32 [128, 128, 128], replicated, may hold values from -16.5 to 16.5, as said below
- diag_ids: int32 [4096], P('rows'), may hold values from 0 to 127
- diag_gain: float32 [4096], P('rows'), may hold values from 0.3 to 1.5
- cycle_ids: int32 [4096, 2], P('rows'), may hold values from 0 to 127, as said below
- cycle_weights: float32 [4096, 2], P('rows'), may hold values from 0.3 to 1.5, as said below
- link_rows: int32 [32, 5, 64], P('rows'), may hold values from 0 to 127, as said below
- link_ids: int32 [32, 5, 64], P('rows'), may hold values from 0 to 127, as said below
- link_weights: float32 [32, 5, 64], P('rows'), may hold values from 0.3 to 1.5, as said below
Outputs:
- solution_field: float32 [524288], P('rows')
- residual: float32 [524288], P('rows')
Inputs may be any that keep to these rules, and one draw needn't show every extreme that they name: `dictionary`: every block is symmetric positive definite. cycle_ids[i,1] equals cycle_ids[(i+1) mod 4096,0]. cycle_weights[i,1] equals cycle_weights[(i+1) mod 4096,0]. `link_rows`: for each device and level the 64 entries are distinct. `link_ids`: devices d and d XOR 2^b at level m (b = log2 of the number of devices - 1 - m) hold the same entries in the same order. `link_weights`: devices d and d XOR 2^b at level m (b = log2 of the number of devices - 1 - m) hold the same entries in the same order.
All inputs are finite; a program needn't handle non-finite values.
Results may differ from a plain program's by a relative error of at most 0.0003.
Values sent between devices are 32-bit elements; how exact they have to be, the bound alone decides.
No kernel may reach another device: no remote copies, remote signals or barrier semaphores. Data moves between devices by JAX's collectives and lax.ppermute only.
A program may use at most 128 MiB of HBM per device.

v0:
```python
import functools

import jax
import jax.numpy as jnp
from jax import lax
from jax.experimental import pallas as pl
from jax.experimental.pallas import tpu as pltpu
from jax.sharding import PartitionSpec as P


ITERS = 4
SLOT = 8
GROUP = 128
SHIFT = 1.5
F32 = jnp.float32
BF16 = jnp.bfloat16


def dot(a, b, dims=((1,), (0,))):
    return lax.dot_general(a, b, (dims, ((), ())), preferred_element_type=F32)


NT = ((1,), (1,))
TN = ((0,), (0,))


def halves(x):
    high = x.astype(BF16).astype(F32)
    return high, x - high


def halves_wide(x):
    high, low = halves(x)
    return jnp.concatenate([high, low], axis=1).astype(BF16)


def iota(shape, dim):
    return lax.broadcasted_iota(jnp.int32, shape, dim)


def onehot(cond):
    return jnp.where(cond, 1.0, 0.0)


def send_blocks(select_ref, block_vec, send_refs, edge_ref, merged):
    nb = block_vec.shape[0]
    edge = jnp.concatenate([block_vec[0:1], block_vec[nb - 1 :]], axis=0)
    edge = jnp.concatenate([edge, jnp.zeros((6, block_vec.shape[1]), F32)], axis=0)
    wide = halves_wide(block_vec)
    picked = dot(select_ref[...], wide)
    width = block_vec.shape[1]
    picked = picked[:, :width] + picked[:, width:]
    half = picked.shape[0] // len(send_refs)
    for level, ref in enumerate(send_refs):
        ref[0:half, :] = picked[level * half : (level + 1) * half]
        if level == merged:
            ref[half : half + 8, :] = edge
    edge_ref[...] = edge


def prepare(
    parity_ref, dict_hbm, *refs, nb, levels, half, merged, groups, sure, entries, sources,
):
    small_hbm, refs = refs[:8], refs[8:]
    sends, (edge_ref, select_ref, gather_ref, scatter_ref, wide_ref, table_ref, scale_ref) = (
        refs[:levels], refs[levels : levels + 7],
    )
    dict_vmem, here_ref, source_ref, signed_ref, *small, small_sems, sems = refs[levels + 7 :]
    vec_vmem, own_ids_ref, own_weights_ref, near_ids_ref, near_weights_ref, *link_refs = small
    link_rows_ref, link_ids_ref, link_weights_ref = link_refs
    blocks, width, _ = dict_hbm.shape
    parts = sems.shape[0]
    per = blocks // parts

    def load(part):
        span = pl.ds(part * per, per)
        return pltpu.make_async_copy(dict_hbm.at[span], dict_vmem.at[span], sems.at[part])

    load_small = [
        pltpu.make_async_copy(source, target, small_sems.at[k])
        for k, (source, target) in enumerate(zip(small_hbm, small))
    ]
    for copy in load_small[1:] + load_small[:1]:
        copy.start()
    for part in range(parts):
        load(part).start()
    for copy in load_small[1:]:
        copy.wait()

    links = levels * half
    tail = 2 * nb + links
    pad = entries - tail - 1

    def row_of(own, near, link, last):
        pieces = [own, near] + [link[level] for level in range(levels)]
        return jnp.concatenate(pieces + [last, jnp.zeros((1, pad), last.dtype)], axis=1)

    lane = iota((1, entries), 1)
    ids = row_of(own_ids_ref[...], near_ids_ref[0:1, :], link_ids_ref, near_ids_ref[1:2, nb - 1 : nb])
    ids = jnp.where(lane > tail, -1, ids)
    weights = row_of(
        own_weights_ref[...], near_weights_ref[0:1, :], link_weights_ref, near_weights_ref[1:2, nb - 1 : nb]
    )
    zeros = jnp.zeros((1, nb), jnp.int32)
    rows = row_of(zeros, zeros, link_rows_ref, zeros[:, 0:1])
    is_lower = (lane >= nb) & (lane < 2 * nb)
    is_link = (lane >= 2 * nb) & (lane < tail)
    is_tail = lane == tail
    even = parity_ref[0] == 0
    edge_base = nb + links
    before = jnp.where(even, edge_base + 9, edge_base + 1)
    after = jnp.where(even, edge_base, edge_base + 8)
    plus = jnp.where(is_link, rows, jnp.where(is_tail, nb - 1, -1))
    plus = jnp.where(lane < nb, lane, jnp.where(is_lower, lane - nb, plus))
    minus = jnp.where(is_lower & (lane > nb), lane - nb - 1, -1)
    away = jnp.where(is_link, lane - nb, jnp.where(is_tail, after, -1))
    away = jnp.where(is_lower, jnp.where(lane > nb, lane - nb - 1, before), away)

    member = onehot(iota((blocks, entries), 0) == ids)
    earlier = onehot(iota((entries, entries), 0) < iota((entries, entries), 1)).astype(BF16)
    ahead = dot(member.astype(BF16), earlier)
    rank = jnp.sum(member * ahead, axis=0, keepdims=True)
    count = jnp.sum(member, axis=1, keepdims=True)
    more = jnp.maximum(jnp.floor((count - 1.0) * (1.0 / SLOT)), 0.0)
    before_block = onehot(iota((blocks, blocks), 1) < iota((blocks, blocks), 0)).astype(BF16)
    more_wide = jnp.broadcast_to(more, (blocks, 128))
    base = dot(before_block, more_wide.astype(BF16))
    base_entry = jnp.sum(member * base[:, 0:1], axis=0, keepdims=True)
    chunk = jnp.floor(rank * (1.0 / SLOT))
    place = rank - SLOT * chunk
    idf = ids.astype(F32)
    slot = jnp.where(
        chunk == 0.0,
        idf * SLOT + place,
        (blocks + base_entry + chunk - 1.0) * SLOT + place,
    )
    slot = jnp.where(ids >= 0, slot, -1.0).astype(jnp.int32)

    chunk_lane = iota((blocks, 128), 1).astype(F32)
    owner = (chunk_lane >= base) & (chunk_lane < base + more_wide)
    block_id = iota((blocks, 128), 0).astype(F32)
    table = jnp.sum(jnp.where(owner, block_id, 0.0), axis=0, keepdims=True)
    total = jnp.sum(more_wide, axis=0, keepdims=True)
    table_ref[...] = jnp.where(iota((1, 128), 1) == 127, total, table).astype(jnp.int32)

    row_iota = iota((nb, entries), 0)
    target = onehot(row_iota == plus)
    source_iota = iota((sources, entries), 0)
    source_ref[...] = (onehot(source_iota == plus) - onehot(source_iota == away)).astype(BF16)
    signed = target - onehot(row_iota == minus)
    high, low = halves(weights)
    signed_ref[...] = jnp.concatenate([signed * high, signed * low], axis=0).astype(BF16)
    span = sure * GROUP
    here_ref[...] = onehot(iota((span, entries), 0) == slot).astype(BF16)
    gather_ref[0:span, :] = dot(here_ref[...], source_ref[...], NT).astype(BF16)
    scatter_ref[:, 0:span] = dot(signed_ref[...], here_ref[...], NT).astype(BF16)
    used_chunks = jnp.sum(more).astype(jnp.int32)
    chunks = GROUP // SLOT
    for group in range(sure, groups):

        @pl.when(used_chunks > (group - blocks * SLOT // GROUP) * chunks)
        def _(group=group):
            at = slice(group * GROUP, (group + 1) * GROUP)
            here = onehot(iota((GROUP, entries), 0) + group * GROUP == slot).astype(BF16)
            gather_ref[at, :] = dot(here, source_ref[...], NT).astype(BF16)
            scatter_ref[:, at] = dot(signed_ref[...], here, NT).astype(BF16)

    eye = onehot(iota((nb, nb), 0) == iota((nb, nb), 1)).astype(BF16)
    select_ref[...] = dot(target[:, 2 * nb : tail].astype(BF16), eye, TN).astype(BF16)
    load_small[0].wait()
    send_blocks(select_ref, vec_vmem[...], sends, edge_ref, merged)

    def split_block(k, acc):
        block = dict_vmem[k]
        block_high = block.astype(BF16)
        wide_ref[k, :, 0:width] = block_high
        wide_ref[k, :, width : 2 * width] = (block - block_high.astype(F32)).astype(BF16)
        return acc + block

    acc = jnp.zeros((width, width), F32)
    for part in range(parts):
        load(part).wait()
        acc = lax.fori_loop(part * per, (part + 1) * per, split_block, acc, unroll=4)
    diagonal = onehot(iota((width, width), 0) == iota((width, width), 1))
    trace = jnp.sum(jnp.sum(acc * diagonal, axis=0, keepdims=True), axis=1, keepdims=True)
    scale = 1.0 / (trace * (4.25 / (blocks * width)) + 0.5)
    scale_ref[...] = jnp.broadcast_to(scale, (1, 128))


def apply_operator(
    table_ref, vec_ref, shift_ref, scale_ref, recv_refs, edge_ref,
    gather_ref, scatter_ref, wide_ref, scratch, *, half, merged, sure,
):
    sources_ref, lhs_ref, prod_ref = scratch
    nb, width = vec_ref.shape
    blocks = wide_ref.shape[0]
    chunks = GROUP // SLOT
    levels = len(recv_refs)
    vec = vec_ref[...]
    sources_ref[0:nb, :] = halves_wide(vec)
    for level, ref in enumerate(recv_refs):
        start = nb + level * half
        sources_ref[start : start + half, :] = halves_wide(ref[0:half, :])
    start = nb + levels * half
    mine = recv_refs[merged][half : half + 8, :] if merged >= 0 else edge_ref[8:16, :]
    sources_ref[start : start + 16, :] = halves_wide(jnp.concatenate([mine, edge_ref[0:8, :]], axis=0))
    rest = sources_ref.shape[0] - start - 16
    if rest:
        sources_ref[start + 16 :, :] = jnp.zeros((rest, 2 * width), BF16)

    def stage(picked):
        picked = picked[:, :width] + picked[:, width:]
        high, low = halves(picked)
        for chunk in range(picked.shape[0] // SLOT):
            span = slice(chunk * SLOT, (chunk + 1) * SLOT)
            yield jnp.concatenate([high[span], low[span]], axis=0).astype(BF16)

    def product(lhs, block):
        wide = dot(lhs, block)
        return wide[:SLOT, :width] + wide[:SLOT, width:] + wide[SLOT:, :width]

    def rows_of(total):
        return total[:nb, :width] + total[:nb, width:] + total[nb:, :width]

    span = sure * GROUP
    picked = dot(gather_ref[0:span, :], sources_ref[...])
    for c, lhs in enumerate(stage(picked)):
        lhs_ref[c * 2 * SLOT : (c + 1) * 2 * SLOT, :] = lhs
    for pair in range(span // SLOT // 2):
        prods = []
        for c in (2 * pair, 2 * pair + 1):
            block = wide_ref[c] if c < blocks else wide_ref[table_ref[0, c - blocks]]
            prods.append(product(lhs_ref[c * 2 * SLOT : (c + 1) * 2 * SLOT, :], block))
        prod_ref[pair * 2 * SLOT : (pair + 1) * 2 * SLOT, :] = halves_wide(jnp.concatenate(prods, axis=0))
    out = rows_of(dot(scatter_ref[:, 0:span], prod_ref[...]))

    def further(group, out):
        at = pl.ds(pl.multiple_of(blocks * SLOT + group * GROUP, GROUP), GROUP)
        lhs = list(stage(dot(gather_ref[at, :], sources_ref[...])))
        prods = [product(lhs[c], wide_ref[table_ref[0, group * chunks + c]]) for c in range(chunks)]
        return out + rows_of(dot(scatter_ref[:, at], halves_wide(jnp.concatenate(prods, axis=0))))

    out = lax.fori_loop(sure - blocks * SLOT // GROUP, (table_ref[0, 127] + chunks - 1) // chunks, further, out)
    return (shift_ref[...] * vec + out) * scale_ref[...] - SHIFT * vec


def step_kernel(*refs, levels, half, merged, sure):
    table_ref, vec_ref, shift_ref, scale_ref, *rest = refs
    recv_refs, rest = rest[:levels], rest[levels:]
    edge_ref, select_ref, gather_ref, scatter_ref, wide_ref, next_ref, *rest = rest
    sends, (send_edge_ref, *scratch) = rest[:levels], rest[levels:]
    following = apply_operator(
        table_ref, vec_ref, shift_ref, scale_ref, recv_refs, edge_ref,
        gather_ref, scatter_ref, wide_ref, scratch, half=half, merged=merged, sure=sure,
    )
    next_ref[...] = following
    send_blocks(select_ref, following, sends, send_edge_ref, merged)


PAIRS = [(i, j) for i in range(ITERS + 1) for j in range(i, ITERS + 1)]


def last_kernel(*refs, levels, half, merged, sure):
    table_ref, vec_ref, shift_ref, scale_ref, *rest = refs
    recv_refs, rest = rest[:levels], rest[levels:]
    edge_ref, gather_ref, scatter_ref, wide_ref, *rest = rest
    older, (next_ref, sums_ref, *scratch) = rest[: ITERS - 1], rest[ITERS - 1 :]
    following = apply_operator(
        table_ref, vec_ref, shift_ref, scale_ref, recv_refs, edge_ref,
        gather_ref, scatter_ref, wide_ref, scratch, half=half, merged=merged, sure=sure,
    )
    next_ref[...] = following
    basis = [ref[...] for ref in older] + [vec_ref[...], following]
    sums = [jnp.sum(basis[i] * basis[j], axis=0, keepdims=True) for i, j in PAIRS]
    sums = jnp.concatenate(sums + [jnp.zeros((1, sums[0].shape[1]), F32)] * (-len(PAIRS) % 8), axis=0)
    column = jnp.sum(sums, axis=1, keepdims=True)
    at = iota((column.shape[0], 128), 0) == iota((column.shape[0], 128), 1)
    row = jnp.sum(jnp.where(at, column, 0.0), axis=0, keepdims=True)
    sums_ref[...] = jnp.broadcast_to(row, sums_ref.shape)


def finish(sums_ref, scale_ref, *refs):
    basis_refs, (solution_ref, residual_ref) = refs[: ITERS + 1], refs[ITERS + 1 :]
    row = jnp.sum(sums_ref[...], axis=0, keepdims=True)
    lane = iota(row.shape, 1)
    gram = {}
    for index, (i, j) in enumerate(PAIRS):
        entry = jnp.sum(jnp.where(lane == index, row, 0.0), axis=1, keepdims=True)
        gram[i, j] = gram[j, i] = entry
    unscale = 1.0 / scale_ref[0:1, 0:1]
    one = jnp.ones((1, 1), F32)

    def image_of(coefs):
        out = [None] * (len(coefs) + 1)
        for k, c in enumerate(coefs):
            up = c * unscale
            out[k] = SHIFT * up if out[k] is None else out[k] + SHIFT * up
            out[k + 1] = up
        return out

    def inner(a, b):
        rows = []
        for i, x in enumerate(a):
            rows.append(x * sum(gram[i, j] * y for j, y in enumerate(b)))
        return sum(rows)

    def plus(a, factor, b):
        out = list(a) + [None] * (len(b) - len(a))
        for k, y in enumerate(b):
            out[k] = factor * y if out[k] is None else out[k] + factor * y
        return out

    residual = [one]
    field = []
    image = image_of(residual)
    norm = inner(residual, residual)
    step = norm / inner(residual, image)
    direction, along = residual, image
    for k in range(ITERS):
        field = plus(field, step, direction)
        residual = plus(residual, -step, along)
        if k + 1 < ITERS:
            image = image_of(residual)
            following = inner(residual, residual)
            product = inner(residual, image)
            ratio = following / norm
            step = following / (product - ratio * following / step)
            direction = plus(residual, ratio, direction)
            along = plus(image, ratio, along)
            norm = following
    basis = [ref[...] for ref in basis_refs]
    solution_ref[...] = sum(c * v for c, v in zip(field, basis))
    residual_ref[...] = sum(c * v for c, v in zip(residual, basis))


def params(mib):
    return pltpu.CompilerParams(vmem_limit_bytes=mib * 1024 * 1024)


def vmem(count):
    return [pl.BlockSpec(memory_space=pltpu.VMEM)] * count


def shape(dims, dtype=F32):
    return jax.ShapeDtypeStruct(dims, dtype)


def per_device(
    right_side, diag_shift, dictionary, diag_ids, diag_gain, cycle_ids, cycle_weights,
    link_rows, link_ids, link_weights, *, devices,
):
    nb = diag_ids.shape[0]
    blocks, width, _ = dictionary.shape
    _, levels, half = link_rows.shape
    bits = devices.bit_length() - 1
    masks = [2 ** (bits - 1 - level) for level in range(levels)]
    merged = masks.index(1) if 1 in masks else -1
    links = levels * half
    used = 2 * nb + links + 1
    entries = -(-used // 128) * 128
    sources = -(-(nb + links + 16) // 128) * 128
    extra = -(-(used // SLOT) // (GROUP // SLOT))
    groups = blocks * SLOT // GROUP + extra

    sure = blocks * SLOT // GROUP + 1
    parity = (lax.axis_index("rows") & 1).astype(jnp.int32)[None]
    first = right_side.reshape(nb, width)
    shifts = diag_shift.reshape(nb, width)

    small = [first, diag_ids[None], diag_gain[None], cycle_ids.T, cycle_weights.T]
    small += [jnp.swapaxes(array, 0, 1) for array in (link_rows, link_ids, link_weights)]
    send_shapes = [shape((half + 8 * (level == merged), width)) for level in range(levels)]
    edge_shape = shape((8, width))
    outs = pl.pallas_call(
        functools.partial(
            prepare, nb=nb, levels=levels, half=half, merged=merged, groups=groups, sure=sure,
            entries=entries, sources=sources,
        ),
        out_shape=send_shapes
        + [
            edge_shape,
            shape((links, nb), BF16),
            shape((groups * GROUP, sources), BF16),
            shape((2 * nb, groups * GROUP), BF16),
            shape((blocks, width, 2 * width), BF16),
            shape((1, 128), jnp.int32),
            shape((1, 128)),
        ],
        in_specs=[pl.BlockSpec(memory_space=pltpu.SMEM)] + [pl.BlockSpec(memory_space=pltpu.HBM)] * 9,
        out_specs=vmem(levels + 7),
        scratch_shapes=[
            pltpu.VMEM((blocks, width, width), F32),
            pltpu.VMEM((sure * GROUP, entries), BF16),
            pltpu.VMEM((sources, entries), BF16),
            pltpu.VMEM((2 * nb, entries), BF16),
            *(pltpu.VMEM(array.shape, array.dtype) for array in small),
            pltpu.SemaphoreType.DMA((len(small),)),
            pltpu.SemaphoreType.DMA((4,)),
        ],
        compiler_params=params(40),
        name="prepare",
)(parity, *(pltpu.with_memory_space_constraint(array, pltpu.HBM) for array in [dictionary] + small))
    sends, (edge, select, gather, scatter, wide, table, scale) = outs[:levels], outs[levels:]

    def exchange(sends, edge):
        near = [(i, i ^ 1) for i in range(devices)]
        far = [(i, (i + 1) % devices if i % 2 else (i - 1) % devices) for i in range(devices)]
        edges = lax.ppermute(edge, "rows", far)
        if merged < 0:
            edges = jnp.concatenate([edges, lax.ppermute(edge, "rows", near)], axis=0)
        got = []
        for level in range(levels):
            pairs = [(i, i ^ masks[level]) for i in range(devices)]
            got.append(lax.ppermute(sends[level], "rows", pairs))
        return got, edges

    scratch = [
        pltpu.VMEM((sources, 2 * width), BF16),
        pltpu.VMEM((2 * sure * GROUP, width), BF16),
        pltpu.VMEM((sure * GROUP, 2 * width), BF16),
    ]
    smem = [pl.BlockSpec(memory_space=pltpu.SMEM)]
    basis = [first]
    for k in range(ITERS):
        got, edges = exchange(sends, edge)
        common = dict(levels=levels, half=half, merged=merged, sure=sure)
        if k + 1 < ITERS:
            following, *outs = pl.pallas_call(
                functools.partial(step_kernel, **common),
                out_shape=[shape((nb, width))] + send_shapes + [edge_shape],
                in_specs=smem + vmem(8 + levels),
                out_specs=vmem(levels + 2),
                scratch_shapes=scratch,
                compiler_params=params(24),
                name="step",
            )(table, basis[-1], shifts, scale, *got, edges, select, gather, scatter, wide)
            sends, edge = outs[:levels], outs[levels]
        else:
            following, sums = pl.pallas_call(
                functools.partial(last_kernel, **common),
                out_shape=[shape((nb, width)), shape((devices, 128))],
                in_specs=smem + vmem(7 + levels + ITERS - 1),
                out_specs=vmem(2),
                scratch_shapes=scratch,
                compiler_params=params(24),
                name="last",
            )(table, basis[-1], shifts, scale, *got, edges, gather, scatter, wide, *basis[:-1])
        basis.append(following)
    sums = lax.all_to_all(sums, "rows", 0, 0, tiled=True)
    field, residual = pl.pallas_call(
        finish,
        out_shape=[shape((nb, width))] * 2,
        in_specs=vmem(2 + len(basis)),
        out_specs=vmem(2),
        compiler_params=params(8),
        name="finish",
    )(sums, scale, *basis)
    return field.reshape(-1), residual.reshape(-1)


def solution(mesh):
    placed = (
        P("rows"), P("rows"), P(), P("rows"), P("rows"), P("rows", None), P("rows", None),
        P("rows", None, None), P("rows", None, None), P("rows", None, None),
    )
    return jax.shard_map(
        functools.partial(per_device, devices=mesh.shape["rows"]),
        mesh=mesh, in_specs=placed, out_specs=(P("rows"), P("rows")), check_vma=False,
    )
```

profile of v0, /device:TPU:0, one launch (start us, length us, event | category | flops | bytes accessed | tf_op | source)
XLA Modules:
  0.0 74.4 jit_solution(9223071451635231357)
XLA Ops:
  0.7 6.8 %prepare.1 = (f32[64,128]{1,0:T(8,128)S(1)}, f32[64,128]{1,0:T(8,128)S(1)}, f32[64,128]{1,0:T(8,128)S(1)}, f32[64,128]{1,0:T(8,128)S(1)}, f32[72,128]{1,0:T(8,12...) custom-call(s32[1]{0:T(128)} %bitcast.parity_ref, ...), custom_call_target="tpu_custom_call" | custom-call | tf_op jit(solution)/shard_map/prepare/pallas_call | solution.py:374
  7.5 6.5 %collective-permute-start.5 = (f32[8,128]{1,0:T(8,128)S(1)}, f32[8,128]{1,0:T(8,128)S(1)}, u32[]{:S(2)}, u32[]{:S(2)}) collective-permute-start(f32[8,128]{1,0:T(8,128)S(1)} %get-tuple-element.46), channel_id=1, source_target_pairs={{0,31},{1,2},{2,1},{3,4},{4,3},{5,6},{6,5},{7,8},{8,7},{9,10},{10,... | collective-permute-start | bytes 12296 | tf_op jit(solution)/shard_map/ppermute | solution.py:408
  14.0 0.0 collective-permute-start.4
  14.0 0.0 collective-permute-start
  14.0 1.0 %collective-permute-start.1 = (f32[64,128]{1,0:T(8,128)S(1)}, f32[64,128]{1,0:T(8,128)S(1)}, u32[]{:S(2)}, u32[]{:S(2)}) collective-permute-start(f32[64,128]{1,0:T(8,128)S(1)} %get-tuple-element.42), channel_id=1, source_target_pairs={{0,8},{1,9},{2,10},{3,11},{4,12},{5,13},{6,14},{7,15},{8,0},{9,1},... | collective-permute-start | bytes 98312 | tf_op jit(solution)/shard_map/ppermute | solution.py:414
  15.0 1.4 %collective-permute-start.2 = (f32[64,128]{1,0:T(8,128)S(1)}, f32[64,128]{1,0:T(8,128)S(1)}, u32[]{:S(2)}, u32[]{:S(2)}) collective-permute-start(f32[64,128]{1,0:T(8,128)S(1)} %get-tuple-element.43), channel_id=1, source_target_pairs={{0,4},{1,5},{2,6},{3,7},{4,0},{5,1},{6,2},{7,3},{8,12},{9,13},{10,... | collective-permute-start | bytes 98312 | tf_op jit(solution)/shard_map/ppermute | solution.py:414
  16.3 0.0 collective-permute-done.5.refs_9_
  16.3 0.0 collective-permute-start.3
  16.4 2.4 %collective-permute-done.refs_4_ = f32[64,128]{1,0:T(8,128)S(1)} collective-permute-done((f32[64,128]{1,0:T(8,128)S(1)}, f32[64,128]{1,0:T(8,128)S(1)}, u32[]{:S(2)}, u32[]{:S(2)}) %collective-permute-start) | collective-permute-done | bytes 32800 | tf_op jit(solution)/shard_map/ppermute | solution.py:414
  18.8 0.0 collective-permute-done.1.refs_5_
  18.8 0.1 collective-permute-done.2.refs_6_
  18.9 1.4 %collective-permute-done.3.refs_7_ = f32[64,128]{1,0:T(8,128)S(1)} collective-permute-done((f32[64,128]{1,0:T(8,128)S(1)}, f32[64,128]{1,0:T(8,128)S(1)}, u32[]{:S(2)}, u32[]{:S(2)}) %collective-permute-start.3) | collective-permute-done | bytes 32800 | tf_op jit(solution)/shard_map/ppermute | solution.py:414
  20.2 0.0 collective-permute-done.4.refs_8_
  20.2 3.1 %step.3 = (f32[128,128]{1,0:T(8,128)S(1)}, f32[64,128]{1,0:T(8,128)S(1)}, f32[64,128]{1,0:T(8,128)S(1)}, f32[64,128]{1,0:T(8,128)S(1)}, f32[64,128]{1,0:T(8,128)...) custom-call(s32[1,128]{1,0:T(1,128)S(1)} %get-tuple-element.39.refs_0_, f32[128,128]{1,0:T(8,128)S(1)} %bitcast.21, ...), custom_call_target="tpu_custom_call" | custom-call | tf_op jit(solution)/shard_map/step/pallas_call | solution.py:428
  23.3 3.3 %collective-permute-start.11 = (f32[8,128]{1,0:T(8,128)S(1)}, f32[8,128]{1,0:T(8,128)S(1)}, u32[]{:S(2)}, u32[]{:S(2)}) collective-permute-start(f32[8,128]{1,0:T(8,128)S(1)} %get-tuple-element.57), channel_id=1, source_target_pairs={{0,31},{1,2},{2,1},{3,4},{4,3},{5,6},{6,5},{7,8},{8,7},{9,10},{10,... | collective-permute-start | bytes 12296 | tf_op jit(solution)/shard_map/ppermute | solution.py:408
  26.6 0.0 collective-permute-start.10
  26.6 0.0 collective-permute-start.6
  26.6 0.0 collective-permute-start.7
  26.6 1.5 %collective-permute-start.8 = (f32[64,128]{1,0:T(8,128)S(1)}, f32[64,128]{1,0:T(8,128)S(1)}, u32[]{:S(2)}, u32[]{:S(2)}) collective-permute-start(f32[64,128]{1,0:T(8,128)S(1)} %get-tuple-element.54), channel_id=1, source_target_pairs={{0,4},{1,5},{2,6},{3,7},{4,0},{5,1},{6,2},{7,3},{8,12},{9,13},{10,... | collective-permute-start | bytes 98312 | tf_op jit(solution)/shard_map/ppermute | solution.py:414
  28.2 2.0 %collective-permute-done.11.refs_9_ = f32[8,128]{1,0:T(8,128)S(1)} collective-permute-done((f32[8,128]{1,0:T(8,128)S(1)}, f32[8,128]{1,0:T(8,128)S(1)}, u32[]{:S(2)}, u32[]{:S(2)}) %collective-permute-start.11) | collective-permute-done | bytes 4128 | tf_op jit(solution)/shard_map/ppermute | solution.py:408
  30.1 0.7 collective-permute-start.9
  30.8 0.6 collective-permute-done.6.refs_4_
  31.5 0.0 collective-permute-done.7.refs_5_
  31.5 0.0 collective-permute-done.8.refs_6_
  31.5 2.6 %collective-permute-done.9.refs_7_ = f32[64,128]{1,0:T(8,128)S(1)} collective-permute-done((f32[64,128]{1,0:T(8,128)S(1)}, f32[64,128]{1,0:T(8,128)S(1)}, u32[]{:S(2)}, u32[]{:S(2)}) %collective-permute-start.9) | collective-permute-done | bytes 32800 | tf_op jit(solution)/shard_map/ppermute | solution.py:414
  34.0 0.0 collective-permute-done.10.refs_8_
  34.1 3.1 %step.4 = (f32[128,128]{1,0:T(8,128)S(1)}, f32[64,128]{1,0:T(8,128)S(1)}, f32[64,128]{1,0:T(8,128)S(1)}, f32[64,128]{1,0:T(8,128)S(1)}, f32[64,128]{1,0:T(8,128)...) custom-call(s32[1,128]{1,0:T(1,128)S(1)} %get-tuple-element.39.refs_0_, ...), custom_call_target="tpu_custom_call" | custom-call | tf_op jit(solution)/shard_map/step/pallas_call | solution.py:428
  37.1 2.1 %collective-permute-start.17 = (f32[8,128]{1,0:T(8,128)S(1)}, f32[8,128]{1,0:T(8,128)S(1)}, u32[]{:S(2)}, u32[]{:S(2)}) collective-permute-start(f32[8,128]{1,0:T(8,128)S(1)} %get-tuple-element.64), channel_id=1, source_target_pairs={{0,31},{1,2},{2,1},{3,4},{4,3},{5,6},{6,5},{7,8},{8,7},{9,10},{10,... | collective-permute-start | bytes 12296 | tf_op jit(solution)/shard_map/ppermute | solution.py:408
  39.2 0.0 collective-permute-start.16
  39.2 0.0 collective-permute-start.12
  39.2 0.0 collective-permute-start.13
  39.2 1.6 %collective-permute-start.14 = (f32[64,128]{1,0:T(8,128)S(1)}, f32[64,128]{1,0:T(8,128)S(1)}, u32[]{:S(2)}, u32[]{:S(2)}) collective-permute-start(f32[64,128]{1,0:T(8,128)S(1)} %get-tuple-element.61), channel_id=1, source_target_pairs={{0,4},{1,5},{2,6},{3,7},{4,0},{5,1},{6,2},{7,3},{8,12},{9,13},{10,... | collective-permute-start | bytes 98312 | tf_op jit(solution)/shard_map/ppermute | solution.py:414
  40.8 3.0 %collective-permute-done.17.refs_9_ = f32[8,128]{1,0:T(8,128)S(1)} collective-permute-done((f32[8,128]{1,0:T(8,128)S(1)}, f32[8,128]{1,0:T(8,128)S(1)}, u32[]{:S(2)}, u32[]{:S(2)}) %collective-permute-start.17) | collective-permute-done | bytes 4128 | tf_op jit(solution)/shard_map/ppermute | solution.py:408
  43.8 0.8 %collective-permute-start.15 = (f32[64,128]{1,0:T(8,128)S(1)}, f32[64,128]{1,0:T(8,128)S(1)}, u32[]{:S(2)}, u32[]{:S(2)}) collective-permute-start(f32[64,128]{1,0:T(8,128)S(1)} %get-tuple-element.62), channel_id=1, source_target_pairs={{0,2},{1,3},{2,0},{3,1},{4,6},{5,7},{6,4},{7,5},{8,10},{9,11},{10,... | collective-permute-start | bytes 98312 | tf_op jit(solution)/shard_map/ppermute | solution.py:414
  44.6 0.0 collective-permute-done.12.refs_4_
  44.6 0.0 collective-permute-done.13.refs_5_
  44.6 3.1 %collective-permute-done.15.refs_7_ = f32[64,128]{1,0:T(8,128)S(1)} collective-permute-done((f32[64,128]{1,0:T(8,128)S(1)}, f32[64,128]{1,0:T(8,128)S(1)}, u32[]{:S(2)}, u32[]{:S(2)}) %collective-permute-start.15) | collective-permute-done | bytes 32800 | tf_op jit(solution)/shard_map/ppermute | solution.py:414
  47.7 3.2 %step.5 = (f32[128,128]{1,0:T(8,128)S(1)}, f32[64,128]{1,0:T(8,128)S(1)}, f32[64,128]{1,0:T(8,128)S(1)}, f32[64,128]{1,0:T(8,128)S(1)}, f32[64,128]{1,0:T(8,128)...) custom-call(s32[1,128]{1,0:T(1,128)S(1)} %get-tuple-element.39.refs_0_, ...), custom_call_target="tpu_custom_call" | custom-call | tf_op jit(solution)/shard_map/step/pallas_call | solution.py:428
  51.0 1.0 %collective-permute-start.23 = (f32[8,128]{1,0:T(8,128)S(1)}, f32[8,128]{1,0:T(8,128)S(1)}, u32[]{:S(2)}, u32[]{:S(2)}) collective-permute-start(f32[8,128]{1,0:T(8,128)S(1)} %get-tuple-element.71), channel_id=1, source_target_pairs={{0,31},{1,2},{2,1},{3,4},{4,3},{5,6},{6,5},{7,8},{8,7},{9,10},{10,... | collective-permute-start | bytes 12296 | tf_op jit(solution)/shard_map/ppermute | solution.py:408
  52.0 0.0 collective-permute-start.22
  52.0 0.0 collective-permute-start.18
  52.0 1.6 %collective-permute-start.20 = (f32[64,128]{1,0:T(8,128)S(1)}, f32[64,128]{1,0:T(8,128)S(1)}, u32[]{:S(2)}, u32[]{:S(2)}) collective-permute-start(f32[64,128]{1,0:T(8,128)S(1)} %get-tuple-element.68), channel_id=1, source_target_pairs={{0,4},{1,5},{2,6},{3,7},{4,0},{5,1},{6,2},{7,3},{8,12},{9,13},{10,... | collective-permute-start | bytes 98312 | tf_op jit(solution)/shard_map/ppermute | solution.py:414
  53.6 4.1 %collective-permute-done.23.refs_9_ = f32[8,128]{1,0:T(8,128)S(1)} collective-permute-done((f32[8,128]{1,0:T(8,128)S(1)}, f32[8,128]{1,0:T(8,128)S(1)}, u32[]{:S(2)}, u32[]{:S(2)}) %collective-permute-start.23) | collective-permute-done | bytes 4128 | tf_op jit(solution)/shard_map/ppermute | solution.py:408
  57.7 0.8 %collective-permute-start.21 = (f32[64,128]{1,0:T(8,128)S(1)}, f32[64,128]{1,0:T(8,128)S(1)}, u32[]{:S(2)}, u32[]{:S(2)}) collective-permute-start(f32[64,128]{1,0:T(8,128)S(1)} %get-tuple-element.69), channel_id=1, source_target_pairs={{0,2},{1,3},{2,0},{3,1},{4,6},{5,7},{6,4},{7,5},{8,10},{9,11},{10,... | collective-permute-start | bytes 98312 | tf_op jit(solution)/shard_map/ppermute | solution.py:414
  58.5 3.1 %collective-permute-done.21.refs_7_ = f32[64,128]{1,0:T(8,128)S(1)} collective-permute-done((f32[64,128]{1,0:T(8,128)S(1)}, f32[64,128]{1,0:T(8,128)S(1)}, u32[]{:S(2)}, u32[]{:S(2)}) %collective-permute-start.21) | collective-permute-done | bytes 32800 | tf_op jit(solution)/shard_map/ppermute | solution.py:414
  61.6 3.1 %last.1 = (f32[128,128]{1,0:T(8,128)S(1)}, f32[32,128]{1,0:T(8,128)S(1)}) custom-call(s32[1,128]{1,0:T(1,128)S(1)} %get-tuple-element.39.refs_0_, f32[128,128]{1,0:T(8,128)S(1)} %get-tuple-element.65.refs_1_.refs_3_, f32[128,128]{1,0:T(8,128)S(1)} %bitcast.19, f32[1,128]{1,0:T(1,128)S(1)} %get-tuple-element.40.refs_3_.scale_ref, ...), custom_call_target="tpu_custom_call" | custom-call | tf_op jit(solution)/shard_map/last/pallas_call | solution.py:439
  64.7 8.9 %all_to_all.11 = f32[32,1,128]{2,1,0:T(1,128)S(1)} all-to-all(f32[32,1,128]{2,1,0:T(1,128)S(1)} %bitcast.25), channel_id=1, replica_groups=mesh['rows'=32] {'rows'}, dimensions={0} | all-to-all | bytes 32768 | tf_op jit(solution)/shard_map/all_to_all | solution.py:449
  73.5 0.9 %finish.1 = (f32[128,128]{1,0:T(8,128)}, f32[128,128]{1,0:T(8,128)}) custom-call(f32[32,128]{1,0:T(8,128)S(1)} %bitcast.24, f32[1,128]{1,0:T(1,128)S(1)} %get-tuple-element.40.refs_3_.scale_ref, f32[128,128]{1,0:T(8,128)S(1)} %bitcast.23, f32[128,128]{1,0:T(8,128)S(1)} %get-tuple-element.51.refs_1_.refs_14_, ...), custom_call_target="tpu_custom_call" | custom-call | tf_op jit(solution)/shard_map/finish/pallas_call | solution.py:450
  (11 shorter events, 0.0 us)
Async XLA Ops:
  0.6 19.6 %copy-start.1 = (f32[16384]{0:T(1024)S(1)}, f32[16384]{0:T(1024)}, u32[]{:S(2)}) copy-start(f32[16384]{0:T(1024)} %param.10) | copy-start | bytes 196612
  0.6 19.6 %copy-start = (f32[16384]{0:T(1024)S(1)}, f32[16384]{0:T(1024)}, u32[]{:S(2)}) copy-start(f32[16384]{0:T(1024)} %param.11) | copy-start | bytes 196612
  7.5 8.8 %collective-permute-start.5 = (f32[8,128]{1,0:T(8,128)S(1)}, f32[8,128]{1,0:T(8,128)S(1)}, u32[]{:S(2)}, u32[]{:S(2)}) collective-permute-start(f32[8,128]{1,0:T(8,128)S(1)} %get-tuple-element.46), channel_id=1, source_target_pairs={{0,31},{1,2},{2,1},{3,4},{4,3},{5,6},{6,5},{7,8},{8,7},{9,10},{10,... | collective-permute-start | bytes 12296 | tf_op jit(solution)/shard_map/ppermute | solution.py:408
  14.0 6.3 %collective-permute-start.4 = (f32[72,128]{1,0:T(8,128)S(1)}, f32[72,128]{1,0:T(8,128)S(1)}, u32[]{:S(2)}, u32[]{:S(2)}) collective-permute-start(f32[72,128]{1,0:T(8,128)S(1)} %get-tuple-element.45), channel_id=1, source_target_pairs={{0,1},{1,0},{2,3},{3,2},{4,5},{5,4},{6,7},{7,6},{8,9},{9,8},{10,11... | collective-permute-start | bytes 110600 | tf_op jit(solution)/shard_map/ppermute | solution.py:414
  14.0 4.8 %collective-permute-start = (f32[64,128]{1,0:T(8,128)S(1)}, f32[64,128]{1,0:T(8,128)S(1)}, u32[]{:S(2)}, u32[]{:S(2)}) collective-permute-start(f32[64,128]{1,0:T(8,128)S(1)} %get-tuple-element.41), channel_id=1, source_target_pairs={{0,16},{1,17},{2,18},{3,19},{4,20},{5,21},{6,22},{7,23},{8,24},{9,... | collective-permute-start | bytes 98312 | tf_op jit(solution)/shard_map/ppermute | solution.py:414
  14.0 4.8 %collective-permute-start.1 = (f32[64,128]{1,0:T(8,128)S(1)}, f32[64,128]{1,0:T(8,128)S(1)}, u32[]{:S(2)}, u32[]{:S(2)}) collective-permute-start(f32[64,128]{1,0:T(8,128)S(1)} %get-tuple-element.42), channel_id=1, source_target_pairs={{0,8},{1,9},{2,10},{3,11},{4,12},{5,13},{6,14},{7,15},{8,0},{9,1},... | collective-permute-start | bytes 98312 | tf_op jit(solution)/shard_map/ppermute | solution.py:414
  15.0 3.9 %collective-permute-start.2 = (f32[64,128]{1,0:T(8,128)S(1)}, f32[64,128]{1,0:T(8,128)S(1)}, u32[]{:S(2)}, u32[]{:S(2)}) collective-permute-start(f32[64,128]{1,0:T(8,128)S(1)} %get-tuple-element.43), channel_id=1, source_target_pairs={{0,4},{1,5},{2,6},{3,7},{4,0},{5,1},{6,2},{7,3},{8,12},{9,13},{10,... | collective-permute-start | bytes 98312 | tf_op jit(solution)/shard_map/ppermute | solution.py:414
  16.3 3.9 %collective-permute-start.3 = (f32[64,128]{1,0:T(8,128)S(1)}, f32[64,128]{1,0:T(8,128)S(1)}, u32[]{:S(2)}, u32[]{:S(2)}) collective-permute-start(f32[64,128]{1,0:T(8,128)S(1)} %get-tuple-element.44), channel_id=1, source_target_pairs={{0,2},{1,3},{2,0},{3,1},{4,6},{5,7},{6,4},{7,5},{8,10},{9,11},{10,... | collective-permute-start | bytes 98312 | tf_op jit(solution)/shard_map/ppermute | solution.py:414
  23.3 6.8 %collective-permute-start.11 = (f32[8,128]{1,0:T(8,128)S(1)}, f32[8,128]{1,0:T(8,128)S(1)}, u32[]{:S(2)}, u32[]{:S(2)}) collective-permute-start(f32[8,128]{1,0:T(8,128)S(1)} %get-tuple-element.57), channel_id=1, source_target_pairs={{0,31},{1,2},{2,1},{3,4},{4,3},{5,6},{6,5},{7,8},{8,7},{9,10},{10,... | collective-permute-start | bytes 12296 | tf_op jit(solution)/shard_map/ppermute | solution.py:408
  26.6 7.4 %collective-permute-start.10 = (f32[72,128]{1,0:T(8,128)S(1)}, f32[72,128]{1,0:T(8,128)S(1)}, u32[]{:S(2)}, u32[]{:S(2)}) collective-permute-start(f32[72,128]{1,0:T(8,128)S(1)} %get-tuple-element.56), channel_id=1, source_target_pairs={{0,1},{1,0},{2,3},{3,2},{4,5},{5,4},{6,7},{7,6},{8,9},{9,8},{10,11... | collective-permute-start | bytes 110600 | tf_op jit(solution)/shard_map/ppermute | solution.py:414
  26.6 4.8 %collective-permute-start.6 = (f32[64,128]{1,0:T(8,128)S(1)}, f32[64,128]{1,0:T(8,128)S(1)}, u32[]{:S(2)}, u32[]{:S(2)}) collective-permute-start(f32[64,128]{1,0:T(8,128)S(1)} %get-tuple-element.52), channel_id=1, source_target_pairs={{0,16},{1,17},{2,18},{3,19},{4,20},{5,21},{6,22},{7,23},{8,24},{9,... | collective-permute-start | bytes 98312 | tf_op jit(solution)/shard_map/ppermute | solution.py:414
  26.6 4.8 %collective-permute-start.7 = (f32[64,128]{1,0:T(8,128)S(1)}, f32[64,128]{1,0:T(8,128)S(1)}, u32[]{:S(2)}, u32[]{:S(2)}) collective-permute-start(f32[64,128]{1,0:T(8,128)S(1)} %get-tuple-element.53), channel_id=1, source_target_pairs={{0,8},{1,9},{2,10},{3,11},{4,12},{5,13},{6,14},{7,15},{8,0},{9,1},... | collective-permute-start | bytes 98312 | tf_op jit(solution)/shard_map/ppermute | solution.py:414
  26.6 4.8 %collective-permute-start.8 = (f32[64,128]{1,0:T(8,128)S(1)}, f32[64,128]{1,0:T(8,128)S(1)}, u32[]{:S(2)}, u32[]{:S(2)}) collective-permute-start(f32[64,128]{1,0:T(8,128)S(1)} %get-tuple-element.54), channel_id=1, source_target_pairs={{0,4},{1,5},{2,6},{3,7},{4,0},{5,1},{6,2},{7,3},{8,12},{9,13},{10,... | collective-permute-start | bytes 98312 | tf_op jit(solution)/shard_map/ppermute | solution.py:414
  30.1 3.9 %collective-permute-start.9 = (f32[64,128]{1,0:T(8,128)S(1)}, f32[64,128]{1,0:T(8,128)S(1)}, u32[]{:S(2)}, u32[]{:S(2)}) collective-permute-start(f32[64,128]{1,0:T(8,128)S(1)} %get-tuple-element.55), channel_id=1, source_target_pairs={{0,2},{1,3},{2,0},{3,1},{4,6},{5,7},{6,4},{7,5},{8,10},{9,11},{10,... | collective-permute-start | bytes 98312 | tf_op jit(solution)/shard_map/ppermute | solution.py:414
  37.1 6.7 %collective-permute-start.17 = (f32[8,128]{1,0:T(8,128)S(1)}, f32[8,128]{1,0:T(8,128)S(1)}, u32[]{:S(2)}, u32[]{:S(2)}) collective-permute-start(f32[8,128]{1,0:T(8,128)S(1)} %get-tuple-element.64), channel_id=1, source_target_pairs={{0,31},{1,2},{2,1},{3,4},{4,3},{5,6},{6,5},{7,8},{8,7},{9,10},{10,... | collective-permute-start | bytes 12296 | tf_op jit(solution)/shard_map/ppermute | solution.py:408
  39.2 8.5 %collective-permute-start.16 = (f32[72,128]{1,0:T(8,128)S(1)}, f32[72,128]{1,0:T(8,128)S(1)}, u32[]{:S(2)}, u32[]{:S(2)}) collective-permute-start(f32[72,128]{1,0:T(8,128)S(1)} %get-tuple-element.63), channel_id=1, source_target_pairs={{0,1},{1,0},{2,3},{3,2},{4,5},{5,4},{6,7},{7,6},{8,9},{9,8},{10,11... | collective-permute-start | bytes 110600 | tf_op jit(solution)/shard_map/ppermute | solution.py:414
  39.2 5.4 %collective-permute-start.12 = (f32[64,128]{1,0:T(8,128)S(1)}, f32[64,128]{1,0:T(8,128)S(1)}, u32[]{:S(2)}, u32[]{:S(2)}) collective-permute-start(f32[64,128]{1,0:T(8,128)S(1)} %get-tuple-element.59), channel_id=1, source_target_pairs={{0,16},{1,17},{2,18},{3,19},{4,20},{5,21},{6,22},{7,23},{8,24},{9,... | collective-permute-start | bytes 98312 | tf_op jit(solution)/shard_map/ppermute | solution.py:414
  39.2 5.4 %collective-permute-start.13 = (f32[64,128]{1,0:T(8,128)S(1)}, f32[64,128]{1,0:T(8,128)S(1)}, u32[]{:S(2)}, u32[]{:S(2)}) collective-permute-start(f32[64,128]{1,0:T(8,128)S(1)} %get-tuple-element.60), channel_id=1, source_target_pairs={{0,8},{1,9},{2,10},{3,11},{4,12},{5,13},{6,14},{7,15},{8,0},{9,1},... | collective-permute-start | bytes 98312 | tf_op jit(solution)/shard_map/ppermute | solution.py:414
  39.2 5.4 %collective-permute-start.14 = (f32[64,128]{1,0:T(8,128)S(1)}, f32[64,128]{1,0:T(8,128)S(1)}, u32[]{:S(2)}, u32[]{:S(2)}) collective-permute-start(f32[64,128]{1,0:T(8,128)S(1)} %get-tuple-element.61), channel_id=1, source_target_pairs={{0,4},{1,5},{2,6},{3,7},{4,0},{5,1},{6,2},{7,3},{8,12},{9,13},{10,... | collective-permute-start | bytes 98312 | tf_op jit(solution)/shard_map/ppermute | solution.py:414
  43.8 3.9 %collective-permute-start.15 = (f32[64,128]{1,0:T(8,128)S(1)}, f32[64,128]{1,0:T(8,128)S(1)}, u32[]{:S(2)}, u32[]{:S(2)}) collective-permute-start(f32[64,128]{1,0:T(8,128)S(1)} %get-tuple-element.62), channel_id=1, source_target_pairs={{0,2},{1,3},{2,0},{3,1},{4,6},{5,7},{6,4},{7,5},{8,10},{9,11},{10,... | collective-permute-start | bytes 98312 | tf_op jit(solution)/shard_map/ppermute | solution.py:414
  51.0 6.7 %collective-permute-start.23 = (f32[8,128]{1,0:T(8,128)S(1)}, f32[8,128]{1,0:T(8,128)S(1)}, u32[]{:S(2)}, u32[]{:S(2)}) collective-permute-start(f32[8,128]{1,0:T(8,128)S(1)} %get-tuple-element.71), channel_id=1, source_target_pairs={{0,31},{1,2},{2,1},{3,4},{4,3},{5,6},{6,5},{7,8},{8,7},{9,10},{10,... | collective-permute-start | bytes 12296 | tf_op jit(solution)/shard_map/ppermute | solution.py:408
  52.0 9.6 %collective-permute-start.22 = (f32[72,128]{1,0:T(8,128)S(1)}, f32[72,128]{1,0:T(8,128)S(1)}, u32[]{:S(2)}, u32[]{:S(2)}) collective-permute-start(f32[72,128]{1,0:T(8,128)S(1)} %get-tuple-element.70), channel_id=1, source_target_pairs={{0,1},{1,0},{2,3},{3,2},{4,5},{5,4},{6,7},{7,6},{8,9},{9,8},{10,11... | collective-permute-start | bytes 110600 | tf_op jit(solution)/shard_map/ppermute | solution.py:414
  52.0 6.5 %collective-permute-start.18 = (f32[64,128]{1,0:T(8,128)S(1)}, f32[64,128]{1,0:T(8,128)S(1)}, u32[]{:S(2)}, u32[]{:S(2)}) collective-permute-start(f32[64,128]{1,0:T(8,128)S(1)} %get-tuple-element.66), channel_id=1, source_target_pairs={{0,16},{1,17},{2,18},{3,19},{4,20},{5,21},{6,22},{7,23},{8,24},{9,... | collective-permute-start | bytes 98312 | tf_op jit(solution)/shard_map/ppermute | solution.py:414
  52.0 6.5 %collective-permute-start.19 = (f32[64,128]{1,0:T(8,128)S(1)}, f32[64,128]{1,0:T(8,128)S(1)}, u32[]{:S(2)}, u32[]{:S(2)}) collective-permute-start(f32[64,128]{1,0:T(8,128)S(1)} %get-tuple-element.67), channel_id=1, source_target_pairs={{0,8},{1,9},{2,10},{3,11},{4,12},{5,13},{6,14},{7,15},{8,0},{9,1},... | collective-permute-start | bytes 98312 | tf_op jit(solution)/shard_map/ppermute | solution.py:414
  52.0 6.5 %collective-permute-start.20 = (f32[64,128]{1,0:T(8,128)S(1)}, f32[64,128]{1,0:T(8,128)S(1)}, u32[]{:S(2)}, u32[]{:S(2)}) collective-permute-start(f32[64,128]{1,0:T(8,128)S(1)} %get-tuple-element.68), channel_id=1, source_target_pairs={{0,4},{1,5},{2,6},{3,7},{4,0},{5,1},{6,2},{7,3},{8,12},{9,13},{10,... | collective-permute-start | bytes 98312 | tf_op jit(solution)/shard_map/ppermute | solution.py:414
  57.7 3.9 %collective-permute-start.21 = (f32[64,128]{1,0:T(8,128)S(1)}, f32[64,128]{1,0:T(8,128)S(1)}, u32[]{:S(2)}, u32[]{:S(2)}) collective-permute-start(f32[64,128]{1,0:T(8,128)S(1)} %get-tuple-element.69), channel_id=1, source_target_pairs={{0,2},{1,3},{2,0},{3,1},{4,6},{5,7},{6,4},{7,5},{8,10},{9,11},{10,... | collective-permute-start | bytes 98312 | tf_op jit(solution)/shard_map/ppermute | solution.py:414
where the time goes:
time: 74.6 us; the launch traced here: 74.4 us
  starting transfers between devices  22.3 us (30%)
  waiting for transfers between devices  22.3 us (30%)
  Pallas kernels  20.2 us (27%)
  blocking collectives  8.86 us (12%)
    ppermute x20, waiting for transfers between devices, exchange(): got.append(lax.ppermute(sends[level], 'rows', pairs))  13.3 us
    ppermute x4, starting transfers between devices, exchange(): edges = lax.ppermute(edge, 'rows', far)  12.8 us
    ppermute x20, starting transfers between devices, exchange(): got.append(lax.ppermute(sends[level], 'rows', pairs))  9.48 us
    pallas_call x3, Pallas kernels, per_device(): pl.pallas_call(functools.partial(step_kernel, **common), out_shape=[shape...  9.39 us
    ppermute x4, waiting for transfers between devices, exchange(): edges = lax.ppermute(edge, 'rows', far)  9.03 us
    all_to_all x1, blocking collectives, per_device(): sums = lax.all_to_all(sums, 'rows', 0, 0, tiled=True)  8.86 us
    pallas_call x1, Pallas kernels, per_device(): pl.pallas_call(functools.partial(prepare, nb=nb, levels=levels, half=half...  6.82 us
    pallas_call x1, Pallas kernels, per_device(): pl.pallas_call(functools.partial(last_kernel, **common), out_shape=[shape...  3.06 us
  transfers between devices with their start and end apart: 24, of which 10 were waited for; matrix products, arithmetic and copies ran while one was open for 0% of the time, Pallas kernels for 0%

commit v1 on v0

--- a/solution.py
+++ b/solution.py
@@ -62,13 +62,13 @@
     parity_ref, dict_hbm, *refs, nb, levels, half, merged, groups, sure, entries, sources,
 ):
     small_hbm, refs = refs[:8], refs[8:]
-    sends, (edge_ref, select_ref, gather_ref, scatter_ref, wide_ref, table_ref, scale_ref) = (
-        refs[:levels], refs[levels : levels + 7],
-    )
-    dict_vmem, here_ref, source_ref, signed_ref, *small, small_sems, sems = refs[levels + 7 :]
+    sends, (edge_ref, select_ref, gather_ref, scatter_ref, dict_vmem, table_ref) = (
+        refs[:levels], refs[levels : levels + 6],
+    )
+    facts_ref, *small, small_sems, sems = refs[levels + 6 :]
     vec_vmem, own_ids_ref, own_weights_ref, near_ids_ref, near_weights_ref, *link_refs = small
     link_rows_ref, link_ids_ref, link_weights_ref = link_refs
-    blocks, width, _ = dict_hbm.shape
+    blocks, _, _ = dict_hbm.shape
     parts = sems.shape[0]
     per = blocks // parts
 
@@ -116,11 +116,20 @@
     away = jnp.where(is_link, lane - nb, jnp.where(is_tail, after, -1))
     away = jnp.where(is_lower, jnp.where(lane > nb, lane - nb - 1, before), away)
 
+    eye = onehot(iota((nb, nb), 0) == iota((nb, nb), 1)).astype(BF16)
+    linked = onehot(iota((nb, links), 0) == plus[:, 2 * nb : tail]).astype(BF16)
+    select_ref[...] = dot(linked, eye, TN).astype(BF16)
+
     member = onehot(iota((blocks, entries), 0) == ids)
-    earlier = onehot(iota((entries, entries), 0) < iota((entries, entries), 1)).astype(BF16)
-    ahead = dot(member.astype(BF16), earlier)
-    rank = jnp.sum(member * ahead, axis=0, keepdims=True)
-    count = jnp.sum(member, axis=1, keepdims=True)
+    earlier = onehot(iota((128, 128), 0) < iota((128, 128), 1)).astype(BF16)
+    ahead = []
+    so_far = jnp.zeros((blocks, 1), F32)
+    for start in range(0, entries, 128):
+        part = member[:, start : start + 128]
+        ahead.append(dot(part.astype(BF16), earlier) + so_far)
+        so_far = so_far + jnp.sum(part, axis=1, keepdims=True)
+    rank = jnp.sum(member * jnp.concatenate(ahead, axis=1), axis=0, keepdims=True)
+    count = so_far
     more = jnp.maximum(jnp.floor((count - 1.0) * (1.0 / SLOT)), 0.0)
     before_block = onehot(iota((blocks, blocks), 1) < iota((blocks, blocks), 0)).astype(BF16)
     more_wide = jnp.broadcast_to(more, (blocks, 128))
@@ -143,55 +152,52 @@
     total = jnp.sum(more_wide, axis=0, keepdims=True)
     table_ref[...] = jnp.where(iota((1, 128), 1) == 127, total, table).astype(jnp.int32)
 
-    row_iota = iota((nb, entries), 0)
-    target = onehot(row_iota == plus)
-    source_iota = iota((sources, entries), 0)
-    source_ref[...] = (onehot(source_iota == plus) - onehot(source_iota == away)).astype(BF16)
-    signed = target - onehot(row_iota == minus)
     high, low = halves(weights)
-    signed_ref[...] = jnp.concatenate([signed * high, signed * low], axis=0).astype(BF16)
-    span = sure * GROUP
-    here_ref[...] = onehot(iota((span, entries), 0) == slot).astype(BF16)
-    gather_ref[0:span, :] = dot(here_ref[...], source_ref[...], NT).astype(BF16)
-    scatter_ref[:, 0:span] = dot(signed_ref[...], here_ref[...], NT).astype(BF16)
+    absent = away < 0
+    facts = [
+        plus.astype(F32), jnp.where(absent, 256, away - 256).astype(F32), minus.astype(F32), high, low,
+    ]
+    facts = jnp.concatenate(facts + [jnp.zeros((128 - len(facts), entries), F32)], axis=0)
+    facts_ref[...] = facts.astype(BF16)
+
+    def fill(start, count):
+        here = onehot(iota((count, entries), 0) + start == slot).astype(BF16)
+        known = dot(here, facts_ref[...], NT)
+        source = iota((count, sources), 1).astype(F32)
+        picked = jnp.where(source == known[:, 0:1], 1.0, jnp.where(source - 256.0 == known[:, 1:2], -1.0, 0.0))
+        gather_ref[start : start + count, :] = picked.astype(BF16)
+        for at in range(0, count, 128):
+            across = known[at : at + 128].T
+            row = iota((nb, 128), 0).astype(F32)
+            up, down = row == across[0:1], row == across[2:3]
+            span = slice(start + at, start + at + 128)
+            for half_index in range(2):
+                weight = across[3 + half_index : 4 + half_index]
+                signed = jnp.where(up, weight, jnp.where(down, -weight, 0.0))
+                scatter_ref[half_index * nb : (half_index + 1) * nb, span] = signed.astype(BF16)
+
+    fill(0, sure * GROUP)
     used_chunks = jnp.sum(more).astype(jnp.int32)
     chunks = GROUP // SLOT
     for group in range(sure, groups):
 
         @pl.when(used_chunks > (group - blocks * SLOT // GROUP) * chunks)
         def _(group=group):
-            at = slice(group * GROUP, (group + 1) * GROUP)
-            here = onehot(iota((GROUP, entries), 0) + group * GROUP == slot).astype(BF16)
-            gather_ref[at, :] = dot(here, source_ref[...], NT).astype(BF16)
-            scatter_ref[:, at] = dot(signed_ref[...], here, NT).astype(BF16)
-
-    eye = onehot(iota((nb, nb), 0) == iota((nb, nb), 1)).astype(BF16)
-    select_ref[...] = dot(target[:, 2 * nb : tail].astype(BF16), eye, TN).astype(BF16)
+            fill(group * GROUP, GROUP)
+
     load_small[0].wait()
     send_blocks(select_ref, vec_vmem[...], sends, edge_ref, merged)
-
-    def split_block(k, acc):
-        block = dict_vmem[k]
-        block_high = block.astype(BF16)
-        wide_ref[k, :, 0:width] = block_high
-        wide_ref[k, :, width : 2 * width] = (block - block_high.astype(F32)).astype(BF16)
-        return acc + block
-
-    acc = jnp.zeros((width, width), F32)
     for part in range(parts):
         load(part).wait()
-        acc = lax.fori_loop(part * per, (part + 1) * per, split_block, acc, unroll=4)
-    diagonal = onehot(iota((width, width), 0) == iota((width, width), 1))
-    trace = jnp.sum(jnp.sum(acc * diagonal, axis=0, keepdims=True), axis=1, keepdims=True)
-    scale = 1.0 / (trace * (4.25 / (blocks * width)) + 0.5)
-    scale_ref[...] = jnp.broadcast_to(scale, (1, 128))
 
 
 def apply_operator(
     table_ref, vec_ref, shift_ref, scale_ref, recv_refs, edge_ref,
-    gather_ref, scatter_ref, wide_ref, scratch, *, half, merged, sure,
+    gather_ref, scatter_ref, wide_ref, scratch, *, half, merged, sure, dict_ref=None,
 ):
-    sources_ref, lhs_ref, prod_ref = scratch
+    sources_ref, lhs_ref, prod_ref, table_smem, table_sem = scratch
+    copy_table = pltpu.make_async_copy(table_ref, table_smem, table_sem)
+    copy_table.start()
     nb, width = vec_ref.shape
     blocks = wide_ref.shape[0]
     chunks = GROUP // SLOT
@@ -226,10 +232,21 @@
     picked = dot(gather_ref[0:span, :], sources_ref[...])
     for c, lhs in enumerate(stage(picked)):
         lhs_ref[c * 2 * SLOT : (c + 1) * 2 * SLOT, :] = lhs
+    total = jnp.zeros((width, width), F32)
     for pair in range(span // SLOT // 2):
         prods = []
         for c in (2 * pair, 2 * pair + 1):
-            block = wide_ref[c] if c < blocks else wide_ref[table_ref[0, c - blocks]]
+            if c == blocks:
+                copy_table.wait()
+            if c >= blocks:
+                block = wide_ref[table_smem[0, c - blocks]]
+            elif dict_ref is None:
+                block = wide_ref[c]
+            else:
+                block = dict_ref[c]
+                total = total + block
+                block = halves_wide(block)
+                wide_ref[c] = block
             prods.append(product(lhs_ref[c * 2 * SLOT : (c + 1) * 2 * SLOT, :], block))
         prod_ref[pair * 2 * SLOT : (pair + 1) * 2 * SLOT, :] = halves_wide(jnp.concatenate(prods, axis=0))
     out = rows_of(dot(scatter_ref[:, 0:span], prod_ref[...]))
@@ -237,11 +254,29 @@
     def further(group, out):
         at = pl.ds(pl.multiple_of(blocks * SLOT + group * GROUP, GROUP), GROUP)
         lhs = list(stage(dot(gather_ref[at, :], sources_ref[...])))
-        prods = [product(lhs[c], wide_ref[table_ref[0, group * chunks + c]]) for c in range(chunks)]
+        prods = [product(lhs[c], wide_ref[table_smem[0, group * chunks + c]]) for c in range(chunks)]
         return out + rows_of(dot(scatter_ref[:, at], halves_wide(jnp.concatenate(prods, axis=0))))
 
-    out = lax.fori_loop(sure - blocks * SLOT // GROUP, (table_ref[0, 127] + chunks - 1) // chunks, further, out)
+    out = lax.fori_loop(sure - blocks * SLOT // GROUP, (table_smem[0, 127] + chunks - 1) // chunks, further, out)
+    if dict_ref is not None:
+        diagonal = onehot(iota((width, width), 0) == iota((width, width), 1))
+        trace = jnp.sum(jnp.sum(total * diagonal, axis=0, keepdims=True), axis=1, keepdims=True)
+        scale = 1.0 / (trace * (4.25 / (blocks * width)) + 0.5)
+        scale_ref[...] = jnp.broadcast_to(scale, (1, 128))
     return (shift_ref[...] * vec + out) * scale_ref[...] - SHIFT * vec
+
+
+def first_kernel(*refs, levels, half, merged, sure):
+    table_ref, vec_ref, shift_ref, *rest = refs
+    recv_refs, rest = rest[:levels], rest[levels:]
+    edge_ref, select_ref, gather_ref, scatter_ref, dict_ref, next_ref, *rest = rest
+    sends, (send_edge_ref, wide_ref, scale_ref, *scratch) = rest[:levels], rest[levels:]
+    following = apply_operator(
+        table_ref, vec_ref, shift_ref, scale_ref, recv_refs, edge_ref,
+        gather_ref, scatter_ref, wide_ref, scratch, half=half, merged=merged, sure=sure, dict_ref=dict_ref,
+    )
+    next_ref[...] = following
+    send_blocks(select_ref, following, sends, send_edge_ref, merged)
 
 
 def step_kernel(*refs, levels, half, merged, sure):
@@ -359,6 +394,7 @@
     used = 2 * nb + links + 1
     entries = -(-used // 128) * 128
     sources = -(-(nb + links + 16) // 128) * 128
+    assert sources <= 512 and nb <= 256
     extra = -(-(used // SLOT) // (GROUP // SLOT))
     groups = blocks * SLOT // GROUP + extra
 
@@ -382,25 +418,21 @@
             shape((links, nb), BF16),
             shape((groups * GROUP, sources), BF16),
             shape((2 * nb, groups * GROUP), BF16),
-            shape((blocks, width, 2 * width), BF16),
+            shape((blocks, width, width)),
             shape((1, 128), jnp.int32),
-            shape((1, 128)),
         ],
         in_specs=[pl.BlockSpec(memory_space=pltpu.SMEM)] + [pl.BlockSpec(memory_space=pltpu.HBM)] * 9,
-        out_specs=vmem(levels + 7),
+        out_specs=vmem(levels + 6),
         scratch_shapes=[
-            pltpu.VMEM((blocks, width, width), F32),
-            pltpu.VMEM((sure * GROUP, entries), BF16),
-            pltpu.VMEM((sources, entries), BF16),
-            pltpu.VMEM((2 * nb, entries), BF16),
+            pltpu.VMEM((128, entries), BF16),
             *(pltpu.VMEM(array.shape, array.dtype) for array in small),
             pltpu.SemaphoreType.DMA((len(small),)),
             pltpu.SemaphoreType.DMA((4,)),
         ],
-        compiler_params=params(40),
+        compiler_params=params(24),
         name="prepare",
 )(parity, *(pltpu.with_memory_space_constraint(array, pltpu.HBM) for array in [dictionary] + small))
-    sends, (edge, select, gather, scatter, wide, table, scale) = outs[:levels], outs[levels:]
+    sends, (edge, select, gather, scatter, blocks_vmem, table) = outs[:levels], outs[levels:]
 
     def exchange(sends, edge):
         near = [(i, i ^ 1) for i in range(devices)]
@@ -418,17 +450,30 @@
         pltpu.VMEM((sources, 2 * width), BF16),
         pltpu.VMEM((2 * sure * GROUP, width), BF16),
         pltpu.VMEM((sure * GROUP, 2 * width), BF16),
+        pltpu.SMEM((1, 128), jnp.int32),
+        pltpu.SemaphoreType.DMA,
     ]
-    smem = [pl.BlockSpec(memory_space=pltpu.SMEM)]
     basis = [first]
     for k in range(ITERS):
         got, edges = exchange(sends, edge)
         common = dict(levels=levels, half=half, merged=merged, sure=sure)
-        if k + 1 < ITERS:
+        if k == 0:
+            following, *outs = pl.pallas_call(
+                functools.partial(first_kernel, **common),
+                out_shape=[shape((nb, width))] + send_shapes
+                + [edge_shape, shape((blocks, width, 2 * width), BF16), shape((1, 128))],
+                in_specs=vmem(8 + levels),
+                out_specs=vmem(levels + 4),
+                scratch_shapes=scratch,
+                compiler_params=params(24),
+                name="first",
+            )(table, first, shifts, *got, edges, select, gather, scatter, blocks_vmem)
+            sends, (edge, wide, scale) = outs[:levels], outs[levels:]
+        elif k + 1 < ITERS:
             following, *outs = pl.pallas_call(
                 functools.partial(step_kernel, **common),
                 out_shape=[shape((nb, width))] + send_shapes + [edge_shape],
-                in_specs=smem + vmem(8 + levels),
+                in_specs=vmem(9 + levels),
                 out_specs=vmem(levels + 2),
                 scratch_shapes=scratch,
                 compiler_params=params(24),
@@ -439,7 +484,7 @@
             following, sums = pl.pallas_call(
                 functools.partial(last_kernel, **common),
                 out_shape=[shape((nb, width)), shape((devices, 128))],
-                in_specs=smem + vmem(7 + levels + ITERS - 1),
+                in_specs=vmem(8 + levels + ITERS - 1),
                 out_specs=vmem(2),
                 scratch_shapes=scratch,
                 compiler_params=params(24),

time: 74.6 us -> 70.9 us (0.950)
  Pallas kernels: 20.2 us -> 16.5 us
    pallas_call x3 -> x2, Pallas kernels: 9.39 us -> 5.58 us  [per_device(): pl.pallas_call(functools.partial(step_kernel, **common), out_shape=[shape...]
    pallas_call x0 -> x1, Pallas kernels: none -> 3.2 us  [per_device(): pl.pallas_call(functools.partial(first_kernel, **common), out_shape=[shap...]
    pallas_call x1, Pallas kernels: 6.82 us -> 4.06 us  [per_device(): pl.pallas_call(functools.partial(prepare, nb=nb, levels=levels, half=half...]
where the time goes in v1:
time: 70.9 us; the launch traced here: 70.7 us
  starting transfers between devices  22.4 us (32%)
  waiting for transfers between devices  22.3 us (31%)
  Pallas kernels  16.5 us (23%)
  blocking collectives  8.87 us (13%)
  between operations  0.75 us (1%)
    ppermute x20, waiting for transfers between devices, exchange(): got.append(lax.ppermute(sends[level], 'rows', pairs))  13.3 us
    ppermute x4, starting transfers between devices, exchange(): edges = lax.ppermute(edge, 'rows', far)  12.9 us
    ppermute x20, starting transfers between devices, exchange(): got.append(lax.ppermute(sends[level], 'rows', pairs))  9.46 us
    ppermute x4, waiting for transfers between devices, exchange(): edges = lax.ppermute(edge, 'rows', far)  8.97 us
    all_to_all x1, blocking collectives, per_device(): sums = lax.all_to_all(sums, 'rows', 0, 0, tiled=True)  8.87 us
    pallas_call x2, Pallas kernels, per_device(): pl.pallas_call(functools.partial(step_kernel, **common), out_shape=[shape...  5.58 us
    pallas_call x1, Pallas kernels, per_device(): pl.pallas_call(functools.partial(prepare, nb=nb, levels=levels, half=half...  4.06 us
    pallas_call x1, Pallas kernels, per_device(): pl.pallas_call(functools.partial(first_kernel, **common), out_shape=[shap...  3.2 us
  transfers between devices with their start and end apart: 24, of which 10 were waited for; matrix products, arithmetic and copies ran while one was open for 0% of the time, Pallas kernels for 0%

profile of v1, /device:TPU:0, one launch (start us, length us, event | category | flops | bytes accessed | tf_op | source)
XLA Modules:
  0.0 70.7 jit_solution(13867902813614510855)
XLA Ops:
  0.7 4.1 %prepare.1 = (f32[64,128]{1,0:T(8,128)S(1)}, f32[64,128]{1,0:T(8,128)S(1)}, f32[64,128]{1,0:T(8,128)S(1)}, f32[64,128]{1,0:T(8,128)S(1)}, f32[72,128]{1,0:T(8,12...) custom-call(s32[1]{0:T(128)} %bitcast.parity_ref, ...), custom_call_target="tpu_custom_call" | custom-call | tf_op jit(solution)/shard_map/prepare/pallas_call | solution.py:410
  4.7 6.5 %collective-permute-start.5 = (f32[8,128]{1,0:T(8,128)S(1)}, f32[8,128]{1,0:T(8,128)S(1)}, u32[]{:S(2)}, u32[]{:S(2)}) collective-permute-start(f32[8,128]{1,0:T(8,128)S(1)} %get-tuple-element.46), channel_id=1, source_target_pairs={{0,31},{1,2},{2,1},{3,4},{4,3},{5,6},{6,5},{7,8},{8,7},{9,10},{10,... | collective-permute-start | bytes 12296 | tf_op jit(solution)/shard_map/ppermute | solution.py:440
  11.2 0.0 collective-permute-start.4
  11.2 0.0 collective-permute-start
  11.2 1.0 %collective-permute-start.1 = (f32[64,128]{1,0:T(8,128)S(1)}, f32[64,128]{1,0:T(8,128)S(1)}, u32[]{:S(2)}, u32[]{:S(2)}) collective-permute-start(f32[64,128]{1,0:T(8,128)S(1)} %get-tuple-element.42), channel_id=1, source_target_pairs={{0,8},{1,9},{2,10},{3,11},{4,12},{5,13},{6,14},{7,15},{8,0},{9,1},... | collective-permute-start | bytes 98312 | tf_op jit(solution)/shard_map/ppermute | solution.py:446
  12.2 1.3 %collective-permute-start.2 = (f32[64,128]{1,0:T(8,128)S(1)}, f32[64,128]{1,0:T(8,128)S(1)}, u32[]{:S(2)}, u32[]{:S(2)}) collective-permute-start(f32[64,128]{1,0:T(8,128)S(1)} %get-tuple-element.43), channel_id=1, source_target_pairs={{0,4},{1,5},{2,6},{3,7},{4,0},{5,1},{6,2},{7,3},{8,12},{9,13},{10,... | collective-permute-start | bytes 98312 | tf_op jit(solution)/shard_map/ppermute | solution.py:446
  13.6 0.0 collective-permute-done.5.refs_8_
  13.6 0.0 collective-permute-start.3
  13.6 2.4 %collective-permute-done.refs_3_ = f32[64,128]{1,0:T(8,128)S(1)} collective-permute-done((f32[64,128]{1,0:T(8,128)S(1)}, f32[64,128]{1,0:T(8,128)S(1)}, u32[]{:S(2)}, u32[]{:S(2)}) %collective-permute-start) | collective-permute-done | bytes 32800 | tf_op jit(solution)/shard_map/ppermute | solution.py:446
  16.0 0.0 collective-permute-done.1.refs_4_
  16.0 0.1 collective-permute-done.2.refs_5_
  16.1 1.3 %collective-permute-done.3.refs_6_ = f32[64,128]{1,0:T(8,128)S(1)} collective-permute-done((f32[64,128]{1,0:T(8,128)S(1)}, f32[64,128]{1,0:T(8,128)S(1)}, u32[]{:S(2)}, u32[]{:S(2)}) %collective-permute-start.3) | collective-permute-done | bytes 32800 | tf_op jit(solution)/shard_map/ppermute | solution.py:446
  17.5 0.0 collective-permute-done.4.refs_7_
  17.5 3.2 %first.1 = (f32[128,128]{1,0:T(8,128)S(1)}, f32[64,128]{1,0:T(8,128)S(1)}, f32[64,128]{1,0:T(8,128)S(1)}, f32[64,128]{1,0:T(8,128)S(1)}, f32[64,128]{1,0:T(8,128...) custom-call(s32[1,128]{1,0:T(1,128)S(1)} %get-tuple-element.40.refs_, ...), custom_call_target="tpu_custom_call" | custom-call | tf_op jit(solution)/shard_map/first/pallas_call | solution.py:461
  20.7 3.3 %collective-permute-start.11 = (f32[8,128]{1,0:T(8,128)S(1)}, f32[8,128]{1,0:T(8,128)S(1)}, u32[]{:S(2)}, u32[]{:S(2)}) collective-permute-start(f32[8,128]{1,0:T(8,128)S(1)} %get-tuple-element.58), channel_id=1, source_target_pairs={{0,31},{1,2},{2,1},{3,4},{4,3},{5,6},{6,5},{7,8},{8,7},{9,10},{10,... | collective-permute-start | bytes 12296 | tf_op jit(solution)/shard_map/ppermute | solution.py:440
  24.0 0.0 collective-permute-start.10
  24.0 0.0 collective-permute-start.6
  24.0 0.0 collective-permute-start.7
  24.0 1.5 %collective-permute-start.8 = (f32[64,128]{1,0:T(8,128)S(1)}, f32[64,128]{1,0:T(8,128)S(1)}, u32[]{:S(2)}, u32[]{:S(2)}) collective-permute-start(f32[64,128]{1,0:T(8,128)S(1)} %get-tuple-element.55), channel_id=1, source_target_pairs={{0,4},{1,5},{2,6},{3,7},{4,0},{5,1},{6,2},{7,3},{8,12},{9,13},{10,... | collective-permute-start | bytes 98312 | tf_op jit(solution)/shard_map/ppermute | solution.py:446
  25.5 1.9 %collective-permute-done.11.refs_9_ = f32[8,128]{1,0:T(8,128)S(1)} collective-permute-done((f32[8,128]{1,0:T(8,128)S(1)}, f32[8,128]{1,0:T(8,128)S(1)}, u32[]{:S(2)}, u32[]{:S(2)}) %collective-permute-start.11) | collective-permute-done | bytes 4128 | tf_op jit(solution)/shard_map/ppermute | solution.py:440
  27.5 0.7 collective-permute-start.9
  28.2 0.6 collective-permute-done.6.refs_4_
  28.8 0.0 collective-permute-done.7.refs_5_
  28.8 2.6 %collective-permute-done.9.refs_7_ = f32[64,128]{1,0:T(8,128)S(1)} collective-permute-done((f32[64,128]{1,0:T(8,128)S(1)}, f32[64,128]{1,0:T(8,128)S(1)}, u32[]{:S(2)}, u32[]{:S(2)}) %collective-permute-start.9) | collective-permute-done | bytes 32800 | tf_op jit(solution)/shard_map/ppermute | solution.py:446
  31.4 0.0 collective-permute-done.10.refs_8_
  31.4 2.7 %step.2 = (f32[128,128]{1,0:T(8,128)S(1)}, f32[64,128]{1,0:T(8,128)S(1)}, f32[64,128]{1,0:T(8,128)S(1)}, f32[64,128]{1,0:T(8,128)S(1)}, f32[64,128]{1,0:T(8,128)...) custom-call(s32[1,128]{1,0:T(1,128)S(1)} %get-tuple-element.40.refs_0_, ...), custom_call_target="tpu_custom_call" | custom-call | tf_op jit(solution)/shard_map/step/pallas_call | solution.py:473
  34.1 2.1 %collective-permute-start.17 = (f32[8,128]{1,0:T(8,128)S(1)}, f32[8,128]{1,0:T(8,128)S(1)}, u32[]{:S(2)}, u32[]{:S(2)}) collective-permute-start(f32[8,128]{1,0:T(8,128)S(1)} %get-tuple-element.66), channel_id=1, source_target_pairs={{0,31},{1,2},{2,1},{3,4},{4,3},{5,6},{6,5},{7,8},{8,7},{9,10},{10,... | collective-permute-start | bytes 12296 | tf_op jit(solution)/shard_map/ppermute | solution.py:440
  36.2 0.0 collective-permute-start.12
  36.3 0.0 collective-permute-start.13
  36.3 1.6 %collective-permute-start.14 = (f32[64,128]{1,0:T(8,128)S(1)}, f32[64,128]{1,0:T(8,128)S(1)}, u32[]{:S(2)}, u32[]{:S(2)}) collective-permute-start(f32[64,128]{1,0:T(8,128)S(1)} %get-tuple-element.63), channel_id=1, source_target_pairs={{0,4},{1,5},{2,6},{3,7},{4,0},{5,1},{6,2},{7,3},{8,12},{9,13},{10,... | collective-permute-start | bytes 98312 | tf_op jit(solution)/shard_map/ppermute | solution.py:446
  37.9 3.0 %collective-permute-done.17.refs_9_ = f32[8,128]{1,0:T(8,128)S(1)} collective-permute-done((f32[8,128]{1,0:T(8,128)S(1)}, f32[8,128]{1,0:T(8,128)S(1)}, u32[]{:S(2)}, u32[]{:S(2)}) %collective-permute-start.17) | collective-permute-done | bytes 4128 | tf_op jit(solution)/shard_map/ppermute | solution.py:440
  40.8 0.8 %collective-permute-start.15 = (f32[64,128]{1,0:T(8,128)S(1)}, f32[64,128]{1,0:T(8,128)S(1)}, u32[]{:S(2)}, u32[]{:S(2)}) collective-permute-start(f32[64,128]{1,0:T(8,128)S(1)} %get-tuple-element.64), channel_id=1, source_target_pairs={{0,2},{1,3},{2,0},{3,1},{4,6},{5,7},{6,4},{7,5},{8,10},{9,11},{10,... | collective-permute-start | bytes 98312 | tf_op jit(solution)/shard_map/ppermute | solution.py:446
  41.6 0.0 collective-permute-done.14.refs_6_
  41.6 3.1 %collective-permute-done.15.refs_7_ = f32[64,128]{1,0:T(8,128)S(1)} collective-permute-done((f32[64,128]{1,0:T(8,128)S(1)}, f32[64,128]{1,0:T(8,128)S(1)}, u32[]{:S(2)}, u32[]{:S(2)}) %collective-permute-start.15) | collective-permute-done | bytes 32800 | tf_op jit(solution)/shard_map/ppermute | solution.py:446
  44.7 0.0 collective-permute-done.16.refs_8_
  44.7 2.9 %step.3 = (f32[128,128]{1,0:T(8,128)S(1)}, f32[64,128]{1,0:T(8,128)S(1)}, f32[64,128]{1,0:T(8,128)S(1)}, f32[64,128]{1,0:T(8,128)S(1)}, f32[64,128]{1,0:T(8,128)...) custom-call(s32[1,128]{1,0:T(1,128)S(1)} %get-tuple-element.40.refs_0_, ...), custom_call_target="tpu_custom_call" | custom-call | tf_op jit(solution)/shard_map/step/pallas_call | solution.py:473
  47.6 1.0 %collective-permute-start.23 = (f32[8,128]{1,0:T(8,128)S(1)}, f32[8,128]{1,0:T(8,128)S(1)}, u32[]{:S(2)}, u32[]{:S(2)}) collective-permute-start(f32[8,128]{1,0:T(8,128)S(1)} %get-tuple-element.73), channel_id=1, source_target_pairs={{0,31},{1,2},{2,1},{3,4},{4,3},{5,6},{6,5},{7,8},{8,7},{9,10},{10,... | collective-permute-start | bytes 12296 | tf_op jit(solution)/shard_map/ppermute | solution.py:440
  48.6 0.0 collective-permute-start.19
  48.7 1.6 %collective-permute-start.20 = (f32[64,128]{1,0:T(8,128)S(1)}, f32[64,128]{1,0:T(8,128)S(1)}, u32[]{:S(2)}, u32[]{:S(2)}) collective-permute-start(f32[64,128]{1,0:T(8,128)S(1)} %get-tuple-element.70), channel_id=1, source_target_pairs={{0,4},{1,5},{2,6},{3,7},{4,0},{5,1},{6,2},{7,3},{8,12},{9,13},{10,... | collective-permute-start | bytes 98312 | tf_op jit(solution)/shard_map/ppermute | solution.py:446
  50.3 4.1 %collective-permute-done.23.refs_9_ = f32[8,128]{1,0:T(8,128)S(1)} collective-permute-done((f32[8,128]{1,0:T(8,128)S(1)}, f32[8,128]{1,0:T(8,128)S(1)}, u32[]{:S(2)}, u32[]{:S(2)}) %collective-permute-start.23) | collective-permute-done | bytes 4128 | tf_op jit(solution)/shard_map/ppermute | solution.py:440
  54.3 0.8 %collective-permute-start.21 = (f32[64,128]{1,0:T(8,128)S(1)}, f32[64,128]{1,0:T(8,128)S(1)}, u32[]{:S(2)}, u32[]{:S(2)}) collective-permute-start(f32[64,128]{1,0:T(8,128)S(1)} %get-tuple-element.71), channel_id=1, source_target_pairs={{0,2},{1,3},{2,0},{3,1},{4,6},{5,7},{6,4},{7,5},{8,10},{9,11},{10,... | collective-permute-start | bytes 98312 | tf_op jit(solution)/shard_map/ppermute | solution.py:446
  55.1 0.0 collective-permute-done.19.refs_5_
  55.1 0.0 collective-permute-done.20.refs_6_
  55.1 3.1 %collective-permute-done.21.refs_7_ = f32[64,128]{1,0:T(8,128)S(1)} collective-permute-done((f32[64,128]{1,0:T(8,128)S(1)}, f32[64,128]{1,0:T(8,128)S(1)}, u32[]{:S(2)}, u32[]{:S(2)}) %collective-permute-start.21) | collective-permute-done | bytes 32800 | tf_op jit(solution)/shard_map/ppermute | solution.py:446
  58.2 0.0 collective-permute-done.22.refs_8_
  58.2 2.7 %last.1 = (f32[128,128]{1,0:T(8,128)S(1)}, f32[32,128]{1,0:T(8,128)S(1)}) custom-call(s32[1,128]{1,0:T(1,128)S(1)} %get-tuple-element.40.refs_0_, f32[128,128]{1,0:T(8,128)S(1)} %get-tuple-element.67.refs_1_.refs_3_, f32[128,128]{1,0:T(8,128)S(1)} %bitcast.19, f32[1,128]{1,0:T(1,128)S(1)} %get-tuple-element.52.refs_3_.scale_ref, ...), custom_call_target="tpu_custom_call" | custom-call | tf_op jit(solution)/shard_map/last/pallas_call | solution.py:484
  61.0 8.9 %all_to_all.11 = f32[32,1,128]{2,1,0:T(1,128)S(1)} all-to-all(f32[32,1,128]{2,1,0:T(1,128)S(1)} %bitcast.25), channel_id=1, replica_groups=mesh['rows'=32] {'rows'}, dimensions={0} | all-to-all | bytes 32768 | tf_op jit(solution)/shard_map/all_to_all | solution.py:494
  69.8 0.9 %finish.1 = (f32[128,128]{1,0:T(8,128)}, f32[128,128]{1,0:T(8,128)}) custom-call(f32[32,128]{1,0:T(8,128)S(1)} %bitcast.24, f32[1,128]{1,0:T(1,128)S(1)} %get-tuple-element.52.refs_3_.scale_ref, f32[128,128]{1,0:T(8,128)S(1)} %bitcast.23, f32[128,128]{1,0:T(8,128)S(1)} %get-tuple-element.51.refs_1_.refs_14_, ...), custom_call_target="tpu_custom_call" | custom-call | tf_op jit(solution)/shard_map/finish/pallas_call | solution.py:495
  (11 shorter events, 0.0 us)
Async XLA Ops:
  0.6 16.8 %copy-start.1 = (f32[16384]{0:T(1024)S(1)}, f32[16384]{0:T(1024)}, u32[]{:S(2)}) copy-start(f32[16384]{0:T(1024)} %param.10) | copy-start | bytes 196612
  0.6 16.8 %copy-start = (f32[16384]{0:T(1024)S(1)}, f32[16384]{0:T(1024)}, u32[]{:S(2)}) copy-start(f32[16384]{0:T(1024)} %param.11) | copy-start | bytes 196612
  4.7 8.8 %collective-permute-start.5 = (f32[8,128]{1,0:T(8,128)S(1)}, f32[8,128]{1,0:T(8,128)S(1)}, u32[]{:S(2)}, u32[]{:S(2)}) collective-permute-start(f32[8,128]{1,0:T(8,128)S(1)} %get-tuple-element.46), channel_id=1, source_target_pairs={{0,31},{1,2},{2,1},{3,4},{4,3},{5,6},{6,5},{7,8},{8,7},{9,10},{10,... | collective-permute-start | bytes 12296 | tf_op jit(solution)/shard_map/ppermute | solution.py:440
  11.2 6.3 %collective-permute-start.4 = (f32[72,128]{1,0:T(8,128)S(1)}, f32[72,128]{1,0:T(8,128)S(1)}, u32[]{:S(2)}, u32[]{:S(2)}) collective-permute-start(f32[72,128]{1,0:T(8,128)S(1)} %get-tuple-element.45), channel_id=1, source_target_pairs={{0,1},{1,0},{2,3},{3,2},{4,5},{5,4},{6,7},{7,6},{8,9},{9,8},{10,11... | collective-permute-start | bytes 110600 | tf_op jit(solution)/shard_map/ppermute | solution.py:446
  11.2 4.8 %collective-permute-start = (f32[64,128]{1,0:T(8,128)S(1)}, f32[64,128]{1,0:T(8,128)S(1)}, u32[]{:S(2)}, u32[]{:S(2)}) collective-permute-start(f32[64,128]{1,0:T(8,128)S(1)} %get-tuple-element.41), channel_id=1, source_target_pairs={{0,16},{1,17},{2,18},{3,19},{4,20},{5,21},{6,22},{7,23},{8,24},{9,... | collective-permute-start | bytes 98312 | tf_op jit(solution)/shard_map/ppermute | solution.py:446
  11.2 4.8 %collective-permute-start.1 = (f32[64,128]{1,0:T(8,128)S(1)}, f32[64,128]{1,0:T(8,128)S(1)}, u32[]{:S(2)}, u32[]{:S(2)}) collective-permute-start(f32[64,128]{1,0:T(8,128)S(1)} %get-tuple-element.42), channel_id=1, source_target_pairs={{0,8},{1,9},{2,10},{3,11},{4,12},{5,13},{6,14},{7,15},{8,0},{9,1},... | collective-permute-start | bytes 98312 | tf_op jit(solution)/shard_map/ppermute | solution.py:446
  12.2 3.9 %collective-permute-start.2 = (f32[64,128]{1,0:T(8,128)S(1)}, f32[64,128]{1,0:T(8,128)S(1)}, u32[]{:S(2)}, u32[]{:S(2)}) collective-permute-start(f32[64,128]{1,0:T(8,128)S(1)} %get-tuple-element.43), channel_id=1, source_target_pairs={{0,4},{1,5},{2,6},{3,7},{4,0},{5,1},{6,2},{7,3},{8,12},{9,13},{10,... | collective-permute-start | bytes 98312 | tf_op jit(solution)/shard_map/ppermute | solution.py:446
  13.6 3.9 %collective-permute-start.3 = (f32[64,128]{1,0:T(8,128)S(1)}, f32[64,128]{1,0:T(8,128)S(1)}, u32[]{:S(2)}, u32[]{:S(2)}) collective-permute-start(f32[64,128]{1,0:T(8,128)S(1)} %get-tuple-element.44), channel_id=1, source_target_pairs={{0,2},{1,3},{2,0},{3,1},{4,6},{5,7},{6,4},{7,5},{8,10},{9,11},{10,... | collective-permute-start | bytes 98312 | tf_op jit(solution)/shard_map/ppermute | solution.py:446
  20.7 6.8 %collective-permute-start.11 = (f32[8,128]{1,0:T(8,128)S(1)}, f32[8,128]{1,0:T(8,128)S(1)}, u32[]{:S(2)}, u32[]{:S(2)}) collective-permute-start(f32[8,128]{1,0:T(8,128)S(1)} %get-tuple-element.58), channel_id=1, source_target_pairs={{0,31},{1,2},{2,1},{3,4},{4,3},{5,6},{6,5},{7,8},{8,7},{9,10},{10,... | collective-permute-start | bytes 12296 | tf_op jit(solution)/shard_map/ppermute | solution.py:440
  24.0 7.4 %collective-permute-start.10 = (f32[72,128]{1,0:T(8,128)S(1)}, f32[72,128]{1,0:T(8,128)S(1)}, u32[]{:S(2)}, u32[]{:S(2)}) collective-permute-start(f32[72,128]{1,0:T(8,128)S(1)} %get-tuple-element.57), channel_id=1, source_target_pairs={{0,1},{1,0},{2,3},{3,2},{4,5},{5,4},{6,7},{7,6},{8,9},{9,8},{10,11... | collective-permute-start | bytes 110600 | tf_op jit(solution)/shard_map/ppermute | solution.py:446
  24.0 4.8 %collective-permute-start.6 = (f32[64,128]{1,0:T(8,128)S(1)}, f32[64,128]{1,0:T(8,128)S(1)}, u32[]{:S(2)}, u32[]{:S(2)}) collective-permute-start(f32[64,128]{1,0:T(8,128)S(1)} %get-tuple-element.53), channel_id=1, source_target_pairs={{0,16},{1,17},{2,18},{3,19},{4,20},{5,21},{6,22},{7,23},{8,24},{9,... | collective-permute-start | bytes 98312 | tf_op jit(solution)/shard_map/ppermute | solution.py:446
  24.0 4.8 %collective-permute-start.7 = (f32[64,128]{1,0:T(8,128)S(1)}, f32[64,128]{1,0:T(8,128)S(1)}, u32[]{:S(2)}, u32[]{:S(2)}) collective-permute-start(f32[64,128]{1,0:T(8,128)S(1)} %get-tuple-element.54), channel_id=1, source_target_pairs={{0,8},{1,9},{2,10},{3,11},{4,12},{5,13},{6,14},{7,15},{8,0},{9,1},... | collective-permute-start | bytes 98312 | tf_op jit(solution)/shard_map/ppermute | solution.py:446
  24.0 4.8 %collective-permute-start.8 = (f32[64,128]{1,0:T(8,128)S(1)}, f32[64,128]{1,0:T(8,128)S(1)}, u32[]{:S(2)}, u32[]{:S(2)}) collective-permute-start(f32[64,128]{1,0:T(8,128)S(1)} %get-tuple-element.55), channel_id=1, source_target_pairs={{0,4},{1,5},{2,6},{3,7},{4,0},{5,1},{6,2},{7,3},{8,12},{9,13},{10,... | collective-permute-start | bytes 98312 | tf_op jit(solution)/shard_map/ppermute | solution.py:446
  27.5 3.9 %collective-permute-start.9 = (f32[64,128]{1,0:T(8,128)S(1)}, f32[64,128]{1,0:T(8,128)S(1)}, u32[]{:S(2)}, u32[]{:S(2)}) collective-permute-start(f32[64,128]{1,0:T(8,128)S(1)} %get-tuple-element.56), channel_id=1, source_target_pairs={{0,2},{1,3},{2,0},{3,1},{4,6},{5,7},{6,4},{7,5},{8,10},{9,11},{10,... | collective-permute-start | bytes 98312 | tf_op jit(solution)/shard_map/ppermute | solution.py:446
  34.1 6.7 %collective-permute-start.17 = (f32[8,128]{1,0:T(8,128)S(1)}, f32[8,128]{1,0:T(8,128)S(1)}, u32[]{:S(2)}, u32[]{:S(2)}) collective-permute-start(f32[8,128]{1,0:T(8,128)S(1)} %get-tuple-element.66), channel_id=1, source_target_pairs={{0,31},{1,2},{2,1},{3,4},{4,3},{5,6},{6,5},{7,8},{8,7},{9,10},{10,... | collective-permute-start | bytes 12296 | tf_op jit(solution)/shard_map/ppermute | solution.py:440
  36.2 8.5 %collective-permute-start.16 = (f32[72,128]{1,0:T(8,128)S(1)}, f32[72,128]{1,0:T(8,128)S(1)}, u32[]{:S(2)}, u32[]{:S(2)}) collective-permute-start(f32[72,128]{1,0:T(8,128)S(1)} %get-tuple-element.65), channel_id=1, source_target_pairs={{0,1},{1,0},{2,3},{3,2},{4,5},{5,4},{6,7},{7,6},{8,9},{9,8},{10,11... | collective-permute-start | bytes 110600 | tf_op jit(solution)/shard_map/ppermute | solution.py:446
  36.2 5.4 %collective-permute-start.12 = (f32[64,128]{1,0:T(8,128)S(1)}, f32[64,128]{1,0:T(8,128)S(1)}, u32[]{:S(2)}, u32[]{:S(2)}) collective-permute-start(f32[64,128]{1,0:T(8,128)S(1)} %get-tuple-element.61), channel_id=1, source_target_pairs={{0,16},{1,17},{2,18},{3,19},{4,20},{5,21},{6,22},{7,23},{8,24},{9,... | collective-permute-start | bytes 98312 | tf_op jit(solution)/shard_map/ppermute | solution.py:446
  36.3 5.4 %collective-permute-start.13 = (f32[64,128]{1,0:T(8,128)S(1)}, f32[64,128]{1,0:T(8,128)S(1)}, u32[]{:S(2)}, u32[]{:S(2)}) collective-permute-start(f32[64,128]{1,0:T(8,128)S(1)} %get-tuple-element.62), channel_id=1, source_target_pairs={{0,8},{1,9},{2,10},{3,11},{4,12},{5,13},{6,14},{7,15},{8,0},{9,1},... | collective-permute-start | bytes 98312 | tf_op jit(solution)/shard_map/ppermute | solution.py:446
  36.3 5.4 %collective-permute-start.14 = (f32[64,128]{1,0:T(8,128)S(1)}, f32[64,128]{1,0:T(8,128)S(1)}, u32[]{:S(2)}, u32[]{:S(2)}) collective-permute-start(f32[64,128]{1,0:T(8,128)S(1)} %get-tuple-element.63), channel_id=1, source_target_pairs={{0,4},{1,5},{2,6},{3,7},{4,0},{5,1},{6,2},{7,3},{8,12},{9,13},{10,... | collective-permute-start | bytes 98312 | tf_op jit(solution)/shard_map/ppermute | solution.py:446
  40.8 3.9 %collective-permute-start.15 = (f32[64,128]{1,0:T(8,128)S(1)}, f32[64,128]{1,0:T(8,128)S(1)}, u32[]{:S(2)}, u32[]{:S(2)}) collective-permute-start(f32[64,128]{1,0:T(8,128)S(1)} %get-tuple-element.64), channel_id=1, source_target_pairs={{0,2},{1,3},{2,0},{3,1},{4,6},{5,7},{6,4},{7,5},{8,10},{9,11},{10,... | collective-permute-start | bytes 98312 | tf_op jit(solution)/shard_map/ppermute | solution.py:446
  47.6 6.7 %collective-permute-start.23 = (f32[8,128]{1,0:T(8,128)S(1)}, f32[8,128]{1,0:T(8,128)S(1)}, u32[]{:S(2)}, u32[]{:S(2)}) collective-permute-start(f32[8,128]{1,0:T(8,128)S(1)} %get-tuple-element.73), channel_id=1, source_target_pairs={{0,31},{1,2},{2,1},{3,4},{4,3},{5,6},{6,5},{7,8},{8,7},{9,10},{10,... | collective-permute-start | bytes 12296 | tf_op jit(solution)/shard_map/ppermute | solution.py:440
  48.6 9.6 %collective-permute-start.22 = (f32[72,128]{1,0:T(8,128)S(1)}, f32[72,128]{1,0:T(8,128)S(1)}, u32[]{:S(2)}, u32[]{:S(2)}) collective-permute-start(f32[72,128]{1,0:T(8,128)S(1)} %get-tuple-element.72), channel_id=1, source_target_pairs={{0,1},{1,0},{2,3},{3,2},{4,5},{5,4},{6,7},{7,6},{8,9},{9,8},{10,11... | collective-permute-start | bytes 110600 | tf_op jit(solution)/shard_map/ppermute | solution.py:446
  48.6 6.5 %collective-permute-start.18 = (f32[64,128]{1,0:T(8,128)S(1)}, f32[64,128]{1,0:T(8,128)S(1)}, u32[]{:S(2)}, u32[]{:S(2)}) collective-permute-start(f32[64,128]{1,0:T(8,128)S(1)} %get-tuple-element.68), channel_id=1, source_target_pairs={{0,16},{1,17},{2,18},{3,19},{4,20},{5,21},{6,22},{7,23},{8,24},{9,... | collective-permute-start | bytes 98312 | tf_op jit(solution)/shard_map/ppermute | solution.py:446
  48.6 6.5 %collective-permute-start.19 = (f32[64,128]{1,0:T(8,128)S(1)}, f32[64,128]{1,0:T(8,128)S(1)}, u32[]{:S(2)}, u32[]{:S(2)}) collective-permute-start(f32[64,128]{1,0:T(8,128)S(1)} %get-tuple-element.69), channel_id=1, source_target_pairs={{0,8},{1,9},{2,10},{3,11},{4,12},{5,13},{6,14},{7,15},{8,0},{9,1},... | collective-permute-start | bytes 98312 | tf_op jit(solution)/shard_map/ppermute | solution.py:446
  48.7 6.5 %collective-permute-start.20 = (f32[64,128]{1,0:T(8,128)S(1)}, f32[64,128]{1,0:T(8,128)S(1)}, u32[]{:S(2)}, u32[]{:S(2)}) collective-permute-start(f32[64,128]{1,0:T(8,128)S(1)} %get-tuple-element.70), channel_id=1, source_target_pairs={{0,4},{1,5},{2,6},{3,7},{4,0},{5,1},{6,2},{7,3},{8,12},{9,13},{10,... | collective-permute-start | bytes 98312 | tf_op jit(solution)/shard_map/ppermute | solution.py:446
  54.3 3.9 %collective-permute-start.21 = (f32[64,128]{1,0:T(8,128)S(1)}, f32[64,128]{1,0:T(8,128)S(1)}, u32[]{:S(2)}, u32[]{:S(2)}) collective-permute-start(f32[64,128]{1,0:T(8,128)S(1)} %get-tuple-element.71), channel_id=1, source_target_pairs={{0,2},{1,3},{2,0},{3,1},{4,6},{5,7},{6,4},{7,5},{8,10},{9,11},{10,... | collective-permute-start | bytes 98312 | tf_op jit(solution)/shard_map/ppermute | solution.py:446

commit v2 on v1

--- a/solution.py
+++ b/solution.py
@@ -11,6 +11,7 @@
 ITERS = 4
 SLOT = 8
 GROUP = 128
+PARTS = 3
 SHIFT = 1.5
 F32 = jnp.float32
 BF16 = jnp.bfloat16
@@ -228,28 +229,39 @@
     def rows_of(total):
         return total[:nb, :width] + total[:nb, width:] + total[nb:, :width]
 
-    span = sure * GROUP
-    picked = dot(gather_ref[0:span, :], sources_ref[...])
-    for c, lhs in enumerate(stage(picked)):
-        lhs_ref[c * 2 * SLOT : (c + 1) * 2 * SLOT, :] = lhs
+    parts = PARTS if sure % PARTS == 0 else 1
+    part_span = sure // parts * GROUP
+
+    def gather_part(part):
+        at = part * part_span
+        picked = dot(gather_ref[at : at + part_span, :], sources_ref[...])
+        for c, lhs in enumerate(stage(picked)):
+            lhs_ref[2 * at + c * 2 * SLOT : 2 * at + (c + 1) * 2 * SLOT, :] = lhs
+
     total = jnp.zeros((width, width), F32)
-    for pair in range(span // SLOT // 2):
-        prods = []
-        for c in (2 * pair, 2 * pair + 1):
-            if c == blocks:
-                copy_table.wait()
-            if c >= blocks:
-                block = wide_ref[table_smem[0, c - blocks]]
-            elif dict_ref is None:
-                block = wide_ref[c]
-            else:
-                block = dict_ref[c]
-                total = total + block
-                block = halves_wide(block)
-                wide_ref[c] = block
-            prods.append(product(lhs_ref[c * 2 * SLOT : (c + 1) * 2 * SLOT, :], block))
-        prod_ref[pair * 2 * SLOT : (pair + 1) * 2 * SLOT, :] = halves_wide(jnp.concatenate(prods, axis=0))
-    out = rows_of(dot(scatter_ref[:, 0:span], prod_ref[...]))
+    out = jnp.zeros((nb, width), F32)
+    gather_part(0)
+    for part in range(parts):
+        if part + 1 < parts:
+            gather_part(part + 1)
+        for pair in range(part * part_span // SLOT // 2, (part + 1) * part_span // SLOT // 2):
+            prods = []
+            for c in (2 * pair, 2 * pair + 1):
+                if c == blocks:
+                    copy_table.wait()
+                if c >= blocks:
+                    block = wide_ref[table_smem[0, c - blocks]]
+                elif dict_ref is None:
+                    block = wide_ref[c]
+                else:
+                    block = dict_ref[c]
+                    total = total + block
+                    block = halves_wide(block)
+                    wide_ref[c] = block
+                prods.append(product(lhs_ref[c * 2 * SLOT : (c + 1) * 2 * SLOT, :], block))
+            prod_ref[pair * 2 * SLOT : (pair + 1) * 2 * SLOT, :] = halves_wide(jnp.concatenate(prods, axis=0))
+        span = slice(part * part_span, (part + 1) * part_span)
+        out = out + rows_of(dot(scatter_ref[:, span], prod_ref[span, :]))
 
     def further(group, out):
         at = pl.ds(pl.multiple_of(blocks * SLOT + group * GROUP, GROUP), GROUP)

time: 70.9 us -> 70.3 us (level)
  no operation moved by 1% of the time
where the time goes in v2:
time: 70.3 us; the launch traced here: 70.2 us
  starting transfers between devices  22.4 us (32%)
  waiting for transfers between devices  22.3 us (32%)
  Pallas kernels  15.9 us (23%)
  blocking collectives  8.87 us (13%)
  between operations  0.75 us (1%)
    ppermute x20, waiting for transfers between devices, exchange(): got.append(lax.ppermute(sends[level], 'rows', pairs))  13.3 us
    ppermute x4, starting transfers between devices, exchange(): edges = lax.ppermute(edge, 'rows', far)  12.9 us
    ppermute x20, starting transfers between devices, exchange(): got.append(lax.ppermute(sends[level], 'rows', pairs))  9.48 us
    ppermute x4, waiting for transfers between devices, exchange(): edges = lax.ppermute(edge, 'rows', far)  8.99 us
    all_to_all x1, blocking collectives, per_device(): sums = lax.all_to_all(sums, 'rows', 0, 0, tiled=True)  8.87 us
    pallas_call x2, Pallas kernels, per_device(): pl.pallas_call(functools.partial(step_kernel, **common), out_shape=[shape...  5.31 us
    pallas_call x1, Pallas kernels, per_device(): pl.pallas_call(functools.partial(prepare, nb=nb, levels=levels, half=half...  4.06 us
    pallas_call x1, Pallas kernels, per_device(): pl.pallas_call(functools.partial(first_kernel, **common), out_shape=[shap...  3.07 us
  transfers between devices with their start and end apart: 24, of which 10 were waited for; matrix products, arithmetic and copies ran while one was open for 0% of the time, Pallas kernels for 0%

profile of v2, /device:TPU:0, one launch (start us, length us, event | category | flops | bytes accessed | tf_op | source)
XLA Modules:
  0.0 70.2 jit_solution(15630544662810745832)
XLA Ops:
  0.7 4.1 %prepare.1 = (f32[64,128]{1,0:T(8,128)S(1)}, f32[64,128]{1,0:T(8,128)S(1)}, f32[64,128]{1,0:T(8,128)S(1)}, f32[64,128]{1,0:T(8,128)S(1)}, f32[72,128]{1,0:T(8,12...) custom-call(s32[1]{0:T(128)} %bitcast.parity_ref, ...), custom_call_target="tpu_custom_call" | custom-call | tf_op jit(solution)/shard_map/prepare/pallas_call | solution.py:422
  4.7 6.5 %collective-permute-start.5 = (f32[8,128]{1,0:T(8,128)S(1)}, f32[8,128]{1,0:T(8,128)S(1)}, u32[]{:S(2)}, u32[]{:S(2)}) collective-permute-start(f32[8,128]{1,0:T(8,128)S(1)} %get-tuple-element.46), channel_id=1, source_target_pairs={{0,31},{1,2},{2,1},{3,4},{4,3},{5,6},{6,5},{7,8},{8,7},{9,10},{10,... | collective-permute-start | bytes 12296 | tf_op jit(solution)/shard_map/ppermute | solution.py:452
  11.2 0.0 collective-permute-start.4
  11.2 0.0 collective-permute-start
  11.2 1.0 %collective-permute-start.1 = (f32[64,128]{1,0:T(8,128)S(1)}, f32[64,128]{1,0:T(8,128)S(1)}, u32[]{:S(2)}, u32[]{:S(2)}) collective-permute-start(f32[64,128]{1,0:T(8,128)S(1)} %get-tuple-element.42), channel_id=1, source_target_pairs={{0,8},{1,9},{2,10},{3,11},{4,12},{5,13},{6,14},{7,15},{8,0},{9,1},... | collective-permute-start | bytes 98312 | tf_op jit(solution)/shard_map/ppermute | solution.py:458
  12.2 1.3 %collective-permute-start.2 = (f32[64,128]{1,0:T(8,128)S(1)}, f32[64,128]{1,0:T(8,128)S(1)}, u32[]{:S(2)}, u32[]{:S(2)}) collective-permute-start(f32[64,128]{1,0:T(8,128)S(1)} %get-tuple-element.43), channel_id=1, source_target_pairs={{0,4},{1,5},{2,6},{3,7},{4,0},{5,1},{6,2},{7,3},{8,12},{9,13},{10,... | collective-permute-start | bytes 98312 | tf_op jit(solution)/shard_map/ppermute | solution.py:458
  13.6 0.0 collective-permute-done.5.refs_8_
  13.6 0.0 collective-permute-start.3
  13.6 2.4 %collective-permute-done.refs_3_ = f32[64,128]{1,0:T(8,128)S(1)} collective-permute-done((f32[64,128]{1,0:T(8,128)S(1)}, f32[64,128]{1,0:T(8,128)S(1)}, u32[]{:S(2)}, u32[]{:S(2)}) %collective-permute-start) | collective-permute-done | bytes 32800 | tf_op jit(solution)/shard_map/ppermute | solution.py:458
  16.0 0.0 collective-permute-done.1.refs_4_
  16.0 0.1 collective-permute-done.2.refs_5_
  16.1 1.3 %collective-permute-done.3.refs_6_ = f32[64,128]{1,0:T(8,128)S(1)} collective-permute-done((f32[64,128]{1,0:T(8,128)S(1)}, f32[64,128]{1,0:T(8,128)S(1)}, u32[]{:S(2)}, u32[]{:S(2)}) %collective-permute-start.3) | collective-permute-done | bytes 32800 | tf_op jit(solution)/shard_map/ppermute | solution.py:458
  17.5 0.0 collective-permute-done.4.refs_7_
  17.5 3.1 %first.1 = (f32[128,128]{1,0:T(8,128)S(1)}, f32[64,128]{1,0:T(8,128)S(1)}, f32[64,128]{1,0:T(8,128)S(1)}, f32[64,128]{1,0:T(8,128)S(1)}, f32[64,128]{1,0:T(8,128...) custom-call(s32[1,128]{1,0:T(1,128)S(1)} %get-tuple-element.40.refs_, ...), custom_call_target="tpu_custom_call" | custom-call | tf_op jit(solution)/shard_map/first/pallas_call | solution.py:473
  20.6 3.3 %collective-permute-start.11 = (f32[8,128]{1,0:T(8,128)S(1)}, f32[8,128]{1,0:T(8,128)S(1)}, u32[]{:S(2)}, u32[]{:S(2)}) collective-permute-start(f32[8,128]{1,0:T(8,128)S(1)} %get-tuple-element.58), channel_id=1, source_target_pairs={{0,31},{1,2},{2,1},{3,4},{4,3},{5,6},{6,5},{7,8},{8,7},{9,10},{10,... | collective-permute-start | bytes 12296 | tf_op jit(solution)/shard_map/ppermute | solution.py:452
  23.9 0.0 collective-permute-start.10
  23.9 0.0 collective-permute-start.6
  23.9 0.0 collective-permute-start.7
  23.9 1.5 %collective-permute-start.8 = (f32[64,128]{1,0:T(8,128)S(1)}, f32[64,128]{1,0:T(8,128)S(1)}, u32[]{:S(2)}, u32[]{:S(2)}) collective-permute-start(f32[64,128]{1,0:T(8,128)S(1)} %get-tuple-element.55), channel_id=1, source_target_pairs={{0,4},{1,5},{2,6},{3,7},{4,0},{5,1},{6,2},{7,3},{8,12},{9,13},{10,... | collective-permute-start | bytes 98312 | tf_op jit(solution)/shard_map/ppermute | solution.py:458
  25.4 1.9 %collective-permute-done.11.refs_9_ = f32[8,128]{1,0:T(8,128)S(1)} collective-permute-done((f32[8,128]{1,0:T(8,128)S(1)}, f32[8,128]{1,0:T(8,128)S(1)}, u32[]{:S(2)}, u32[]{:S(2)}) %collective-permute-start.11) | collective-permute-done | bytes 4128 | tf_op jit(solution)/shard_map/ppermute | solution.py:452
  27.4 0.7 %collective-permute-start.9 = (f32[64,128]{1,0:T(8,128)S(1)}, f32[64,128]{1,0:T(8,128)S(1)}, u32[]{:S(2)}, u32[]{:S(2)}) collective-permute-start(f32[64,128]{1,0:T(8,128)S(1)} %get-tuple-element.56), channel_id=1, source_target_pairs={{0,2},{1,3},{2,0},{3,1},{4,6},{5,7},{6,4},{7,5},{8,10},{9,11},{10,... | collective-permute-start | bytes 98312 | tf_op jit(solution)/shard_map/ppermute | solution.py:458
  28.1 0.6 collective-permute-done.6.refs_4_
  28.7 0.0 collective-permute-done.7.refs_5_
  28.7 0.0 collective-permute-done.8.refs_6_
  28.7 2.6 %collective-permute-done.9.refs_7_ = f32[64,128]{1,0:T(8,128)S(1)} collective-permute-done((f32[64,128]{1,0:T(8,128)S(1)}, f32[64,128]{1,0:T(8,128)S(1)}, u32[]{:S(2)}, u32[]{:S(2)}) %collective-permute-start.9) | collective-permute-done | bytes 32800 | tf_op jit(solution)/shard_map/ppermute | solution.py:458
  31.3 2.6 %step.2 = (f32[128,128]{1,0:T(8,128)S(1)}, f32[64,128]{1,0:T(8,128)S(1)}, f32[64,128]{1,0:T(8,128)S(1)}, f32[64,128]{1,0:T(8,128)S(1)}, f32[64,128]{1,0:T(8,128)...) custom-call(s32[1,128]{1,0:T(1,128)S(1)} %get-tuple-element.40.refs_0_, ...), custom_call_target="tpu_custom_call" | custom-call | tf_op jit(solution)/shard_map/step/pallas_call | solution.py:485
  33.8 2.1 %collective-permute-start.17 = (f32[8,128]{1,0:T(8,128)S(1)}, f32[8,128]{1,0:T(8,128)S(1)}, u32[]{:S(2)}, u32[]{:S(2)}) collective-permute-start(f32[8,128]{1,0:T(8,128)S(1)} %get-tuple-element.66), channel_id=1, source_target_pairs={{0,31},{1,2},{2,1},{3,4},{4,3},{5,6},{6,5},{7,8},{8,7},{9,10},{10,... | collective-permute-start | bytes 12296 | tf_op jit(solution)/shard_map/ppermute | solution.py:452
  36.0 0.0 collective-permute-start.12
  36.0 0.0 collective-permute-start.13
  36.0 1.6 %collective-permute-start.14 = (f32[64,128]{1,0:T(8,128)S(1)}, f32[64,128]{1,0:T(8,128)S(1)}, u32[]{:S(2)}, u32[]{:S(2)}) collective-permute-start(f32[64,128]{1,0:T(8,128)S(1)} %get-tuple-element.63), channel_id=1, source_target_pairs={{0,4},{1,5},{2,6},{3,7},{4,0},{5,1},{6,2},{7,3},{8,12},{9,13},{10,... | collective-permute-start | bytes 98312 | tf_op jit(solution)/shard_map/ppermute | solution.py:458
  37.6 3.0 %collective-permute-done.17.refs_9_ = f32[8,128]{1,0:T(8,128)S(1)} collective-permute-done((f32[8,128]{1,0:T(8,128)S(1)}, f32[8,128]{1,0:T(8,128)S(1)}, u32[]{:S(2)}, u32[]{:S(2)}) %collective-permute-start.17) | collective-permute-done | bytes 4128 | tf_op jit(solution)/shard_map/ppermute | solution.py:452
  40.5 0.8 %collective-permute-start.15 = (f32[64,128]{1,0:T(8,128)S(1)}, f32[64,128]{1,0:T(8,128)S(1)}, u32[]{:S(2)}, u32[]{:S(2)}) collective-permute-start(f32[64,128]{1,0:T(8,128)S(1)} %get-tuple-element.64), channel_id=1, source_target_pairs={{0,2},{1,3},{2,0},{3,1},{4,6},{5,7},{6,4},{7,5},{8,10},{9,11},{10,... | collective-permute-start | bytes 98312 | tf_op jit(solution)/shard_map/ppermute | solution.py:458
  41.3 0.0 collective-permute-done.12.refs_4_
  41.4 0.0 collective-permute-done.13.refs_5_
  41.4 0.0 collective-permute-done.14.refs_6_
  41.4 3.1 %collective-permute-done.15.refs_7_ = f32[64,128]{1,0:T(8,128)S(1)} collective-permute-done((f32[64,128]{1,0:T(8,128)S(1)}, f32[64,128]{1,0:T(8,128)S(1)}, u32[]{:S(2)}, u32[]{:S(2)}) %collective-permute-start.15) | collective-permute-done | bytes 32800 | tf_op jit(solution)/shard_map/ppermute | solution.py:458
  44.5 0.0 collective-permute-done.16.refs_8_
  44.5 2.7 %step.3 = (f32[128,128]{1,0:T(8,128)S(1)}, f32[64,128]{1,0:T(8,128)S(1)}, f32[64,128]{1,0:T(8,128)S(1)}, f32[64,128]{1,0:T(8,128)S(1)}, f32[64,128]{1,0:T(8,128)...) custom-call(s32[1,128]{1,0:T(1,128)S(1)} %get-tuple-element.40.refs_0_, ...), custom_call_target="tpu_custom_call" | custom-call | tf_op jit(solution)/shard_map/step/pallas_call | solution.py:485
  47.2 1.0 %collective-permute-start.23 = (f32[8,128]{1,0:T(8,128)S(1)}, f32[8,128]{1,0:T(8,128)S(1)}, u32[]{:S(2)}, u32[]{:S(2)}) collective-permute-start(f32[8,128]{1,0:T(8,128)S(1)} %get-tuple-element.73), channel_id=1, source_target_pairs={{0,31},{1,2},{2,1},{3,4},{4,3},{5,6},{6,5},{7,8},{8,7},{9,10},{10,... | collective-permute-start | bytes 12296 | tf_op jit(solution)/shard_map/ppermute | solution.py:452
  48.2 0.0 collective-permute-start.22
  48.2 1.6 %collective-permute-start.20 = (f32[64,128]{1,0:T(8,128)S(1)}, f32[64,128]{1,0:T(8,128)S(1)}, u32[]{:S(2)}, u32[]{:S(2)}) collective-permute-start(f32[64,128]{1,0:T(8,128)S(1)} %get-tuple-element.70), channel_id=1, source_target_pairs={{0,4},{1,5},{2,6},{3,7},{4,0},{5,1},{6,2},{7,3},{8,12},{9,13},{10,... | collective-permute-start | bytes 98312 | tf_op jit(solution)/shard_map/ppermute | solution.py:458
  49.8 4.1 %collective-permute-done.23.refs_9_ = f32[8,128]{1,0:T(8,128)S(1)} collective-permute-done((f32[8,128]{1,0:T(8,128)S(1)}, f32[8,128]{1,0:T(8,128)S(1)}, u32[]{:S(2)}, u32[]{:S(2)}) %collective-permute-start.23) | collective-permute-done | bytes 4128 | tf_op jit(solution)/shard_map/ppermute | solution.py:452
  53.9 0.8 %collective-permute-start.21 = (f32[64,128]{1,0:T(8,128)S(1)}, f32[64,128]{1,0:T(8,128)S(1)}, u32[]{:S(2)}, u32[]{:S(2)}) collective-permute-start(f32[64,128]{1,0:T(8,128)S(1)} %get-tuple-element.71), channel_id=1, source_target_pairs={{0,2},{1,3},{2,0},{3,1},{4,6},{5,7},{6,4},{7,5},{8,10},{9,11},{10,... | collective-permute-start | bytes 98312 | tf_op jit(solution)/shard_map/ppermute | solution.py:458
  54.7 0.0 collective-permute-done.18.refs_4_
  54.7 3.1 %collective-permute-done.21.refs_7_ = f32[64,128]{1,0:T(8,128)S(1)} collective-permute-done((f32[64,128]{1,0:T(8,128)S(1)}, f32[64,128]{1,0:T(8,128)S(1)}, u32[]{:S(2)}, u32[]{:S(2)}) %collective-permute-start.21) | collective-permute-done | bytes 32800 | tf_op jit(solution)/shard_map/ppermute | solution.py:458
  57.8 2.6 %last.1 = (f32[128,128]{1,0:T(8,128)S(1)}, f32[32,128]{1,0:T(8,128)S(1)}) custom-call(s32[1,128]{1,0:T(1,128)S(1)} %get-tuple-element.40.refs_0_, f32[128,128]{1,0:T(8,128)S(1)} %get-tuple-element.67.refs_1_.refs_3_, f32[128,128]{1,0:T(8,128)S(1)} %bitcast.19, f32[1,128]{1,0:T(1,128)S(1)} %get-tuple-element.52.refs_3_.scale_ref, ...), custom_call_target="tpu_custom_call" | custom-call | tf_op jit(solution)/shard_map/last/pallas_call | solution.py:496
  60.4 8.9 %all_to_all.11 = f32[32,1,128]{2,1,0:T(1,128)S(1)} all-to-all(f32[32,1,128]{2,1,0:T(1,128)S(1)} %bitcast.25), channel_id=1, replica_groups=mesh['rows'=32] {'rows'}, dimensions={0} | all-to-all | bytes 32768 | tf_op jit(solution)/shard_map/all_to_all | solution.py:506
  69.3 0.9 %finish.1 = (f32[128,128]{1,0:T(8,128)}, f32[128,128]{1,0:T(8,128)}) custom-call(f32[32,128]{1,0:T(8,128)S(1)} %bitcast.24, f32[1,128]{1,0:T(1,128)S(1)} %get-tuple-element.52.refs_3_.scale_ref, f32[128,128]{1,0:T(8,128)S(1)} %bitcast.23, f32[128,128]{1,0:T(8,128)S(1)} %get-tuple-element.51.refs_1_.refs_14_, ...), custom_call_target="tpu_custom_call" | custom-call | tf_op jit(solution)/shard_map/finish/pallas_call | solution.py:507
  (11 shorter events, 0.0 us)
Async XLA Ops:
  0.6 16.8 %copy-start.1 = (f32[16384]{0:T(1024)S(1)}, f32[16384]{0:T(1024)}, u32[]{:S(2)}) copy-start(f32[16384]{0:T(1024)} %param.10) | copy-start | bytes 196612
  0.6 16.8 %copy-start = (f32[16384]{0:T(1024)S(1)}, f32[16384]{0:T(1024)}, u32[]{:S(2)}) copy-start(f32[16384]{0:T(1024)} %param.11) | copy-start | bytes 196612
  4.7 8.8 %collective-permute-start.5 = (f32[8,128]{1,0:T(8,128)S(1)}, f32[8,128]{1,0:T(8,128)S(1)}, u32[]{:S(2)}, u32[]{:S(2)}) collective-permute-start(f32[8,128]{1,0:T(8,128)S(1)} %get-tuple-element.46), channel_id=1, source_target_pairs={{0,31},{1,2},{2,1},{3,4},{4,3},{5,6},{6,5},{7,8},{8,7},{9,10},{10,... | collective-permute-start | bytes 12296 | tf_op jit(solution)/shard_map/ppermute | solution.py:452
  11.2 6.3 %collective-permute-start.4 = (f32[72,128]{1,0:T(8,128)S(1)}, f32[72,128]{1,0:T(8,128)S(1)}, u32[]{:S(2)}, u32[]{:S(2)}) collective-permute-start(f32[72,128]{1,0:T(8,128)S(1)} %get-tuple-element.45), channel_id=1, source_target_pairs={{0,1},{1,0},{2,3},{3,2},{4,5},{5,4},{6,7},{7,6},{8,9},{9,8},{10,11... | collective-permute-start | bytes 110600 | tf_op jit(solution)/shard_map/ppermute | solution.py:458
  11.2 4.8 %collective-permute-start = (f32[64,128]{1,0:T(8,128)S(1)}, f32[64,128]{1,0:T(8,128)S(1)}, u32[]{:S(2)}, u32[]{:S(2)}) collective-permute-start(f32[64,128]{1,0:T(8,128)S(1)} %get-tuple-element.41), channel_id=1, source_target_pairs={{0,16},{1,17},{2,18},{3,19},{4,20},{5,21},{6,22},{7,23},{8,24},{9,... | collective-permute-start | bytes 98312 | tf_op jit(solution)/shard_map/ppermute | solution.py:458
  11.2 4.8 %collective-permute-start.1 = (f32[64,128]{1,0:T(8,128)S(1)}, f32[64,128]{1,0:T(8,128)S(1)}, u32[]{:S(2)}, u32[]{:S(2)}) collective-permute-start(f32[64,128]{1,0:T(8,128)S(1)} %get-tuple-element.42), channel_id=1, source_target_pairs={{0,8},{1,9},{2,10},{3,11},{4,12},{5,13},{6,14},{7,15},{8,0},{9,1},... | collective-permute-start | bytes 98312 | tf_op jit(solution)/shard_map/ppermute | solution.py:458
  12.2 3.9 %collective-permute-start.2 = (f32[64,128]{1,0:T(8,128)S(1)}, f32[64,128]{1,0:T(8,128)S(1)}, u32[]{:S(2)}, u32[]{:S(2)}) collective-permute-start(f32[64,128]{1,0:T(8,128)S(1)} %get-tuple-element.43), channel_id=1, source_target_pairs={{0,4},{1,5},{2,6},{3,7},{4,0},{5,1},{6,2},{7,3},{8,12},{9,13},{10,... | collective-permute-start | bytes 98312 | tf_op jit(solution)/shard_map/ppermute | solution.py:458
  13.6 3.9 %collective-permute-start.3 = (f32[64,128]{1,0:T(8,128)S(1)}, f32[64,128]{1,0:T(8,128)S(1)}, u32[]{:S(2)}, u32[]{:S(2)}) collective-permute-start(f32[64,128]{1,0:T(8,128)S(1)} %get-tuple-element.44), channel_id=1, source_target_pairs={{0,2},{1,3},{2,0},{3,1},{4,6},{5,7},{6,4},{7,5},{8,10},{9,11},{10,... | collective-permute-start | bytes 98312 | tf_op jit(solution)/shard_map/ppermute | solution.py:458
  20.6 6.8 %collective-permute-start.11 = (f32[8,128]{1,0:T(8,128)S(1)}, f32[8,128]{1,0:T(8,128)S(1)}, u32[]{:S(2)}, u32[]{:S(2)}) collective-permute-start(f32[8,128]{1,0:T(8,128)S(1)} %get-tuple-element.58), channel_id=1, source_target_pairs={{0,31},{1,2},{2,1},{3,4},{4,3},{5,6},{6,5},{7,8},{8,7},{9,10},{10,... | collective-permute-start | bytes 12296 | tf_op jit(solution)/shard_map/ppermute | solution.py:452
  23.9 7.4 %collective-permute-start.10 = (f32[72,128]{1,0:T(8,128)S(1)}, f32[72,128]{1,0:T(8,128)S(1)}, u32[]{:S(2)}, u32[]{:S(2)}) collective-permute-start(f32[72,128]{1,0:T(8,128)S(1)} %get-tuple-element.57), channel_id=1, source_target_pairs={{0,1},{1,0},{2,3},{3,2},{4,5},{5,4},{6,7},{7,6},{8,9},{9,8},{10,11... | collective-permute-start | bytes 110600 | tf_op jit(solution)/shard_map/ppermute | solution.py:458
  23.9 4.8 %collective-permute-start.6 = (f32[64,128]{1,0:T(8,128)S(1)}, f32[64,128]{1,0:T(8,128)S(1)}, u32[]{:S(2)}, u32[]{:S(2)}) collective-permute-start(f32[64,128]{1,0:T(8,128)S(1)} %get-tuple-element.53), channel_id=1, source_target_pairs={{0,16},{1,17},{2,18},{3,19},{4,20},{5,21},{6,22},{7,23},{8,24},{9,... | collective-permute-start | bytes 98312 | tf_op jit(solution)/shard_map/ppermute | solution.py:458
  23.9 4.8 %collective-permute-start.7 = (f32[64,128]{1,0:T(8,128)S(1)}, f32[64,128]{1,0:T(8,128)S(1)}, u32[]{:S(2)}, u32[]{:S(2)}) collective-permute-start(f32[64,128]{1,0:T(8,128)S(1)} %get-tuple-element.54), channel_id=1, source_target_pairs={{0,8},{1,9},{2,10},{3,11},{4,12},{5,13},{6,14},{7,15},{8,0},{9,1},... | collective-permute-start | bytes 98312 | tf_op jit(solution)/shard_map/ppermute | solution.py:458
  23.9 4.8 %collective-permute-start.8 = (f32[64,128]{1,0:T(8,128)S(1)}, f32[64,128]{1,0:T(8,128)S(1)}, u32[]{:S(2)}, u32[]{:S(2)}) collective-permute-start(f32[64,128]{1,0:T(8,128)S(1)} %get-tuple-element.55), channel_id=1, source_target_pairs={{0,4},{1,5},{2,6},{3,7},{4,0},{5,1},{6,2},{7,3},{8,12},{9,13},{10,... | collective-permute-start | bytes 98312 | tf_op jit(solution)/shard_map/ppermute | solution.py:458
  27.4 3.9 %collective-permute-start.9 = (f32[64,128]{1,0:T(8,128)S(1)}, f32[64,128]{1,0:T(8,128)S(1)}, u32[]{:S(2)}, u32[]{:S(2)}) collective-permute-start(f32[64,128]{1,0:T(8,128)S(1)} %get-tuple-element.56), channel_id=1, source_target_pairs={{0,2},{1,3},{2,0},{3,1},{4,6},{5,7},{6,4},{7,5},{8,10},{9,11},{10,... | collective-permute-start | bytes 98312 | tf_op jit(solution)/shard_map/ppermute | solution.py:458
  33.8 6.7 %collective-permute-start.17 = (f32[8,128]{1,0:T(8,128)S(1)}, f32[8,128]{1,0:T(8,128)S(1)}, u32[]{:S(2)}, u32[]{:S(2)}) collective-permute-start(f32[8,128]{1,0:T(8,128)S(1)} %get-tuple-element.66), channel_id=1, source_target_pairs={{0,31},{1,2},{2,1},{3,4},{4,3},{5,6},{6,5},{7,8},{8,7},{9,10},{10,... | collective-permute-start | bytes 12296 | tf_op jit(solution)/shard_map/ppermute | solution.py:452
  36.0 8.5 %collective-permute-start.16 = (f32[72,128]{1,0:T(8,128)S(1)}, f32[72,128]{1,0:T(8,128)S(1)}, u32[]{:S(2)}, u32[]{:S(2)}) collective-permute-start(f32[72,128]{1,0:T(8,128)S(1)} %get-tuple-element.65), channel_id=1, source_target_pairs={{0,1},{1,0},{2,3},{3,2},{4,5},{5,4},{6,7},{7,6},{8,9},{9,8},{10,11... | collective-permute-start | bytes 110600 | tf_op jit(solution)/shard_map/ppermute | solution.py:458
  36.0 5.4 %collective-permute-start.12 = (f32[64,128]{1,0:T(8,128)S(1)}, f32[64,128]{1,0:T(8,128)S(1)}, u32[]{:S(2)}, u32[]{:S(2)}) collective-permute-start(f32[64,128]{1,0:T(8,128)S(1)} %get-tuple-element.61), channel_id=1, source_target_pairs={{0,16},{1,17},{2,18},{3,19},{4,20},{5,21},{6,22},{7,23},{8,24},{9,... | collective-permute-start | bytes 98312 | tf_op jit(solution)/shard_map/ppermute | solution.py:458
  36.0 5.4 %collective-permute-start.13 = (f32[64,128]{1,0:T(8,128)S(1)}, f32[64,128]{1,0:T(8,128)S(1)}, u32[]{:S(2)}, u32[]{:S(2)}) collective-permute-start(f32[64,128]{1,0:T(8,128)S(1)} %get-tuple-element.62), channel_id=1, source_target_pairs={{0,8},{1,9},{2,10},{3,11},{4,12},{5,13},{6,14},{7,15},{8,0},{9,1},... | collective-permute-start | bytes 98312 | tf_op jit(solution)/shard_map/ppermute | solution.py:458
  36.0 5.4 %collective-permute-start.14 = (f32[64,128]{1,0:T(8,128)S(1)}, f32[64,128]{1,0:T(8,128)S(1)}, u32[]{:S(2)}, u32[]{:S(2)}) collective-permute-start(f32[64,128]{1,0:T(8,128)S(1)} %get-tuple-element.63), channel_id=1, source_target_pairs={{0,4},{1,5},{2,6},{3,7},{4,0},{5,1},{6,2},{7,3},{8,12},{9,13},{10,... | collective-permute-start | bytes 98312 | tf_op jit(solution)/shard_map/ppermute | solution.py:458
  40.5 3.9 %collective-permute-start.15 = (f32[64,128]{1,0:T(8,128)S(1)}, f32[64,128]{1,0:T(8,128)S(1)}, u32[]{:S(2)}, u32[]{:S(2)}) collective-permute-start(f32[64,128]{1,0:T(8,128)S(1)} %get-tuple-element.64), channel_id=1, source_target_pairs={{0,2},{1,3},{2,0},{3,1},{4,6},{5,7},{6,4},{7,5},{8,10},{9,11},{10,... | collective-permute-start | bytes 98312 | tf_op jit(solution)/shard_map/ppermute | solution.py:458
  47.2 6.7 %collective-permute-start.23 = (f32[8,128]{1,0:T(8,128)S(1)}, f32[8,128]{1,0:T(8,128)S(1)}, u32[]{:S(2)}, u32[]{:S(2)}) collective-permute-start(f32[8,128]{1,0:T(8,128)S(1)} %get-tuple-element.73), channel_id=1, source_target_pairs={{0,31},{1,2},{2,1},{3,4},{4,3},{5,6},{6,5},{7,8},{8,7},{9,10},{10,... | collective-permute-start | bytes 12296 | tf_op jit(solution)/shard_map/ppermute | solution.py:452
  48.2 9.6 %collective-permute-start.22 = (f32[72,128]{1,0:T(8,128)S(1)}, f32[72,128]{1,0:T(8,128)S(1)}, u32[]{:S(2)}, u32[]{:S(2)}) collective-permute-start(f32[72,128]{1,0:T(8,128)S(1)} %get-tuple-element.72), channel_id=1, source_target_pairs={{0,1},{1,0},{2,3},{3,2},{4,5},{5,4},{6,7},{7,6},{8,9},{9,8},{10,11... | collective-permute-start | bytes 110600 | tf_op jit(solution)/shard_map/ppermute | solution.py:458
  48.2 6.5 %collective-permute-start.18 = (f32[64,128]{1,0:T(8,128)S(1)}, f32[64,128]{1,0:T(8,128)S(1)}, u32[]{:S(2)}, u32[]{:S(2)}) collective-permute-start(f32[64,128]{1,0:T(8,128)S(1)} %get-tuple-element.68), channel_id=1, source_target_pairs={{0,16},{1,17},{2,18},{3,19},{4,20},{5,21},{6,22},{7,23},{8,24},{9,... | collective-permute-start | bytes 98312 | tf_op jit(solution)/shard_map/ppermute | solution.py:458
  48.2 6.5 %collective-permute-start.19 = (f32[64,128]{1,0:T(8,128)S(1)}, f32[64,128]{1,0:T(8,128)S(1)}, u32[]{:S(2)}, u32[]{:S(2)}) collective-permute-start(f32[64,128]{1,0:T(8,128)S(1)} %get-tuple-element.69), channel_id=1, source_target_pairs={{0,8},{1,9},{2,10},{3,11},{4,12},{5,13},{6,14},{7,15},{8,0},{9,1},... | collective-permute-start | bytes 98312 | tf_op jit(solution)/shard_map/ppermute | solution.py:458
  48.2 6.5 %collective-permute-start.20 = (f32[64,128]{1,0:T(8,128)S(1)}, f32[64,128]{1,0:T(8,128)S(1)}, u32[]{:S(2)}, u32[]{:S(2)}) collective-permute-start(f32[64,128]{1,0:T(8,128)S(1)} %get-tuple-element.70), channel_id=1, source_target_pairs={{0,4},{1,5},{2,6},{3,7},{4,0},{5,1},{6,2},{7,3},{8,12},{9,13},{10,... | collective-permute-start | bytes 98312 | tf_op jit(solution)/shard_map/ppermute | solution.py:458
  53.9 3.9 %collective-permute-start.21 = (f32[64,128]{1,0:T(8,128)S(1)}, f32[64,128]{1,0:T(8,128)S(1)}, u32[]{:S(2)}, u32[]{:S(2)}) collective-permute-start(f32[64,128]{1,0:T(8,128)S(1)} %get-tuple-element.71), channel_id=1, source_target_pairs={{0,2},{1,3},{2,0},{3,1},{4,6},{5,7},{6,4},{7,5},{8,10},{9,11},{10,... | collective-permute-start | bytes 98312 | tf_op jit(solution)/shard_map/ppermute | solution.py:458

commit v3 on v2

--- a/solution.py
+++ b/solution.py
@@ -11,6 +11,7 @@
 ITERS = 4
 SLOT = 8
 GROUP = 128
+COST = 10**10
 PARTS = 3
 SHIFT = 1.5
 F32 = jnp.float32
@@ -60,31 +61,19 @@
 
 
 def prepare(
-    parity_ref, dict_hbm, *refs, nb, levels, half, merged, groups, sure, entries, sources,
+    parity_ref, *refs, nb, blocks, levels, half, merged, groups, sure, entries, sources,
 ):
     small_hbm, refs = refs[:8], refs[8:]
-    sends, (edge_ref, select_ref, gather_ref, scatter_ref, dict_vmem, table_ref) = (
-        refs[:levels], refs[levels : levels + 6],
-    )
-    facts_ref, *small, small_sems, sems = refs[levels + 6 :]
+    sends, (edge_ref, select_ref, gather_ref, scatter_ref, table_ref) = refs[:levels], refs[levels : levels + 5]
+    facts_ref, *small, small_sems = refs[levels + 5 :]
     vec_vmem, own_ids_ref, own_weights_ref, near_ids_ref, near_weights_ref, *link_refs = small
     link_rows_ref, link_ids_ref, link_weights_ref = link_refs
-    blocks, _, _ = dict_hbm.shape
-    parts = sems.shape[0]
-    per = blocks // parts
-
-    def load(part):
-        span = pl.ds(part * per, per)
-        return pltpu.make_async_copy(dict_hbm.at[span], dict_vmem.at[span], sems.at[part])
-
     load_small = [
         pltpu.make_async_copy(source, target, small_sems.at[k])
         for k, (source, target) in enumerate(zip(small_hbm, small))
     ]
     for copy in load_small[1:] + load_small[:1]:
         copy.start()
-    for part in range(parts):
-        load(part).start()
     for copy in load_small[1:]:
         copy.wait()
 
@@ -188,8 +177,6 @@
 
     load_small[0].wait()
     send_blocks(select_ref, vec_vmem[...], sends, edge_ref, merged)
-    for part in range(parts):
-        load(part).wait()
 
 
 def apply_operator(
@@ -421,7 +408,7 @@
     edge_shape = shape((8, width))
     outs = pl.pallas_call(
         functools.partial(
-            prepare, nb=nb, levels=levels, half=half, merged=merged, groups=groups, sure=sure,
+            prepare, nb=nb, blocks=blocks, levels=levels, half=half, merged=merged, groups=groups, sure=sure,
             entries=entries, sources=sources,
         ),
         out_shape=send_shapes
@@ -430,21 +417,20 @@
             shape((links, nb), BF16),
             shape((groups * GROUP, sources), BF16),
             shape((2 * nb, groups * GROUP), BF16),
-            shape((blocks, width, width)),
             shape((1, 128), jnp.int32),
         ],
-        in_specs=[pl.BlockSpec(memory_space=pltpu.SMEM)] + [pl.BlockSpec(memory_space=pltpu.HBM)] * 9,
-        out_specs=vmem(levels + 6),
+        in_specs=[pl.BlockSpec(memory_space=pltpu.SMEM)] + [pl.BlockSpec(memory_space=pltpu.HBM)] * 8,
+        out_specs=vmem(levels + 5),
         scratch_shapes=[
             pltpu.VMEM((128, entries), BF16),
             *(pltpu.VMEM(array.shape, array.dtype) for array in small),
             pltpu.SemaphoreType.DMA((len(small),)),
-            pltpu.SemaphoreType.DMA((4,)),
         ],
         compiler_params=params(24),
+        cost_estimate=pl.CostEstimate(flops=COST, bytes_accessed=0, transcendentals=0),
         name="prepare",
-)(parity, *(pltpu.with_memory_space_constraint(array, pltpu.HBM) for array in [dictionary] + small))
-    sends, (edge, select, gather, scatter, blocks_vmem, table) = outs[:levels], outs[levels:]
+)(parity, *(pltpu.with_memory_space_constraint(array, pltpu.HBM) for array in small))
+    sends, (edge, select, gather, scatter, table) = outs[:levels], outs[levels:]
 
     def exchange(sends, edge):
         near = [(i, i ^ 1) for i in range(devices)]
@@ -479,7 +465,7 @@
                 scratch_shapes=scratch,
                 compiler_params=params(24),
                 name="first",
-            )(table, first, shifts, *got, edges, select, gather, scatter, blocks_vmem)
+            )(table, first, shifts, *got, edges, select, gather, scatter, dictionary)
             sends, (edge, wide, scale) = outs[:levels], outs[levels:]
         elif k + 1 < ITERS:
             following, *outs = pl.pallas_call(

time: 70.3 us -> 69.2 us (0.984)
  Pallas kernels: 15.9 us -> 14.7 us
    pallas_call x1, Pallas kernels: 4.06 us -> 2.86 us  [per_device(): pl.pallas_call(functools.partial(prepare, nb=nb, blocks=blocks, levels=le...]
where the time goes in v3:
time: 69.2 us; the launch traced here: 69 us
  starting transfers between devices  22.3 us (32%)
  waiting for transfers between devices  22.3 us (32%)
  Pallas kernels  14.7 us (21%)
  blocking collectives  8.87 us (13%)
  between operations  0.76 us (1%)
    ppermute x20, waiting for transfers between devices, exchange(): got.append(lax.ppermute(sends[level], 'rows', pairs))  13.3 us
    ppermute x4, starting transfers between devices, exchange(): edges = lax.ppermute(edge, 'rows', far)  12.8 us
    ppermute x20, starting transfers between devices, exchange(): got.append(lax.ppermute(sends[level], 'rows', pairs))  9.52 us
    ppermute x4, waiting for transfers between devices, exchange(): edges = lax.ppermute(edge, 'rows', far)  9.04 us
    all_to_all x1, blocking collectives, per_device(): sums = lax.all_to_all(sums, 'rows', 0, 0, tiled=True)  8.87 us
    pallas_call x2, Pallas kernels, per_device(): pl.pallas_call(functools.partial(step_kernel, **common), out_shape=[shape...  5.3 us
    pallas_call x1, Pallas kernels, per_device(): pl.pallas_call(functools.partial(first_kernel, **common), out_shape=[shap...  3.07 us
    pallas_call x1, Pallas kernels, per_device(): pl.pallas_call(functools.partial(prepare, nb=nb, blocks=blocks, levels=le...  2.86 us
  transfers between devices with their start and end apart: 24, of which 10 were waited for; matrix products, arithmetic and copies ran while one was open for 0% of the time, Pallas kernels for 0%

profile of v3, /device:TPU:0, one launch (start us, length us, event | category | flops | bytes accessed | tf_op | source)
XLA Modules:
  0.0 69.0 jit_solution(1095620047909175100)
XLA Ops:
  0.7 2.9 %prepare.1 = (f32[64,128]{1,0:T(8,128)S(1)}, f32[64,128]{1,0:T(8,128)S(1)}, f32[64,128]{1,0:T(8,128)S(1)}, f32[64,128]{1,0:T(8,128)S(1)}, f32[72,128]{1,0:T(8,12...) custom-call(s32[1]{0:T(128)} %bitcast.parity_ref, ...), custom_call_target="tpu_custom_call" | custom-call | flops 10000000000 | tf_op jit(solution)/shard_map/prepare/pallas_call | solution.py:409
  3.5 6.5 %collective-permute-start.5 = (f32[8,128]{1,0:T(8,128)S(1)}, f32[8,128]{1,0:T(8,128)S(1)}, u32[]{:S(2)}, u32[]{:S(2)}) collective-permute-start(f32[8,128]{1,0:T(8,128)S(1)} %get-tuple-element.45), channel_id=1, source_target_pairs={{0,31},{1,2},{2,1},{3,4},{4,3},{5,6},{6,5},{7,8},{8,7},{9,10},{10,... | collective-permute-start | bytes 12296 | tf_op jit(solution)/shard_map/ppermute | solution.py:438
  10.0 0.0 collective-permute-start.4
  10.0 0.0 collective-permute-start
  10.0 1.0 %collective-permute-start.1 = (f32[64,128]{1,0:T(8,128)S(1)}, f32[64,128]{1,0:T(8,128)S(1)}, u32[]{:S(2)}, u32[]{:S(2)}) collective-permute-start(f32[64,128]{1,0:T(8,128)S(1)} %get-tuple-element.41), channel_id=1, source_target_pairs={{0,8},{1,9},{2,10},{3,11},{4,12},{5,13},{6,14},{7,15},{8,0},{9,1},... | collective-permute-start | bytes 98312 | tf_op jit(solution)/shard_map/ppermute | solution.py:444
  11.0 1.4 %collective-permute-start.2 = (f32[64,128]{1,0:T(8,128)S(1)}, f32[64,128]{1,0:T(8,128)S(1)}, u32[]{:S(2)}, u32[]{:S(2)}) collective-permute-start(f32[64,128]{1,0:T(8,128)S(1)} %get-tuple-element.42), channel_id=1, source_target_pairs={{0,4},{1,5},{2,6},{3,7},{4,0},{5,1},{6,2},{7,3},{8,12},{9,13},{10,... | collective-permute-start | bytes 98312 | tf_op jit(solution)/shard_map/ppermute | solution.py:444
  12.4 0.0 collective-permute-done.5.refs_8_
  12.4 0.0 collective-permute-start.3
  12.4 2.4 %collective-permute-done.refs_3_ = f32[64,128]{1,0:T(8,128)S(1)} collective-permute-done((f32[64,128]{1,0:T(8,128)S(1)}, f32[64,128]{1,0:T(8,128)S(1)}, u32[]{:S(2)}, u32[]{:S(2)}) %collective-permute-start) | collective-permute-done | bytes 32800 | tf_op jit(solution)/shard_map/ppermute | solution.py:444
  14.8 0.0 collective-permute-done.1.refs_4_
  14.8 0.1 collective-permute-done.2.refs_5_
  14.9 1.4 %collective-permute-done.3.refs_6_ = f32[64,128]{1,0:T(8,128)S(1)} collective-permute-done((f32[64,128]{1,0:T(8,128)S(1)}, f32[64,128]{1,0:T(8,128)S(1)}, u32[]{:S(2)}, u32[]{:S(2)}) %collective-permute-start.3) | collective-permute-done | bytes 32800 | tf_op jit(solution)/shard_map/ppermute | solution.py:444
  16.3 0.0 collective-permute-done.4.refs_7_
  16.3 3.1 %first.1 = (f32[128,128]{1,0:T(8,128)S(1)}, f32[64,128]{1,0:T(8,128)S(1)}, f32[64,128]{1,0:T(8,128)S(1)}, f32[64,128]{1,0:T(8,128)S(1)}, f32[64,128]{1,0:T(8,128...) custom-call(s32[1,128]{1,0:T(1,128)S(1)} %get-tuple-element.39.refs_, ...), custom_call_target="tpu_custom_call" | custom-call | tf_op jit(solution)/shard_map/first/pallas_call | solution.py:459
  19.4 3.3 %collective-permute-start.11 = (f32[8,128]{1,0:T(8,128)S(1)}, f32[8,128]{1,0:T(8,128)S(1)}, u32[]{:S(2)}, u32[]{:S(2)}) collective-permute-start(f32[8,128]{1,0:T(8,128)S(1)} %get-tuple-element.56), channel_id=1, source_target_pairs={{0,31},{1,2},{2,1},{3,4},{4,3},{5,6},{6,5},{7,8},{8,7},{9,10},{10,... | collective-permute-start | bytes 12296 | tf_op jit(solution)/shard_map/ppermute | solution.py:438
  22.7 0.0 collective-permute-start.10
  22.7 0.0 collective-permute-start.6
  22.7 0.0 collective-permute-start.7
  22.7 1.5 %collective-permute-start.8 = (f32[64,128]{1,0:T(8,128)S(1)}, f32[64,128]{1,0:T(8,128)S(1)}, u32[]{:S(2)}, u32[]{:S(2)}) collective-permute-start(f32[64,128]{1,0:T(8,128)S(1)} %get-tuple-element.53), channel_id=1, source_target_pairs={{0,4},{1,5},{2,6},{3,7},{4,0},{5,1},{6,2},{7,3},{8,12},{9,13},{10,... | collective-permute-start | bytes 98312 | tf_op jit(solution)/shard_map/ppermute | solution.py:444
  24.2 2.0 %collective-permute-done.11.refs_9_ = f32[8,128]{1,0:T(8,128)S(1)} collective-permute-done((f32[8,128]{1,0:T(8,128)S(1)}, f32[8,128]{1,0:T(8,128)S(1)}, u32[]{:S(2)}, u32[]{:S(2)}) %collective-permute-start.11) | collective-permute-done | bytes 4128 | tf_op jit(solution)/shard_map/ppermute | solution.py:438
  26.2 0.7 %collective-permute-start.9 = (f32[64,128]{1,0:T(8,128)S(1)}, f32[64,128]{1,0:T(8,128)S(1)}, u32[]{:S(2)}, u32[]{:S(2)}) collective-permute-start(f32[64,128]{1,0:T(8,128)S(1)} %get-tuple-element.54), channel_id=1, source_target_pairs={{0,2},{1,3},{2,0},{3,1},{4,6},{5,7},{6,4},{7,5},{8,10},{9,11},{10,... | collective-permute-start | bytes 98312 | tf_op jit(solution)/shard_map/ppermute | solution.py:444
  26.9 0.6 collective-permute-done.6.refs_4_
  27.5 0.0 collective-permute-done.7.refs_5_
  27.5 2.6 %collective-permute-done.9.refs_7_ = f32[64,128]{1,0:T(8,128)S(1)} collective-permute-done((f32[64,128]{1,0:T(8,128)S(1)}, f32[64,128]{1,0:T(8,128)S(1)}, u32[]{:S(2)}, u32[]{:S(2)}) %collective-permute-start.9) | collective-permute-done | bytes 32800 | tf_op jit(solution)/shard_map/ppermute | solution.py:444
  30.1 0.0 collective-permute-done.10.refs_8_
  30.1 2.6 %step.2 = (f32[128,128]{1,0:T(8,128)S(1)}, f32[64,128]{1,0:T(8,128)S(1)}, f32[64,128]{1,0:T(8,128)S(1)}, f32[64,128]{1,0:T(8,128)S(1)}, f32[64,128]{1,0:T(8,128)...) custom-call(s32[1,128]{1,0:T(1,128)S(1)} %get-tuple-element.39.refs_0_, ...), custom_call_target="tpu_custom_call" | custom-call | tf_op jit(solution)/shard_map/step/pallas_call | solution.py:471
  32.7 2.1 %collective-permute-start.17 = (f32[8,128]{1,0:T(8,128)S(1)}, f32[8,128]{1,0:T(8,128)S(1)}, u32[]{:S(2)}, u32[]{:S(2)}) collective-permute-start(f32[8,128]{1,0:T(8,128)S(1)} %get-tuple-element.64), channel_id=1, source_target_pairs={{0,31},{1,2},{2,1},{3,4},{4,3},{5,6},{6,5},{7,8},{8,7},{9,10},{10,... | collective-permute-start | bytes 12296 | tf_op jit(solution)/shard_map/ppermute | solution.py:438
  34.8 0.0 collective-permute-start.16
  34.8 0.0 collective-permute-start.12
  34.8 0.0 collective-permute-start.13
  34.8 1.6 %collective-permute-start.14 = (f32[64,128]{1,0:T(8,128)S(1)}, f32[64,128]{1,0:T(8,128)S(1)}, u32[]{:S(2)}, u32[]{:S(2)}) collective-permute-start(f32[64,128]{1,0:T(8,128)S(1)} %get-tuple-element.61), channel_id=1, source_target_pairs={{0,4},{1,5},{2,6},{3,7},{4,0},{5,1},{6,2},{7,3},{8,12},{9,13},{10,... | collective-permute-start | bytes 98312 | tf_op jit(solution)/shard_map/ppermute | solution.py:444
  36.4 3.0 %collective-permute-done.17.refs_9_ = f32[8,128]{1,0:T(8,128)S(1)} collective-permute-done((f32[8,128]{1,0:T(8,128)S(1)}, f32[8,128]{1,0:T(8,128)S(1)}, u32[]{:S(2)}, u32[]{:S(2)}) %collective-permute-start.17) | collective-permute-done | bytes 4128 | tf_op jit(solution)/shard_map/ppermute | solution.py:438
  39.4 0.8 %collective-permute-start.15 = (f32[64,128]{1,0:T(8,128)S(1)}, f32[64,128]{1,0:T(8,128)S(1)}, u32[]{:S(2)}, u32[]{:S(2)}) collective-permute-start(f32[64,128]{1,0:T(8,128)S(1)} %get-tuple-element.62), channel_id=1, source_target_pairs={{0,2},{1,3},{2,0},{3,1},{4,6},{5,7},{6,4},{7,5},{8,10},{9,11},{10,... | collective-permute-start | bytes 98312 | tf_op jit(solution)/shard_map/ppermute | solution.py:444
  40.2 0.0 collective-permute-done.14.refs_6_
  40.2 3.1 %collective-permute-done.15.refs_7_ = f32[64,128]{1,0:T(8,128)S(1)} collective-permute-done((f32[64,128]{1,0:T(8,128)S(1)}, f32[64,128]{1,0:T(8,128)S(1)}, u32[]{:S(2)}, u32[]{:S(2)}) %collective-permute-start.15) | collective-permute-done | bytes 32800 | tf_op jit(solution)/shard_map/ppermute | solution.py:444
  43.3 0.0 collective-permute-done.16.refs_8_
  43.3 2.7 %step.3 = (f32[128,128]{1,0:T(8,128)S(1)}, f32[64,128]{1,0:T(8,128)S(1)}, f32[64,128]{1,0:T(8,128)S(1)}, f32[64,128]{1,0:T(8,128)S(1)}, f32[64,128]{1,0:T(8,128)...) custom-call(s32[1,128]{1,0:T(1,128)S(1)} %get-tuple-element.39.refs_0_, ...), custom_call_target="tpu_custom_call" | custom-call | tf_op jit(solution)/shard_map/step/pallas_call | solution.py:471
  46.0 1.0 %collective-permute-start.23 = (f32[8,128]{1,0:T(8,128)S(1)}, f32[8,128]{1,0:T(8,128)S(1)}, u32[]{:S(2)}, u32[]{:S(2)}) collective-permute-start(f32[8,128]{1,0:T(8,128)S(1)} %get-tuple-element.71), channel_id=1, source_target_pairs={{0,31},{1,2},{2,1},{3,4},{4,3},{5,6},{6,5},{7,8},{8,7},{9,10},{10,... | collective-permute-start | bytes 12296 | tf_op jit(solution)/shard_map/ppermute | solution.py:438
  47.0 0.0 collective-permute-start.22
  47.0 1.6 %collective-permute-start.20 = (f32[64,128]{1,0:T(8,128)S(1)}, f32[64,128]{1,0:T(8,128)S(1)}, u32[]{:S(2)}, u32[]{:S(2)}) collective-permute-start(f32[64,128]{1,0:T(8,128)S(1)} %get-tuple-element.68), channel_id=1, source_target_pairs={{0,4},{1,5},{2,6},{3,7},{4,0},{5,1},{6,2},{7,3},{8,12},{9,13},{10,... | collective-permute-start | bytes 98312 | tf_op jit(solution)/shard_map/ppermute | solution.py:444
  48.6 4.1 %collective-permute-done.23.refs_9_ = f32[8,128]{1,0:T(8,128)S(1)} collective-permute-done((f32[8,128]{1,0:T(8,128)S(1)}, f32[8,128]{1,0:T(8,128)S(1)}, u32[]{:S(2)}, u32[]{:S(2)}) %collective-permute-start.23) | collective-permute-done | bytes 4128 | tf_op jit(solution)/shard_map/ppermute | solution.py:438
  52.7 0.8 %collective-permute-start.21 = (f32[64,128]{1,0:T(8,128)S(1)}, f32[64,128]{1,0:T(8,128)S(1)}, u32[]{:S(2)}, u32[]{:S(2)}) collective-permute-start(f32[64,128]{1,0:T(8,128)S(1)} %get-tuple-element.69), channel_id=1, source_target_pairs={{0,2},{1,3},{2,0},{3,1},{4,6},{5,7},{6,4},{7,5},{8,10},{9,11},{10,... | collective-permute-start | bytes 98312 | tf_op jit(solution)/shard_map/ppermute | solution.py:444
  53.5 0.0 collective-permute-done.20.refs_6_
  53.5 3.1 %collective-permute-done.21.refs_7_ = f32[64,128]{1,0:T(8,128)S(1)} collective-permute-done((f32[64,128]{1,0:T(8,128)S(1)}, f32[64,128]{1,0:T(8,128)S(1)}, u32[]{:S(2)}, u32[]{:S(2)}) %collective-permute-start.21) | collective-permute-done | bytes 32800 | tf_op jit(solution)/shard_map/ppermute | solution.py:444
  56.6 0.0 collective-permute-done.22.refs_8_
  56.6 2.6 %last.1 = (f32[128,128]{1,0:T(8,128)S(1)}, f32[32,128]{1,0:T(8,128)S(1)}) custom-call(s32[1,128]{1,0:T(1,128)S(1)} %get-tuple-element.39.refs_0_, f32[128,128]{1,0:T(8,128)S(1)} %get-tuple-element.65.refs_1_.refs_3_, f32[128,128]{1,0:T(8,128)S(1)} %bitcast.19, f32[1,128]{1,0:T(1,128)S(1)} %get-tuple-element.50.refs_3_.scale_ref, ...), custom_call_target="tpu_custom_call" | custom-call | tf_op jit(solution)/shard_map/last/pallas_call | solution.py:482
  59.2 8.9 %all_to_all.11 = f32[32,1,128]{2,1,0:T(1,128)S(1)} all-to-all(f32[32,1,128]{2,1,0:T(1,128)S(1)} %bitcast.25), channel_id=1, replica_groups=mesh['rows'=32] {'rows'}, dimensions={0} | all-to-all | bytes 32768 | tf_op jit(solution)/shard_map/all_to_all | solution.py:492
  68.1 0.9 %finish.1 = (f32[128,128]{1,0:T(8,128)}, f32[128,128]{1,0:T(8,128)}) custom-call(f32[32,128]{1,0:T(8,128)S(1)} %bitcast.24, f32[1,128]{1,0:T(1,128)S(1)} %get-tuple-element.50.refs_3_.scale_ref, f32[128,128]{1,0:T(8,128)S(1)} %bitcast.23, f32[128,128]{1,0:T(8,128)S(1)} %get-tuple-element.49.refs_1_.refs_14_, ...), custom_call_target="tpu_custom_call" | custom-call | tf_op jit(solution)/shard_map/finish/pallas_call | solution.py:493
  (13 shorter events, 0.0 us)
Async XLA Ops:
  0.6 15.7 %copy-start = (f32[128,128,128]{2,1,0:T(8,128)S(1)}, f32[128,128,128]{2,1,0:T(8,128)}, u32[]{:S(2)}) copy-start(f32[128,128,128]{2,1,0:T(8,128)} %refs_12_.1) | copy-start | bytes 25165828
  0.6 15.7 %copy-start.1 = (f32[16384]{0:T(1024)S(1)}, f32[16384]{0:T(1024)}, u32[]{:S(2)}) copy-start(f32[16384]{0:T(1024)} %param.11) | copy-start | bytes 196612
  0.7 15.7 %copy-start.2 = (f32[16384]{0:T(1024)S(1)}, f32[16384]{0:T(1024)}, u32[]{:S(2)}) copy-start(f32[16384]{0:T(1024)} %param.10) | copy-start | bytes 196612
  3.5 8.8 %collective-permute-start.5 = (f32[8,128]{1,0:T(8,128)S(1)}, f32[8,128]{1,0:T(8,128)S(1)}, u32[]{:S(2)}, u32[]{:S(2)}) collective-permute-start(f32[8,128]{1,0:T(8,128)S(1)} %get-tuple-element.45), channel_id=1, source_target_pairs={{0,31},{1,2},{2,1},{3,4},{4,3},{5,6},{6,5},{7,8},{8,7},{9,10},{10,... | collective-permute-start | bytes 12296 | tf_op jit(solution)/shard_map/ppermute | solution.py:438
  10.0 6.3 %collective-permute-start.4 = (f32[72,128]{1,0:T(8,128)S(1)}, f32[72,128]{1,0:T(8,128)S(1)}, u32[]{:S(2)}, u32[]{:S(2)}) collective-permute-start(f32[72,128]{1,0:T(8,128)S(1)} %get-tuple-element.44), channel_id=1, source_target_pairs={{0,1},{1,0},{2,3},{3,2},{4,5},{5,4},{6,7},{7,6},{8,9},{9,8},{10,11... | collective-permute-start | bytes 110600 | tf_op jit(solution)/shard_map/ppermute | solution.py:444
  10.0 4.8 %collective-permute-start = (f32[64,128]{1,0:T(8,128)S(1)}, f32[64,128]{1,0:T(8,128)S(1)}, u32[]{:S(2)}, u32[]{:S(2)}) collective-permute-start(f32[64,128]{1,0:T(8,128)S(1)} %get-tuple-element.40), channel_id=1, source_target_pairs={{0,16},{1,17},{2,18},{3,19},{4,20},{5,21},{6,22},{7,23},{8,24},{9,... | collective-permute-start | bytes 98312 | tf_op jit(solution)/shard_map/ppermute | solution.py:444
  10.0 4.8 %collective-permute-start.1 = (f32[64,128]{1,0:T(8,128)S(1)}, f32[64,128]{1,0:T(8,128)S(1)}, u32[]{:S(2)}, u32[]{:S(2)}) collective-permute-start(f32[64,128]{1,0:T(8,128)S(1)} %get-tuple-element.41), channel_id=1, source_target_pairs={{0,8},{1,9},{2,10},{3,11},{4,12},{5,13},{6,14},{7,15},{8,0},{9,1},... | collective-permute-start | bytes 98312 | tf_op jit(solution)/shard_map/ppermute | solution.py:444
  11.0 3.9 %collective-permute-start.2 = (f32[64,128]{1,0:T(8,128)S(1)}, f32[64,128]{1,0:T(8,128)S(1)}, u32[]{:S(2)}, u32[]{:S(2)}) collective-permute-start(f32[64,128]{1,0:T(8,128)S(1)} %get-tuple-element.42), channel_id=1, source_target_pairs={{0,4},{1,5},{2,6},{3,7},{4,0},{5,1},{6,2},{7,3},{8,12},{9,13},{10,... | collective-permute-start | bytes 98312 | tf_op jit(solution)/shard_map/ppermute | solution.py:444
  12.4 3.9 %collective-permute-start.3 = (f32[64,128]{1,0:T(8,128)S(1)}, f32[64,128]{1,0:T(8,128)S(1)}, u32[]{:S(2)}, u32[]{:S(2)}) collective-permute-start(f32[64,128]{1,0:T(8,128)S(1)} %get-tuple-element.43), channel_id=1, source_target_pairs={{0,2},{1,3},{2,0},{3,1},{4,6},{5,7},{6,4},{7,5},{8,10},{9,11},{10,... | collective-permute-start | bytes 98312 | tf_op jit(solution)/shard_map/ppermute | solution.py:444
  19.4 6.8 %collective-permute-start.11 = (f32[8,128]{1,0:T(8,128)S(1)}, f32[8,128]{1,0:T(8,128)S(1)}, u32[]{:S(2)}, u32[]{:S(2)}) collective-permute-start(f32[8,128]{1,0:T(8,128)S(1)} %get-tuple-element.56), channel_id=1, source_target_pairs={{0,31},{1,2},{2,1},{3,4},{4,3},{5,6},{6,5},{7,8},{8,7},{9,10},{10,... | collective-permute-start | bytes 12296 | tf_op jit(solution)/shard_map/ppermute | solution.py:438
  22.7 7.4 %collective-permute-start.10 = (f32[72,128]{1,0:T(8,128)S(1)}, f32[72,128]{1,0:T(8,128)S(1)}, u32[]{:S(2)}, u32[]{:S(2)}) collective-permute-start(f32[72,128]{1,0:T(8,128)S(1)} %get-tuple-element.55), channel_id=1, source_target_pairs={{0,1},{1,0},{2,3},{3,2},{4,5},{5,4},{6,7},{7,6},{8,9},{9,8},{10,11... | collective-permute-start | bytes 110600 | tf_op jit(solution)/shard_map/ppermute | solution.py:444
  22.7 4.8 %collective-permute-start.6 = (f32[64,128]{1,0:T(8,128)S(1)}, f32[64,128]{1,0:T(8,128)S(1)}, u32[]{:S(2)}, u32[]{:S(2)}) collective-permute-start(f32[64,128]{1,0:T(8,128)S(1)} %get-tuple-element.51), channel_id=1, source_target_pairs={{0,16},{1,17},{2,18},{3,19},{4,20},{5,21},{6,22},{7,23},{8,24},{9,... | collective-permute-start | bytes 98312 | tf_op jit(solution)/shard_map/ppermute | solution.py:444
  22.7 4.8 %collective-permute-start.7 = (f32[64,128]{1,0:T(8,128)S(1)}, f32[64,128]{1,0:T(8,128)S(1)}, u32[]{:S(2)}, u32[]{:S(2)}) collective-permute-start(f32[64,128]{1,0:T(8,128)S(1)} %get-tuple-element.52), channel_id=1, source_target_pairs={{0,8},{1,9},{2,10},{3,11},{4,12},{5,13},{6,14},{7,15},{8,0},{9,1},... | collective-permute-start | bytes 98312 | tf_op jit(solution)/shard_map/ppermute | solution.py:444
  22.7 4.8 %collective-permute-start.8 = (f32[64,128]{1,0:T(8,128)S(1)}, f32[64,128]{1,0:T(8,128)S(1)}, u32[]{:S(2)}, u32[]{:S(2)}) collective-permute-start(f32[64,128]{1,0:T(8,128)S(1)} %get-tuple-element.53), channel_id=1, source_target_pairs={{0,4},{1,5},{2,6},{3,7},{4,0},{5,1},{6,2},{7,3},{8,12},{9,13},{10,... | collective-permute-start | bytes 98312 | tf_op jit(solution)/shard_map/ppermute | solution.py:444
  26.2 3.9 %collective-permute-start.9 = (f32[64,128]{1,0:T(8,128)S(1)}, f32[64,128]{1,0:T(8,128)S(1)}, u32[]{:S(2)}, u32[]{:S(2)}) collective-permute-start(f32[64,128]{1,0:T(8,128)S(1)} %get-tuple-element.54), channel_id=1, source_target_pairs={{0,2},{1,3},{2,0},{3,1},{4,6},{5,7},{6,4},{7,5},{8,10},{9,11},{10,... | collective-permute-start | bytes 98312 | tf_op jit(solution)/shard_map/ppermute | solution.py:444
  32.7 6.7 %collective-permute-start.17 = (f32[8,128]{1,0:T(8,128)S(1)}, f32[8,128]{1,0:T(8,128)S(1)}, u32[]{:S(2)}, u32[]{:S(2)}) collective-permute-start(f32[8,128]{1,0:T(8,128)S(1)} %get-tuple-element.64), channel_id=1, source_target_pairs={{0,31},{1,2},{2,1},{3,4},{4,3},{5,6},{6,5},{7,8},{8,7},{9,10},{10,... | collective-permute-start | bytes 12296 | tf_op jit(solution)/shard_map/ppermute | solution.py:438
  34.8 8.5 %collective-permute-start.16 = (f32[72,128]{1,0:T(8,128)S(1)}, f32[72,128]{1,0:T(8,128)S(1)}, u32[]{:S(2)}, u32[]{:S(2)}) collective-permute-start(f32[72,128]{1,0:T(8,128)S(1)} %get-tuple-element.63), channel_id=1, source_target_pairs={{0,1},{1,0},{2,3},{3,2},{4,5},{5,4},{6,7},{7,6},{8,9},{9,8},{10,11... | collective-permute-start | bytes 110600 | tf_op jit(solution)/shard_map/ppermute | solution.py:444
  34.8 5.4 %collective-permute-start.12 = (f32[64,128]{1,0:T(8,128)S(1)}, f32[64,128]{1,0:T(8,128)S(1)}, u32[]{:S(2)}, u32[]{:S(2)}) collective-permute-start(f32[64,128]{1,0:T(8,128)S(1)} %get-tuple-element.59), channel_id=1, source_target_pairs={{0,16},{1,17},{2,18},{3,19},{4,20},{5,21},{6,22},{7,23},{8,24},{9,... | collective-permute-start | bytes 98312 | tf_op jit(solution)/shard_map/ppermute | solution.py:444
  34.8 5.4 %collective-permute-start.13 = (f32[64,128]{1,0:T(8,128)S(1)}, f32[64,128]{1,0:T(8,128)S(1)}, u32[]{:S(2)}, u32[]{:S(2)}) collective-permute-start(f32[64,128]{1,0:T(8,128)S(1)} %get-tuple-element.60), channel_id=1, source_target_pairs={{0,8},{1,9},{2,10},{3,11},{4,12},{5,13},{6,14},{7,15},{8,0},{9,1},... | collective-permute-start | bytes 98312 | tf_op jit(solution)/shard_map/ppermute | solution.py:444
  34.8 5.4 %collective-permute-start.14 = (f32[64,128]{1,0:T(8,128)S(1)}, f32[64,128]{1,0:T(8,128)S(1)}, u32[]{:S(2)}, u32[]{:S(2)}) collective-permute-start(f32[64,128]{1,0:T(8,128)S(1)} %get-tuple-element.61), channel_id=1, source_target_pairs={{0,4},{1,5},{2,6},{3,7},{4,0},{5,1},{6,2},{7,3},{8,12},{9,13},{10,... | collective-permute-start | bytes 98312 | tf_op jit(solution)/shard_map/ppermute | solution.py:444
  39.4 3.9 %collective-permute-start.15 = (f32[64,128]{1,0:T(8,128)S(1)}, f32[64,128]{1,0:T(8,128)S(1)}, u32[]{:S(2)}, u32[]{:S(2)}) collective-permute-start(f32[64,128]{1,0:T(8,128)S(1)} %get-tuple-element.62), channel_id=1, source_target_pairs={{0,2},{1,3},{2,0},{3,1},{4,6},{5,7},{6,4},{7,5},{8,10},{9,11},{10,... | collective-permute-start | bytes 98312 | tf_op jit(solution)/shard_map/ppermute | solution.py:444
  46.0 6.7 %collective-permute-start.23 = (f32[8,128]{1,0:T(8,128)S(1)}, f32[8,128]{1,0:T(8,128)S(1)}, u32[]{:S(2)}, u32[]{:S(2)}) collective-permute-start(f32[8,128]{1,0:T(8,128)S(1)} %get-tuple-element.71), channel_id=1, source_target_pairs={{0,31},{1,2},{2,1},{3,4},{4,3},{5,6},{6,5},{7,8},{8,7},{9,10},{10,... | collective-permute-start | bytes 12296 | tf_op jit(solution)/shard_map/ppermute | solution.py:438
  47.0 9.6 %collective-permute-start.22 = (f32[72,128]{1,0:T(8,128)S(1)}, f32[72,128]{1,0:T(8,128)S(1)}, u32[]{:S(2)}, u32[]{:S(2)}) collective-permute-start(f32[72,128]{1,0:T(8,128)S(1)} %get-tuple-element.70), channel_id=1, source_target_pairs={{0,1},{1,0},{2,3},{3,2},{4,5},{5,4},{6,7},{7,6},{8,9},{9,8},{10,11... | collective-permute-start | bytes 110600 | tf_op jit(solution)/shard_map/ppermute | solution.py:444
  47.0 6.5 %collective-permute-start.18 = (f32[64,128]{1,0:T(8,128)S(1)}, f32[64,128]{1,0:T(8,128)S(1)}, u32[]{:S(2)}, u32[]{:S(2)}) collective-permute-start(f32[64,128]{1,0:T(8,128)S(1)} %get-tuple-element.66), channel_id=1, source_target_pairs={{0,16},{1,17},{2,18},{3,19},{4,20},{5,21},{6,22},{7,23},{8,24},{9,... | collective-permute-start | bytes 98312 | tf_op jit(solution)/shard_map/ppermute | solution.py:444
  47.0 6.5 %collective-permute-start.19 = (f32[64,128]{1,0:T(8,128)S(1)}, f32[64,128]{1,0:T(8,128)S(1)}, u32[]{:S(2)}, u32[]{:S(2)}) collective-permute-start(f32[64,128]{1,0:T(8,128)S(1)} %get-tuple-element.67), channel_id=1, source_target_pairs={{0,8},{1,9},{2,10},{3,11},{4,12},{5,13},{6,14},{7,15},{8,0},{9,1},... | collective-permute-start | bytes 98312 | tf_op jit(solution)/shard_map/ppermute | solution.py:444
  47.0 6.5 %collective-permute-start.20 = (f32[64,128]{1,0:T(8,128)S(1)}, f32[64,128]{1,0:T(8,128)S(1)}, u32[]{:S(2)}, u32[]{:S(2)}) collective-permute-start(f32[64,128]{1,0:T(8,128)S(1)} %get-tuple-element.68), channel_id=1, source_target_pairs={{0,4},{1,5},{2,6},{3,7},{4,0},{5,1},{6,2},{7,3},{8,12},{9,13},{10,... | collective-permute-start | bytes 98312 | tf_op jit(solution)/shard_map/ppermute | solution.py:444
  52.7 3.9 %collective-permute-start.21 = (f32[64,128]{1,0:T(8,128)S(1)}, f32[64,128]{1,0:T(8,128)S(1)}, u32[]{:S(2)}, u32[]{:S(2)}) collective-permute-start(f32[64,128]{1,0:T(8,128)S(1)} %get-tuple-element.69), channel_id=1, source_target_pairs={{0,2},{1,3},{2,0},{3,1},{4,6},{5,7},{6,4},{7,5},{8,10},{9,11},{10,... | collective-permute-start | bytes 98312 | tf_op jit(solution)/shard_map/ppermute | solution.py:444

commit v4 on v3

--- a/solution.py
+++ b/solution.py
@@ -241,10 +241,11 @@
                 elif dict_ref is None:
                     block = wide_ref[c]
                 else:
-                    block = dict_ref[c]
-                    total = total + block
-                    block = halves_wide(block)
+                    block = halves_wide(dict_ref[c])
                     wide_ref[c] = block
+                    some = block[:, :width] if c % 16 == 0 else some + block[:, :width]
+                    if c % 16 == 15 or c + 1 == blocks:
+                        total = total + some.astype(F32)
                 prods.append(product(lhs_ref[c * 2 * SLOT : (c + 1) * 2 * SLOT, :], block))
             prod_ref[pair * 2 * SLOT : (pair + 1) * 2 * SLOT, :] = halves_wide(jnp.concatenate(prods, axis=0))
         span = slice(part * part_span, (part + 1) * part_span)

time: 69.2 us -> 69.1 us (level)
  no operation moved by 1% of the time
where the time goes in v4:
time: 69.1 us; the launch traced here: 68.9 us
  starting transfers between devices  22.3 us (32%)
  waiting for transfers between devices  22.3 us (32%)
  Pallas kernels  14.6 us (21%)
  blocking collectives  8.87 us (13%)
  between operations  0.76 us (1%)
    ppermute x20, waiting for transfers between devices, exchange(): got.append(lax.ppermute(sends[level], 'rows', pairs))  13.3 us
    ppermute x4, starting transfers between devices, exchange(): edges = lax.ppermute(edge, 'rows', far)  12.8 us
    ppermute x20, starting transfers between devices, exchange(): got.append(lax.ppermute(sends[level], 'rows', pairs))  9.52 us
    ppermute x4, waiting for transfers between devices, exchange(): edges = lax.ppermute(edge, 'rows', far)  9.05 us
    all_to_all x1, blocking collectives, per_device(): sums = lax.all_to_all(sums, 'rows', 0, 0, tiled=True)  8.87 us
    pallas_call x2, Pallas kernels, per_device(): pl.pallas_call(functools.partial(step_kernel, **common), out_shape=[shape...  5.3 us
    pallas_call x1, Pallas kernels, per_device(): pl.pallas_call(functools.partial(first_kernel, **common), out_shape=[shap...  3.01 us
    pallas_call x1, Pallas kernels, per_device(): pl.pallas_call(functools.partial(prepare, nb=nb, blocks=blocks, levels=le...  2.86 us
  transfers between devices with their start and end apart: 24, of which 10 were waited for; matrix products, arithmetic and copies ran while one was open for 0% of the time, Pallas kernels for 0%

profile of v4, /device:TPU:0, one launch (start us, length us, event | category | flops | bytes accessed | tf_op | source)
XLA Modules:
  0.0 68.9 jit_solution(14264386792887674050)
XLA Ops:
  0.7 2.9 %prepare.1 = (f32[64,128]{1,0:T(8,128)S(1)}, f32[64,128]{1,0:T(8,128)S(1)}, f32[64,128]{1,0:T(8,128)S(1)}, f32[64,128]{1,0:T(8,128)S(1)}, f32[72,128]{1,0:T(8,12...) custom-call(s32[1]{0:T(128)} %bitcast.parity_ref, ...), custom_call_target="tpu_custom_call" | custom-call | flops 10000000000 | tf_op jit(solution)/shard_map/prepare/pallas_call | solution.py:410
  3.5 6.5 %collective-permute-start.5 = (f32[8,128]{1,0:T(8,128)S(1)}, f32[8,128]{1,0:T(8,128)S(1)}, u32[]{:S(2)}, u32[]{:S(2)}) collective-permute-start(f32[8,128]{1,0:T(8,128)S(1)} %get-tuple-element.45), channel_id=1, source_target_pairs={{0,31},{1,2},{2,1},{3,4},{4,3},{5,6},{6,5},{7,8},{8,7},{9,10},{10,... | collective-permute-start | bytes 12296 | tf_op jit(solution)/shard_map/ppermute | solution.py:439
  10.0 0.0 collective-permute-start.4
  10.0 0.0 collective-permute-start
  10.0 1.0 %collective-permute-start.1 = (f32[64,128]{1,0:T(8,128)S(1)}, f32[64,128]{1,0:T(8,128)S(1)}, u32[]{:S(2)}, u32[]{:S(2)}) collective-permute-start(f32[64,128]{1,0:T(8,128)S(1)} %get-tuple-element.41), channel_id=1, source_target_pairs={{0,8},{1,9},{2,10},{3,11},{4,12},{5,13},{6,14},{7,15},{8,0},{9,1},... | collective-permute-start | bytes 98312 | tf_op jit(solution)/shard_map/ppermute | solution.py:445
  11.0 1.4 %collective-permute-start.2 = (f32[64,128]{1,0:T(8,128)S(1)}, f32[64,128]{1,0:T(8,128)S(1)}, u32[]{:S(2)}, u32[]{:S(2)}) collective-permute-start(f32[64,128]{1,0:T(8,128)S(1)} %get-tuple-element.42), channel_id=1, source_target_pairs={{0,4},{1,5},{2,6},{3,7},{4,0},{5,1},{6,2},{7,3},{8,12},{9,13},{10,... | collective-permute-start | bytes 98312 | tf_op jit(solution)/shard_map/ppermute | solution.py:445
  12.4 0.0 collective-permute-done.5.refs_8_
  12.4 0.0 collective-permute-start.3
  12.4 2.4 %collective-permute-done.refs_3_ = f32[64,128]{1,0:T(8,128)S(1)} collective-permute-done((f32[64,128]{1,0:T(8,128)S(1)}, f32[64,128]{1,0:T(8,128)S(1)}, u32[]{:S(2)}, u32[]{:S(2)}) %collective-permute-start) | collective-permute-done | bytes 32800 | tf_op jit(solution)/shard_map/ppermute | solution.py:445
  14.8 0.0 collective-permute-done.1.refs_4_
  14.8 0.1 collective-permute-done.2.refs_5_
  14.9 1.4 %collective-permute-done.3.refs_6_ = f32[64,128]{1,0:T(8,128)S(1)} collective-permute-done((f32[64,128]{1,0:T(8,128)S(1)}, f32[64,128]{1,0:T(8,128)S(1)}, u32[]{:S(2)}, u32[]{:S(2)}) %collective-permute-start.3) | collective-permute-done | bytes 32800 | tf_op jit(solution)/shard_map/ppermute | solution.py:445
  16.3 3.0 %first.1 = (f32[128,128]{1,0:T(8,128)S(1)}, f32[64,128]{1,0:T(8,128)S(1)}, f32[64,128]{1,0:T(8,128)S(1)}, f32[64,128]{1,0:T(8,128)S(1)}, f32[64,128]{1,0:T(8,128...) custom-call(s32[1,128]{1,0:T(1,128)S(1)} %get-tuple-element.39.refs_, ...), custom_call_target="tpu_custom_call" | custom-call | tf_op jit(solution)/shard_map/first/pallas_call | solution.py:460
  19.3 3.3 %collective-permute-start.11 = (f32[8,128]{1,0:T(8,128)S(1)}, f32[8,128]{1,0:T(8,128)S(1)}, u32[]{:S(2)}, u32[]{:S(2)}) collective-permute-start(f32[8,128]{1,0:T(8,128)S(1)} %get-tuple-element.56), channel_id=1, source_target_pairs={{0,31},{1,2},{2,1},{3,4},{4,3},{5,6},{6,5},{7,8},{8,7},{9,10},{10,... | collective-permute-start | bytes 12296 | tf_op jit(solution)/shard_map/ppermute | solution.py:439
  22.6 1.5 %collective-permute-start.8 = (f32[64,128]{1,0:T(8,128)S(1)}, f32[64,128]{1,0:T(8,128)S(1)}, u32[]{:S(2)}, u32[]{:S(2)}) collective-permute-start(f32[64,128]{1,0:T(8,128)S(1)} %get-tuple-element.53), channel_id=1, source_target_pairs={{0,4},{1,5},{2,6},{3,7},{4,0},{5,1},{6,2},{7,3},{8,12},{9,13},{10,... | collective-permute-start | bytes 98312 | tf_op jit(solution)/shard_map/ppermute | solution.py:445
  24.2 2.0 %collective-permute-done.11.refs_9_ = f32[8,128]{1,0:T(8,128)S(1)} collective-permute-done((f32[8,128]{1,0:T(8,128)S(1)}, f32[8,128]{1,0:T(8,128)S(1)}, u32[]{:S(2)}, u32[]{:S(2)}) %collective-permute-start.11) | collective-permute-done | bytes 4128 | tf_op jit(solution)/shard_map/ppermute | solution.py:439
  26.1 0.7 %collective-permute-start.9 = (f32[64,128]{1,0:T(8,128)S(1)}, f32[64,128]{1,0:T(8,128)S(1)}, u32[]{:S(2)}, u32[]{:S(2)}) collective-permute-start(f32[64,128]{1,0:T(8,128)S(1)} %get-tuple-element.54), channel_id=1, source_target_pairs={{0,2},{1,3},{2,0},{3,1},{4,6},{5,7},{6,4},{7,5},{8,10},{9,11},{10,... | collective-permute-start | bytes 98312 | tf_op jit(solution)/shard_map/ppermute | solution.py:445
  26.8 0.6 collective-permute-done.6.refs_4_
  27.4 0.0 collective-permute-done.7.refs_5_
  27.4 0.0 collective-permute-done.8.refs_6_
  27.4 2.6 %collective-permute-done.9.refs_7_ = f32[64,128]{1,0:T(8,128)S(1)} collective-permute-done((f32[64,128]{1,0:T(8,128)S(1)}, f32[64,128]{1,0:T(8,128)S(1)}, u32[]{:S(2)}, u32[]{:S(2)}) %collective-permute-start.9) | collective-permute-done | bytes 32800 | tf_op jit(solution)/shard_map/ppermute | solution.py:445
  30.0 2.6 %step.2 = (f32[128,128]{1,0:T(8,128)S(1)}, f32[64,128]{1,0:T(8,128)S(1)}, f32[64,128]{1,0:T(8,128)S(1)}, f32[64,128]{1,0:T(8,128)S(1)}, f32[64,128]{1,0:T(8,128)...) custom-call(s32[1,128]{1,0:T(1,128)S(1)} %get-tuple-element.39.refs_0_, ...), custom_call_target="tpu_custom_call" | custom-call | tf_op jit(solution)/shard_map/step/pallas_call | solution.py:472
  32.6 2.1 %collective-permute-start.17 = (f32[8,128]{1,0:T(8,128)S(1)}, f32[8,128]{1,0:T(8,128)S(1)}, u32[]{:S(2)}, u32[]{:S(2)}) collective-permute-start(f32[8,128]{1,0:T(8,128)S(1)} %get-tuple-element.64), channel_id=1, source_target_pairs={{0,31},{1,2},{2,1},{3,4},{4,3},{5,6},{6,5},{7,8},{8,7},{9,10},{10,... | collective-permute-start | bytes 12296 | tf_op jit(solution)/shard_map/ppermute | solution.py:439
  34.7 0.0 collective-permute-start.16
  34.7 0.0 collective-permute-start.12
  34.7 0.0 collective-permute-start.13
  34.7 1.6 %collective-permute-start.14 = (f32[64,128]{1,0:T(8,128)S(1)}, f32[64,128]{1,0:T(8,128)S(1)}, u32[]{:S(2)}, u32[]{:S(2)}) collective-permute-start(f32[64,128]{1,0:T(8,128)S(1)} %get-tuple-element.61), channel_id=1, source_target_pairs={{0,4},{1,5},{2,6},{3,7},{4,0},{5,1},{6,2},{7,3},{8,12},{9,13},{10,... | collective-permute-start | bytes 98312 | tf_op jit(solution)/shard_map/ppermute | solution.py:445
  36.3 3.0 %collective-permute-done.17.refs_9_ = f32[8,128]{1,0:T(8,128)S(1)} collective-permute-done((f32[8,128]{1,0:T(8,128)S(1)}, f32[8,128]{1,0:T(8,128)S(1)}, u32[]{:S(2)}, u32[]{:S(2)}) %collective-permute-start.17) | collective-permute-done | bytes 4128 | tf_op jit(solution)/shard_map/ppermute | solution.py:439
  39.3 0.8 %collective-permute-start.15 = (f32[64,128]{1,0:T(8,128)S(1)}, f32[64,128]{1,0:T(8,128)S(1)}, u32[]{:S(2)}, u32[]{:S(2)}) collective-permute-start(f32[64,128]{1,0:T(8,128)S(1)} %get-tuple-element.62), channel_id=1, source_target_pairs={{0,2},{1,3},{2,0},{3,1},{4,6},{5,7},{6,4},{7,5},{8,10},{9,11},{10,... | collective-permute-start | bytes 98312 | tf_op jit(solution)/shard_map/ppermute | solution.py:445
  40.1 0.0 collective-permute-done.12.refs_4_
  40.1 0.0 collective-permute-done.13.refs_5_
  40.1 0.0 collective-permute-done.14.refs_6_
  40.1 3.1 %collective-permute-done.15.refs_7_ = f32[64,128]{1,0:T(8,128)S(1)} collective-permute-done((f32[64,128]{1,0:T(8,128)S(1)}, f32[64,128]{1,0:T(8,128)S(1)}, u32[]{:S(2)}, u32[]{:S(2)}) %collective-permute-start.15) | collective-permute-done | bytes 32800 | tf_op jit(solution)/shard_map/ppermute | solution.py:445
  43.2 0.0 collective-permute-done.16.refs_8_
  43.2 2.7 %step.3 = (f32[128,128]{1,0:T(8,128)S(1)}, f32[64,128]{1,0:T(8,128)S(1)}, f32[64,128]{1,0:T(8,128)S(1)}, f32[64,128]{1,0:T(8,128)S(1)}, f32[64,128]{1,0:T(8,128)...) custom-call(s32[1,128]{1,0:T(1,128)S(1)} %get-tuple-element.39.refs_0_, ...), custom_call_target="tpu_custom_call" | custom-call | tf_op jit(solution)/shard_map/step/pallas_call | solution.py:472
  46.0 1.0 %collective-permute-start.23 = (f32[8,128]{1,0:T(8,128)S(1)}, f32[8,128]{1,0:T(8,128)S(1)}, u32[]{:S(2)}, u32[]{:S(2)}) collective-permute-start(f32[8,128]{1,0:T(8,128)S(1)} %get-tuple-element.71), channel_id=1, source_target_pairs={{0,31},{1,2},{2,1},{3,4},{4,3},{5,6},{6,5},{7,8},{8,7},{9,10},{10,... | collective-permute-start | bytes 12296 | tf_op jit(solution)/shard_map/ppermute | solution.py:439
  46.9 0.0 collective-permute-start.22
  47.0 0.0 collective-permute-start.18
  47.0 1.6 %collective-permute-start.20 = (f32[64,128]{1,0:T(8,128)S(1)}, f32[64,128]{1,0:T(8,128)S(1)}, u32[]{:S(2)}, u32[]{:S(2)}) collective-permute-start(f32[64,128]{1,0:T(8,128)S(1)} %get-tuple-element.68), channel_id=1, source_target_pairs={{0,4},{1,5},{2,6},{3,7},{4,0},{5,1},{6,2},{7,3},{8,12},{9,13},{10,... | collective-permute-start | bytes 98312 | tf_op jit(solution)/shard_map/ppermute | solution.py:445
  48.6 4.1 %collective-permute-done.23.refs_9_ = f32[8,128]{1,0:T(8,128)S(1)} collective-permute-done((f32[8,128]{1,0:T(8,128)S(1)}, f32[8,128]{1,0:T(8,128)S(1)}, u32[]{:S(2)}, u32[]{:S(2)}) %collective-permute-start.23) | collective-permute-done | bytes 4128 | tf_op jit(solution)/shard_map/ppermute | solution.py:439
  52.7 0.8 %collective-permute-start.21 = (f32[64,128]{1,0:T(8,128)S(1)}, f32[64,128]{1,0:T(8,128)S(1)}, u32[]{:S(2)}, u32[]{:S(2)}) collective-permute-start(f32[64,128]{1,0:T(8,128)S(1)} %get-tuple-element.69), channel_id=1, source_target_pairs={{0,2},{1,3},{2,0},{3,1},{4,6},{5,7},{6,4},{7,5},{8,10},{9,11},{10,... | collective-permute-start | bytes 98312 | tf_op jit(solution)/shard_map/ppermute | solution.py:445
  53.5 0.0 collective-permute-done.18.refs_4_
  53.5 0.0 collective-permute-done.19.refs_5_
  53.5 0.0 collective-permute-done.20.refs_6_
  53.5 3.1 %collective-permute-done.21.refs_7_ = f32[64,128]{1,0:T(8,128)S(1)} collective-permute-done((f32[64,128]{1,0:T(8,128)S(1)}, f32[64,128]{1,0:T(8,128)S(1)}, u32[]{:S(2)}, u32[]{:S(2)}) %collective-permute-start.21) | collective-permute-done | bytes 32800 | tf_op jit(solution)/shard_map/ppermute | solution.py:445
  56.6 2.6 %last.1 = (f32[128,128]{1,0:T(8,128)S(1)}, f32[32,128]{1,0:T(8,128)S(1)}) custom-call(s32[1,128]{1,0:T(1,128)S(1)} %get-tuple-element.39.refs_0_, f32[128,128]{1,0:T(8,128)S(1)} %get-tuple-element.65.refs_1_.refs_3_, f32[128,128]{1,0:T(8,128)S(1)} %bitcast.19, f32[1,128]{1,0:T(1,128)S(1)} %get-tuple-element.50.refs_3_.scale_ref, ...), custom_call_target="tpu_custom_call" | custom-call | tf_op jit(solution)/shard_map/last/pallas_call | solution.py:483
  59.1 8.9 %all_to_all.11 = f32[32,1,128]{2,1,0:T(1,128)S(1)} all-to-all(f32[32,1,128]{2,1,0:T(1,128)S(1)} %bitcast.25), channel_id=1, replica_groups=mesh['rows'=32] {'rows'}, dimensions={0} | all-to-all | bytes 32768 | tf_op jit(solution)/shard_map/all_to_all | solution.py:493
  68.0 0.9 %finish.1 = (f32[128,128]{1,0:T(8,128)}, f32[128,128]{1,0:T(8,128)}) custom-call(f32[32,128]{1,0:T(8,128)S(1)} %bitcast.24, f32[1,128]{1,0:T(1,128)S(1)} %get-tuple-element.50.refs_3_.scale_ref, f32[128,128]{1,0:T(8,128)S(1)} %bitcast.23, f32[128,128]{1,0:T(8,128)S(1)} %get-tuple-element.49.refs_1_.refs_14_, ...), custom_call_target="tpu_custom_call" | custom-call | tf_op jit(solution)/shard_map/finish/pallas_call | solution.py:494
  (13 shorter events, 0.0 us)
Async XLA Ops:
  0.6 15.7 %copy-start = (f32[128,128,128]{2,1,0:T(8,128)S(1)}, f32[128,128,128]{2,1,0:T(8,128)}, u32[]{:S(2)}) copy-start(f32[128,128,128]{2,1,0:T(8,128)} %refs_12_.1) | copy-start | bytes 25165828
  0.6 15.7 %copy-start.1 = (f32[16384]{0:T(1024)S(1)}, f32[16384]{0:T(1024)}, u32[]{:S(2)}) copy-start(f32[16384]{0:T(1024)} %param.11) | copy-start | bytes 196612
  0.7 15.7 %copy-start.2 = (f32[16384]{0:T(1024)S(1)}, f32[16384]{0:T(1024)}, u32[]{:S(2)}) copy-start(f32[16384]{0:T(1024)} %param.10) | copy-start | bytes 196612
  3.5 8.8 %collective-permute-start.5 = (f32[8,128]{1,0:T(8,128)S(1)}, f32[8,128]{1,0:T(8,128)S(1)}, u32[]{:S(2)}, u32[]{:S(2)}) collective-permute-start(f32[8,128]{1,0:T(8,128)S(1)} %get-tuple-element.45), channel_id=1, source_target_pairs={{0,31},{1,2},{2,1},{3,4},{4,3},{5,6},{6,5},{7,8},{8,7},{9,10},{10,... | collective-permute-start | bytes 12296 | tf_op jit(solution)/shard_map/ppermute | solution.py:439
  10.0 6.3 %collective-permute-start.4 = (f32[72,128]{1,0:T(8,128)S(1)}, f32[72,128]{1,0:T(8,128)S(1)}, u32[]{:S(2)}, u32[]{:S(2)}) collective-permute-start(f32[72,128]{1,0:T(8,128)S(1)} %get-tuple-element.44), channel_id=1, source_target_pairs={{0,1},{1,0},{2,3},{3,2},{4,5},{5,4},{6,7},{7,6},{8,9},{9,8},{10,11... | collective-permute-start | bytes 110600 | tf_op jit(solution)/shard_map/ppermute | solution.py:445
  10.0 4.8 %collective-permute-start = (f32[64,128]{1,0:T(8,128)S(1)}, f32[64,128]{1,0:T(8,128)S(1)}, u32[]{:S(2)}, u32[]{:S(2)}) collective-permute-start(f32[64,128]{1,0:T(8,128)S(1)} %get-tuple-element.40), channel_id=1, source_target_pairs={{0,16},{1,17},{2,18},{3,19},{4,20},{5,21},{6,22},{7,23},{8,24},{9,... | collective-permute-start | bytes 98312 | tf_op jit(solution)/shard_map/ppermute | solution.py:445
  10.0 4.8 %collective-permute-start.1 = (f32[64,128]{1,0:T(8,128)S(1)}, f32[64,128]{1,0:T(8,128)S(1)}, u32[]{:S(2)}, u32[]{:S(2)}) collective-permute-start(f32[64,128]{1,0:T(8,128)S(1)} %get-tuple-element.41), channel_id=1, source_target_pairs={{0,8},{1,9},{2,10},{3,11},{4,12},{5,13},{6,14},{7,15},{8,0},{9,1},... | collective-permute-start | bytes 98312 | tf_op jit(solution)/shard_map/ppermute | solution.py:445
  11.0 3.9 %collective-permute-start.2 = (f32[64,128]{1,0:T(8,128)S(1)}, f32[64,128]{1,0:T(8,128)S(1)}, u32[]{:S(2)}, u32[]{:S(2)}) collective-permute-start(f32[64,128]{1,0:T(8,128)S(1)} %get-tuple-element.42), channel_id=1, source_target_pairs={{0,4},{1,5},{2,6},{3,7},{4,0},{5,1},{6,2},{7,3},{8,12},{9,13},{10,... | collective-permute-start | bytes 98312 | tf_op jit(solution)/shard_map/ppermute | solution.py:445
  12.4 3.9 %collective-permute-start.3 = (f32[64,128]{1,0:T(8,128)S(1)}, f32[64,128]{1,0:T(8,128)S(1)}, u32[]{:S(2)}, u32[]{:S(2)}) collective-permute-start(f32[64,128]{1,0:T(8,128)S(1)} %get-tuple-element.43), channel_id=1, source_target_pairs={{0,2},{1,3},{2,0},{3,1},{4,6},{5,7},{6,4},{7,5},{8,10},{9,11},{10,... | collective-permute-start | bytes 98312 | tf_op jit(solution)/shard_map/ppermute | solution.py:445
  19.3 6.8 %collective-permute-start.11 = (f32[8,128]{1,0:T(8,128)S(1)}, f32[8,128]{1,0:T(8,128)S(1)}, u32[]{:S(2)}, u32[]{:S(2)}) collective-permute-start(f32[8,128]{1,0:T(8,128)S(1)} %get-tuple-element.56), channel_id=1, source_target_pairs={{0,31},{1,2},{2,1},{3,4},{4,3},{5,6},{6,5},{7,8},{8,7},{9,10},{10,... | collective-permute-start | bytes 12296 | tf_op jit(solution)/shard_map/ppermute | solution.py:439
  22.6 7.4 %collective-permute-start.10 = (f32[72,128]{1,0:T(8,128)S(1)}, f32[72,128]{1,0:T(8,128)S(1)}, u32[]{:S(2)}, u32[]{:S(2)}) collective-permute-start(f32[72,128]{1,0:T(8,128)S(1)} %get-tuple-element.55), channel_id=1, source_target_pairs={{0,1},{1,0},{2,3},{3,2},{4,5},{5,4},{6,7},{7,6},{8,9},{9,8},{10,11... | collective-permute-start | bytes 110600 | tf_op jit(solution)/shard_map/ppermute | solution.py:445
  22.6 4.8 %collective-permute-start.6 = (f32[64,128]{1,0:T(8,128)S(1)}, f32[64,128]{1,0:T(8,128)S(1)}, u32[]{:S(2)}, u32[]{:S(2)}) collective-permute-start(f32[64,128]{1,0:T(8,128)S(1)} %get-tuple-element.51), channel_id=1, source_target_pairs={{0,16},{1,17},{2,18},{3,19},{4,20},{5,21},{6,22},{7,23},{8,24},{9,... | collective-permute-start | bytes 98312 | tf_op jit(solution)/shard_map/ppermute | solution.py:445
  22.6 4.8 %collective-permute-start.7 = (f32[64,128]{1,0:T(8,128)S(1)}, f32[64,128]{1,0:T(8,128)S(1)}, u32[]{:S(2)}, u32[]{:S(2)}) collective-permute-start(f32[64,128]{1,0:T(8,128)S(1)} %get-tuple-element.52), channel_id=1, source_target_pairs={{0,8},{1,9},{2,10},{3,11},{4,12},{5,13},{6,14},{7,15},{8,0},{9,1},... | collective-permute-start | bytes 98312 | tf_op jit(solution)/shard_map/ppermute | solution.py:445
  22.6 4.8 %collective-permute-start.8 = (f32[64,128]{1,0:T(8,128)S(1)}, f32[64,128]{1,0:T(8,128)S(1)}, u32[]{:S(2)}, u32[]{:S(2)}) collective-permute-start(f32[64,128]{1,0:T(8,128)S(1)} %get-tuple-element.53), channel_id=1, source_target_pairs={{0,4},{1,5},{2,6},{3,7},{4,0},{5,1},{6,2},{7,3},{8,12},{9,13},{10,... | collective-permute-start | bytes 98312 | tf_op jit(solution)/shard_map/ppermute | solution.py:445
  26.1 3.9 %collective-permute-start.9 = (f32[64,128]{1,0:T(8,128)S(1)}, f32[64,128]{1,0:T(8,128)S(1)}, u32[]{:S(2)}, u32[]{:S(2)}) collective-permute-start(f32[64,128]{1,0:T(8,128)S(1)} %get-tuple-element.54), channel_id=1, source_target_pairs={{0,2},{1,3},{2,0},{3,1},{4,6},{5,7},{6,4},{7,5},{8,10},{9,11},{10,... | collective-permute-start | bytes 98312 | tf_op jit(solution)/shard_map/ppermute | solution.py:445
  32.6 6.7 %collective-permute-start.17 = (f32[8,128]{1,0:T(8,128)S(1)}, f32[8,128]{1,0:T(8,128)S(1)}, u32[]{:S(2)}, u32[]{:S(2)}) collective-permute-start(f32[8,128]{1,0:T(8,128)S(1)} %get-tuple-element.64), channel_id=1, source_target_pairs={{0,31},{1,2},{2,1},{3,4},{4,3},{5,6},{6,5},{7,8},{8,7},{9,10},{10,... | collective-permute-start | bytes 12296 | tf_op jit(solution)/shard_map/ppermute | solution.py:439
  34.7 8.5 %collective-permute-start.16 = (f32[72,128]{1,0:T(8,128)S(1)}, f32[72,128]{1,0:T(8,128)S(1)}, u32[]{:S(2)}, u32[]{:S(2)}) collective-permute-start(f32[72,128]{1,0:T(8,128)S(1)} %get-tuple-element.63), channel_id=1, source_target_pairs={{0,1},{1,0},{2,3},{3,2},{4,5},{5,4},{6,7},{7,6},{8,9},{9,8},{10,11... | collective-permute-start | bytes 110600 | tf_op jit(solution)/shard_map/ppermute | solution.py:445
  34.7 5.4 %collective-permute-start.12 = (f32[64,128]{1,0:T(8,128)S(1)}, f32[64,128]{1,0:T(8,128)S(1)}, u32[]{:S(2)}, u32[]{:S(2)}) collective-permute-start(f32[64,128]{1,0:T(8,128)S(1)} %get-tuple-element.59), channel_id=1, source_target_pairs={{0,16},{1,17},{2,18},{3,19},{4,20},{5,21},{6,22},{7,23},{8,24},{9,... | collective-permute-start | bytes 98312 | tf_op jit(solution)/shard_map/ppermute | solution.py:445
  34.7 5.4 %collective-permute-start.13 = (f32[64,128]{1,0:T(8,128)S(1)}, f32[64,128]{1,0:T(8,128)S(1)}, u32[]{:S(2)}, u32[]{:S(2)}) collective-permute-start(f32[64,128]{1,0:T(8,128)S(1)} %get-tuple-element.60), channel_id=1, source_target_pairs={{0,8},{1,9},{2,10},{3,11},{4,12},{5,13},{6,14},{7,15},{8,0},{9,1},... | collective-permute-start | bytes 98312 | tf_op jit(solution)/shard_map/ppermute | solution.py:445
  34.7 5.4 %collective-permute-start.14 = (f32[64,128]{1,0:T(8,128)S(1)}, f32[64,128]{1,0:T(8,128)S(1)}, u32[]{:S(2)}, u32[]{:S(2)}) collective-permute-start(f32[64,128]{1,0:T(8,128)S(1)} %get-tuple-element.61), channel_id=1, source_target_pairs={{0,4},{1,5},{2,6},{3,7},{4,0},{5,1},{6,2},{7,3},{8,12},{9,13},{10,... | collective-permute-start | bytes 98312 | tf_op jit(solution)/shard_map/ppermute | solution.py:445
  39.3 3.9 %collective-permute-start.15 = (f32[64,128]{1,0:T(8,128)S(1)}, f32[64,128]{1,0:T(8,128)S(1)}, u32[]{:S(2)}, u32[]{:S(2)}) collective-permute-start(f32[64,128]{1,0:T(8,128)S(1)} %get-tuple-element.62), channel_id=1, source_target_pairs={{0,2},{1,3},{2,0},{3,1},{4,6},{5,7},{6,4},{7,5},{8,10},{9,11},{10,... | collective-permute-start | bytes 98312 | tf_op jit(solution)/shard_map/ppermute | solution.py:445
  46.0 6.7 %collective-permute-start.23 = (f32[8,128]{1,0:T(8,128)S(1)}, f32[8,128]{1,0:T(8,128)S(1)}, u32[]{:S(2)}, u32[]{:S(2)}) collective-permute-start(f32[8,128]{1,0:T(8,128)S(1)} %get-tuple-element.71), channel_id=1, source_target_pairs={{0,31},{1,2},{2,1},{3,4},{4,3},{5,6},{6,5},{7,8},{8,7},{9,10},{10,... | collective-permute-start | bytes 12296 | tf_op jit(solution)/shard_map/ppermute | solution.py:439
  46.9 9.6 %collective-permute-start.22 = (f32[72,128]{1,0:T(8,128)S(1)}, f32[72,128]{1,0:T(8,128)S(1)}, u32[]{:S(2)}, u32[]{:S(2)}) collective-permute-start(f32[72,128]{1,0:T(8,128)S(1)} %get-tuple-element.70), channel_id=1, source_target_pairs={{0,1},{1,0},{2,3},{3,2},{4,5},{5,4},{6,7},{7,6},{8,9},{9,8},{10,11... | collective-permute-start | bytes 110600 | tf_op jit(solution)/shard_map/ppermute | solution.py:445
  47.0 6.5 %collective-permute-start.18 = (f32[64,128]{1,0:T(8,128)S(1)}, f32[64,128]{1,0:T(8,128)S(1)}, u32[]{:S(2)}, u32[]{:S(2)}) collective-permute-start(f32[64,128]{1,0:T(8,128)S(1)} %get-tuple-element.66), channel_id=1, source_target_pairs={{0,16},{1,17},{2,18},{3,19},{4,20},{5,21},{6,22},{7,23},{8,24},{9,... | collective-permute-start | bytes 98312 | tf_op jit(solution)/shard_map/ppermute | solution.py:445
  47.0 6.5 %collective-permute-start.19 = (f32[64,128]{1,0:T(8,128)S(1)}, f32[64,128]{1,0:T(8,128)S(1)}, u32[]{:S(2)}, u32[]{:S(2)}) collective-permute-start(f32[64,128]{1,0:T(8,128)S(1)} %get-tuple-element.67), channel_id=1, source_target_pairs={{0,8},{1,9},{2,10},{3,11},{4,12},{5,13},{6,14},{7,15},{8,0},{9,1},... | collective-permute-start | bytes 98312 | tf_op jit(solution)/shard_map/ppermute | solution.py:445
  47.0 6.5 %collective-permute-start.20 = (f32[64,128]{1,0:T(8,128)S(1)}, f32[64,128]{1,0:T(8,128)S(1)}, u32[]{:S(2)}, u32[]{:S(2)}) collective-permute-start(f32[64,128]{1,0:T(8,128)S(1)} %get-tuple-element.68), channel_id=1, source_target_pairs={{0,4},{1,5},{2,6},{3,7},{4,0},{5,1},{6,2},{7,3},{8,12},{9,13},{10,... | collective-permute-start | bytes 98312 | tf_op jit(solution)/shard_map/ppermute | solution.py:445
  52.7 3.9 %collective-permute-start.21 = (f32[64,128]{1,0:T(8,128)S(1)}, f32[64,128]{1,0:T(8,128)S(1)}, u32[]{:S(2)}, u32[]{:S(2)}) collective-permute-start(f32[64,128]{1,0:T(8,128)S(1)} %get-tuple-element.69), channel_id=1, source_target_pairs={{0,2},{1,3},{2,0},{3,1},{4,6},{5,7},{6,4},{7,5},{8,10},{9,11},{10,... | collective-permute-start | bytes 98312 | tf_op jit(solution)/shard_map/ppermute | solution.py:445
